TPU v7x, 512 devices: a whole 4x8x8 slice. The times are simulated.
512 devices in a mesh: prow: 8 (over z), pcol: 64 (over y, x, core).
Axes of the slice: x: 4, y: 8, z: 8, core: 2. Of those that a mesh axis runs over, the one named last changes fastest.
Arguments:
- vectors: float32 [32768, 8192], P('prow', 'pcol'), may hold values from -6 to 6
- reflectors: bfloat16 [4, 256, 32768], P(None, 'pcol', 'prow'), may hold values from -0.03125 to 0.03125
- tau_diag: float32 [4, 256], replicated, may hold values from 0.5 to 1.5
- coupling: float32 [4, 256, 256], replicated, may hold values from -0.375 to 0.375
Outputs:
- result: float32 [32768, 8192], P('prow', 'pcol')
All inputs are finite; a program needn't handle non-finite values.
Results may differ from a plain program's by a relative error of at most 0.0003.
Values may be sent and summed in bfloat16 or wider, within the bound.
No kernel may reach another device: no remote copies, remote signals or barrier semaphores. Data moves between devices by JAX's collectives and lax.ppermute only.
A program may use at most 64 MiB of HBM per device.

v0:
```python
import jax
import jax.numpy as jnp
from jax import lax
from jax.sharding import Mesh
from jax.sharding import PartitionSpec as P

PCOL = ("pcol_0", "pcol_1", "pcol_2")


def joined_along(parts, dim):
    lengths = list(parts.shape[1:])
    lengths[dim] *= parts.shape[0]
    return jnp.moveaxis(parts, 0, dim).reshape(lengths)


def stacked_from(x, axes, sequence):
    parts = x[None]
    for k in sequence:
        parts = lax.all_gather(parts, axes[k], axis=0, tiled=True)
    carried = [lax.axis_size(axes[k]) for k in reversed(sequence)]
    parts = parts.reshape(*carried, *x.shape)
    turned = sorted(range(len(sequence)), key=lambda place: sequence[len(sequence) - 1 - place])
    return parts.transpose(*turned, *range(len(sequence), parts.ndim)).reshape(-1, *x.shape)


def gather_axes(x, axes, sequence, dim):
    return joined_along(stacked_from(x, axes, sequence), dim)


def in_blocks(x, dim, devices):
    lengths = x.shape
    parts = x.reshape(*lengths[:dim], devices, lengths[dim] // devices, *lengths[dim + 1 :])
    return jnp.moveaxis(parts, dim, 0)


def sum_at_owner(x, axis, dim):
    parts = in_blocks(x, dim, lax.axis_size(axis))
    arrived = lax.all_to_all(parts, axis, split_axis=0, concat_axis=0, tiled=True)
    return arrived.sum(axis=0)


def copy_for_each(x, axis):
    copies = jnp.broadcast_to(x, (lax.axis_size(axis), *x.shape))
    return lax.all_to_all(copies, axis, split_axis=0, concat_axis=0, tiled=True)


def gather_directly(x, axis, dim):
    return joined_along(copy_for_each(x, axis), dim)


def on_device(vectors, reflectors, tau_diag, coupling):
    count = reflectors.shape[0]
    gathered = gather_axes(reflectors, PCOL, (1, 0, 2), 1)
    current = vectors
    for position in range(count - 1, -1, -1):
        rows_panel = gathered[position]
        widened = rows_panel.astype(jnp.float32)
        tri_factor = jnp.diag(tau_diag[position]) + jnp.triu(coupling[position], 1)
        partial_sum = jnp.dot(
            widened, current, precision=lax.Precision.HIGHEST, preferred_element_type=jnp.float32
        )
        shares = sum_at_owner(partial_sum, "prow", 1)
        local_image = jnp.dot(
            tri_factor, shares, precision=lax.Precision.HIGHEST, preferred_element_type=jnp.float32
        )
        updates = gather_directly(local_image, "prow", 1)
        current = current - lax.dot_general(
            widened,
            updates,
            (((0,), (0,)), ((), ())),
            precision=lax.Precision.HIGHEST,
            preferred_element_type=jnp.float32,
        )
    return current


def solution(mesh):
    finer = Mesh(
        mesh.devices.reshape(mesh.shape["prow"], 8, 4, 2), ("prow", "pcol_0", "pcol_1", "pcol_2")
    )
    placed = (P("prow", PCOL), P(None, PCOL, "prow"), P(), P())
    return jax.shard_map(
        on_device, mesh=finer, in_specs=placed, out_specs=P("prow", PCOL), check_vma=False
    )
```

profile of v0, /device:TPU:2, one launch (start us, length us, event | category | flops | bytes accessed | tf_op | source)
XLA Modules:
  0.0 267.3 jit_solution(2077051281151391013)
XLA Ops:
  6.5 18.3 %all-gather = bf16[16,4,4096]{2,1,0:T(4,128)(2,1)} all-gather(bf16[4,4,4096]{2,1,0:T(4,128)(2,1)} %param.5), channel_id=2, replica_groups=mesh['prow'=8,'pcol_0'=8,'pcol_1'=4,'pcol_2'=2] {'pcol_1'}, dimensions={0}, use_global_device_ids=true | all-gather | bytes 655360 | tf_op jit(solution)/shard_map/all_gather | solution.py:19
  24.8 0.0 all-gather.4.cloned.1.call-update
  24.8 0.0 all-gather.6.cloned.1.call-start
  24.9 57.0 %all-gather.4.cloned.1.call-done = bf16[32,4,4,4096]{3,2,1,0:T(4,128)(2,1)} async-done(((bf16[4,4,4,4096]{3,2,1,0:T(4,128)(2,1)}), bf16[32,4,4,4096]{3,2,1,0:T(4,128)(2,1)}) %all-gather.4.cloned.1.call-update) | async-done | bytes 4194320 | tf_op jit(solution)/shard_map/all_gather | solution.py:19
  81.9 0.0 all-gather.6.cloned.1.call-update
  81.9 1.9 copy.20
  83.8 27.2 %all-gather.6.cloned.1.call-done = bf16[64,4,4,4096]{3,2,1,0:T(4,128)(2,1)} async-done(((bf16[32,4,4,4096]{3,2,1,0:T(4,128)(2,1)}), bf16[64,4,4,4096]{3,2,1,0:T(4,128)(2,1)}) %all-gather.6.cloned.1.call-update) | async-done | bytes 8388624 | tf_op jit(solution)/shard_map/all_gather | solution.py:19
  111.0 5.6 %copy.18 = bf16[8,4,2,4,4,4096]{5,4,3,2,1,0:T(4,128)(2,1)S(1)} copy(bf16[8,4,2,4,4,4096]{5,4,3,1,0,2:T(4,128)(2,1)} %bitcast.111) | data formatting | bytes 16777216 | tf_op jit(solution)/shard_map/transpose | solution.py:23
  116.6 5.4 %fusion.36 = (bf16[1,64,4,4096]{3,2,0,1:T(4,128)(2,1)}, bf16[1,64,4,4096]{3,2,0,1:T(4,128)(2,1)}, bf16[1,64,4,4096]{3,2,0,1:T(4,128)(2,1)}, bf16[1,64,4,4096]{3,2,0,1:T(4,128)(2,1)}) fusion(bf16[4,64,4,4096]{3,2,0,1:T(4,128)(2,1)S(1)} %bitcast.109), kind=kLoop, calls=%fused_computation.43 | loop fusion | bytes 16777216 | tf_op jit(solution)/shard_map/slice | solution.py:56
  122.1 4.0 %reshape.56 = bf16[256,4096,1]{1,0,2:T(8,128)(2,1)} reshape(bf16[1,64,4,4096]{3,2,0,1:T(4,128)(2,1)} %get-tuple-element.8) | data formatting | bytes 4194304 | tf_op jit(solution)/shard_map/squeeze | solution.py:56
  126.1 4.6 %convolution_bitcast_fusion.4 = f32[8,256,16]{1,2,0:T(8,128)} fusion(bf16[256,4096,1]{1,0,2:T(8,128)(2,1)} %reshape.56, f32[8,16,4096]{2,1,0:T(8,128)S(1)} %bitcast.110), kind=kOutput, calls=%fused_computation.8 | convolution fusion | flops 1610612736 | bytes 4325376 | tf_op jit(solution)/shard_map/dot_general | solution.py:59
  130.6 7.4 %all-to-all-start = ((f32[8,256,16]{1,2,0:T(8,128)}), f32[8,256,16]{1,2,0:T(8,128)S(1)}, u32[]{:S(2)}, u32[]{:S(2)}) async-start(f32[8,256,16]{1,2,0:T(8,128)} %convolution_bitcast_fusion.4), calls=%async_computation | async-start | bytes 262144 | tf_op jit(solution)/shard_map/all_to_all | solution.py:38
  138.0 0.0 copy-done.7
  138.0 9.5 %all-to-all-done = f32[8,256,16]{1,2,0:T(8,128)S(1)} async-done(((f32[8,256,16]{1,2,0:T(8,128)}), f32[8,256,16]{1,2,0:T(8,128)S(1)}, u32[]{:S(2)}, u32[]{:S(2)}) %all-to-all-start) | async-done | bytes 131104 | tf_op jit(solution)/shard_map/all_to_all | solution.py:38
  147.5 0.0 copy-done.8
  147.5 0.4 fusion.14
  147.9 0.7 broadcast_in_dim.71
  148.6 3.4 %all-to-all-start.1 = ((f32[8,256,16]{1,2,0:T(8,128)}), f32[8,256,16]{1,2,0:T(8,128)S(1)}, u32[]{:S(2)}, u32[]{:S(2)}) async-start(f32[8,256,16]{1,2,0:T(8,128)} %broadcast_in_dim.71), calls=%async_computation.1 | async-start | bytes 262144 | tf_op jit(solution)/shard_map/all_to_all | solution.py:44
  152.0 4.0 %squeeze.29 = bf16[256,4096]{1,0:T(8,128)(2,1)} reshape(bf16[1,64,4,4096]{3,2,0,1:T(4,128)(2,1)} %get-tuple-element.8) | data formatting | bytes 4194304 | tf_op jit(solution)/shard_map/squeeze | solution.py:56
  156.0 3.9 %squeeze.31 = bf16[256,4096]{1,0:T(8,128)(2,1)} reshape(bf16[1,64,4,4096]{3,2,0,1:T(4,128)(2,1)} %get-tuple-element.7) | data formatting | bytes 4194304 | tf_op jit(solution)/shard_map/squeeze | solution.py:56
  159.9 1.0 all-to-all-done.1
  161.0 2.8 %fusion.3 = f32[4096,128]{0,1:T(8,128)S(1)} fusion(f32[4096,128]{0,1:T(8,128)S(1)} %copy.20, f32[256,128]{0,1:T(8,128)S(1)} %bitcast.113, bf16[256,4096]{1,0:T(8,128)(2,1)} %squeeze.29), kind=kOutput, calls=%fused_computation.7 | convolution fusion | flops 1611137024 | bytes 6422528 | tf_op jit(solution)/shard_map/dot_general | solution.py:67
  163.9 2.2 fusion.38
  166.1 15.0 %all_to_all.40 = f32[8,256,16]{1,2,0:T(8,128)S(1)} all-to-all(f32[8,256,16]{1,2,0:T(8,128)S(1)} %bitcast.117), channel_id=1, replica_groups=mesh['prow'=8,'pcol_0'=8,'pcol_1'=4,'pcol_2'=2] {'prow'}, dimensions={0} | all-to-all | bytes 262144 | tf_op jit(solution)/shard_map/all_to_all | solution.py:38
  181.1 0.4 fusion.11
  181.4 0.7 broadcast_in_dim.74
  182.1 3.4 %all-to-all-start.3 = ((f32[8,256,16]{1,2,0:T(8,128)}), f32[8,256,16]{1,2,0:T(8,128)S(1)}, u32[]{:S(2)}, u32[]{:S(2)}) async-start(f32[8,256,16]{1,2,0:T(8,128)} %broadcast_in_dim.74), calls=%async_computation.3 | async-start | bytes 262144 | tf_op jit(solution)/shard_map/all_to_all | solution.py:44
  185.5 0.0 copy-done.6
  185.5 2.1 squeeze.33
  187.6 6.9 %all-to-all-done.3 = f32[8,256,16]{1,2,0:T(8,128)S(1)} async-done(((f32[8,256,16]{1,2,0:T(8,128)}), f32[8,256,16]{1,2,0:T(8,128)S(1)}, u32[]{:S(2)}, u32[]{:S(2)}) %all-to-all-start.3) | async-done | bytes 131104 | tf_op jit(solution)/shard_map/all_to_all | solution.py:44
  194.5 3.4 %fusion.2 = f32[4096,128]{0,1:T(8,128)S(1)} fusion(f32[4096,128]{0,1:T(8,128)} %copy-done, f32[256,128]{0,1:T(8,128)S(1)} %bitcast.115, bf16[256,4096]{1,0:T(8,128)(2,1)} %squeeze.31), kind=kOutput, calls=%fused_computation.5 | convolution fusion | flops 1611137024 | bytes 6422528 | tf_op jit(solution)/shard_map/dot_general | solution.py:67
  197.9 0.0 copy-done.2
  197.9 2.2 fusion.39
  200.1 11.5 %all_to_all.41 = f32[8,256,16]{1,2,0:T(8,128)S(1)} all-to-all(f32[8,256,16]{1,2,0:T(8,128)S(1)} %bitcast.118), channel_id=1, replica_groups=mesh['prow'=8,'pcol_0'=8,'pcol_1'=4,'pcol_2'=2] {'prow'}, dimensions={0} | all-to-all | bytes 262144 | tf_op jit(solution)/shard_map/all_to_all | solution.py:38
  211.6 0.4 fusion.8
  212.0 0.7 broadcast_in_dim.77
  212.7 3.5 %all-to-all-start.5 = ((f32[8,256,16]{1,2,0:T(8,128)}), f32[8,256,16]{1,2,0:T(8,128)S(1)}, u32[]{:S(2)}, u32[]{:S(2)}) async-start(f32[8,256,16]{1,2,0:T(8,128)} %broadcast_in_dim.77), calls=%async_computation.5 | async-start | bytes 262144 | tf_op jit(solution)/shard_map/all_to_all | solution.py:44
  216.2 4.0 %squeeze.35 = bf16[256,4096]{1,0:T(8,128)(2,1)} reshape(bf16[1,64,4,4096]{3,2,0,1:T(4,128)(2,1)} %get-tuple-element.5) | data formatting | bytes 4194304 | tf_op jit(solution)/shard_map/squeeze | solution.py:56
  220.2 4.9 %all-to-all-done.5 = f32[8,256,16]{1,2,0:T(8,128)S(1)} async-done(((f32[8,256,16]{1,2,0:T(8,128)}), f32[8,256,16]{1,2,0:T(8,128)S(1)}, u32[]{:S(2)}, u32[]{:S(2)}) %all-to-all-start.5) | async-done | bytes 131104 | tf_op jit(solution)/shard_map/all_to_all | solution.py:44
  225.0 2.8 %fusion.1 = f32[4096,128]{0,1:T(8,128)S(1)} fusion(f32[4096,128]{0,1:T(8,128)S(1)} %fusion.2, f32[256,128]{0,1:T(8,128)S(1)} %bitcast.114, bf16[256,4096]{1,0:T(8,128)(2,1)} %squeeze.33), kind=kOutput, calls=%fused_computation.3 | convolution fusion | flops 1611137024 | bytes 6422528 | tf_op jit(solution)/shard_map/dot_general | solution.py:67
  227.9 0.0 copy-start.1
  227.9 2.2 fusion.40
  230.1 11.6 %all_to_all.42 = f32[8,256,16]{1,2,0:T(8,128)S(1)} all-to-all(f32[8,256,16]{1,2,0:T(8,128)S(1)} %bitcast.119), channel_id=1, replica_groups=mesh['prow'=8,'pcol_0'=8,'pcol_1'=4,'pcol_2'=2] {'prow'}, dimensions={0} | all-to-all | bytes 262144 | tf_op jit(solution)/shard_map/all_to_all | solution.py:38
  241.7 0.4 fusion.5
  242.1 0.1 broadcast_in_dim.80
  242.2 11.5 %all_to_all.43 = f32[8,256,16]{1,2,0:T(8,128)S(1)} all-to-all(f32[8,256,16]{1,2,0:T(8,128)S(1)} %broadcast_in_dim.80), channel_id=1, replica_groups=mesh['prow'=8,'pcol_0'=8,'pcol_1'=4,'pcol_2'=2] {'prow'}, dimensions={0} | all-to-all | bytes 262144 | tf_op jit(solution)/shard_map/all_to_all | solution.py:44
  253.6 3.9 %fusion = f32[4096,128]{0,1:T(8,128)} fusion(f32[4096,128]{0,1:T(8,128)} %copy-done.1, f32[256,128]{0,1:T(8,128)S(1)} %bitcast.116, bf16[256,4096]{1,0:T(8,128)(2,1)S(1)} %copy-done.5), kind=kOutput, calls=%fused_computation.1 | convolution fusion | flops 1611137024 | bytes 6422528 | tf_op jit(solution)/shard_map/dot_general | solution.py:67
  257.5 2.9 %copy.21 = f32[4096,128]{1,0:T(8,128)} copy(f32[4096,128]{0,1:T(8,128)} %fusion) | data formatting | bytes 4194304 | tf_op jit(solution)/shard_map/sub | solution.py:67
  (19 shorter events, 0.1 us)
Async XLA Ops:
  6.5 75.3 %all-gather.4.cloned.1.call-start = ((), (), s32[]{:S(2)}) async-start(), calls=%async_computation.8 | async-start | bytes 4718592 | tf_op jit(solution)/shard_map/all_gather | solution.py:19
  24.8 86.2 %all-gather.6.cloned.1.call-start = ((), (), s32[]{:S(2)}) async-start(), calls=%async_computation.9 | async-start | bytes 12582912 | tf_op jit(solution)/shard_map/all_gather | solution.py:19
  126.0 11.9 %copy-start.7 = (f32[4,256]{1,0:T(4,128)S(1)}, f32[4,256]{1,0:T(4,128)}, u32[]{:S(2)}) copy-start(f32[4,256]{1,0:T(4,128)} %param.6) | copy-start | bytes 12292
  126.0 21.5 %copy-start.8 = (f32[4,256,256]{2,1,0:T(8,128)S(1)}, f32[4,256,256]{2,1,0:T(8,128)}, u32[]{:S(2)}) copy-start(f32[4,256,256]{2,1,0:T(8,128)} %param.7) | copy-start | bytes 3145732
  130.6 16.9 %all-to-all-start = ((f32[8,256,16]{1,2,0:T(8,128)}), f32[8,256,16]{1,2,0:T(8,128)S(1)}, u32[]{:S(2)}, u32[]{:S(2)}) async-start(f32[8,256,16]{1,2,0:T(8,128)} %convolution_bitcast_fusion.4), calls=%async_computation | async-start | bytes 262144 | tf_op jit(solution)/shard_map/all_to_all | solution.py:38
  148.6 12.4 %all-to-all-start.1 = ((f32[8,256,16]{1,2,0:T(8,128)}), f32[8,256,16]{1,2,0:T(8,128)S(1)}, u32[]{:S(2)}, u32[]{:S(2)}) async-start(f32[8,256,16]{1,2,0:T(8,128)} %broadcast_in_dim.71), calls=%async_computation.1 | async-start | bytes 262144 | tf_op jit(solution)/shard_map/all_to_all | solution.py:44
  161.0 2.9 %copy-start.3 = (bf16[256,4096]{1,0:T(8,128)(2,1)S(1)}, bf16[256,4096]{1,0:T(8,128)(2,1)}, u32[]{:S(2)}) copy-start(bf16[256,4096]{1,0:T(8,128)(2,1)} %squeeze.31) | copy-start | bytes 6291460
  163.8 2.2 copy-start
  163.9 21.7 %copy-start.6 = (bf16[1,64,4,4096]{3,2,0,1:T(4,128)(2,1)S(1)}, bf16[1,64,4,4096]{3,2,0,1:T(4,128)(2,1)}, u32[]{:S(2)}) copy-start(bf16[1,64,4,4096]{3,2,0,1:T(4,128)(2,1)} %get-tuple-element.6) | copy-start | bytes 6291460
  182.1 12.4 %all-to-all-start.3 = ((f32[8,256,16]{1,2,0:T(8,128)}), f32[8,256,16]{1,2,0:T(8,128)S(1)}, u32[]{:S(2)}, u32[]{:S(2)}) async-start(f32[8,256,16]{1,2,0:T(8,128)} %broadcast_in_dim.74), calls=%async_computation.3 | async-start | bytes 262144 | tf_op jit(solution)/shard_map/all_to_all | solution.py:44
  194.5 3.4 %copy-start.2 = (bf16[256,4096]{1,0:T(8,128)(2,1)S(1)}, bf16[256,4096]{1,0:T(8,128)(2,1)}, u32[]{:S(2)}) copy-start(bf16[256,4096]{1,0:T(8,128)(2,1)} %squeeze.33) | copy-start | bytes 6291460
  212.7 12.4 %all-to-all-start.5 = ((f32[8,256,16]{1,2,0:T(8,128)}), f32[8,256,16]{1,2,0:T(8,128)S(1)}, u32[]{:S(2)}, u32[]{:S(2)}) async-start(f32[8,256,16]{1,2,0:T(8,128)} %broadcast_in_dim.77), calls=%async_computation.5 | async-start | bytes 262144 | tf_op jit(solution)/shard_map/all_to_all | solution.py:44
  225.0 2.9 %copy-start.4 = (bf16[256,4096]{1,0:T(8,128)(2,1)S(1)}, bf16[256,4096]{1,0:T(8,128)(2,1)}, u32[]{:S(2)}) copy-start(bf16[256,4096]{1,0:T(8,128)(2,1)} %squeeze.35) | copy-start | bytes 6291460
  227.9 2.3 copy-start.1
  227.9 25.7 %copy-start.5 = (bf16[256,4096]{1,0:T(8,128)(2,1)S(1)}, bf16[256,4096]{1,0:T(8,128)(2,1)}, u32[]{:S(2)}) copy-start(bf16[256,4096]{1,0:T(8,128)(2,1)} %squeeze.35) | copy-start | bytes 6291460
Sparse Core Ops, SparseCore 0:
  24.9 56.8 all-gather.3
  84.0 27.0 all-gather.5
where the time goes:
time: 268 us; the launch traced here: 267 us
  waiting for transfers between devices  107 us (40%)
  blocking collectives  67.7 us (25%)
  local copies, waits for them, and re-layouts  36 us (13%)
  matrix products  25.6 us (10%)
  starting transfers between devices  17.7 us (7%)
  between operations  13.6 us (5%)
    all_gather x2, waiting for transfers between devices, stacked_from(): parts = lax.all_gather(parts, axes[k], axis=0, tiled=True)  84.2 us
    all_to_all x3, blocking collectives, sum_at_owner(): lax.all_to_all(parts, axis, split_axis=0, concat_axis=0, tiled=True)  38 us
    all_gather x1, blocking collectives, stacked_from(): parts = lax.all_gather(parts, axes[k], axis=0, tiled=True)  18.3 us
    squeeze x5, local copies, waits for them, and re-layouts, on_device(): rows_panel = gathered[position]  17.9 us
    dot_general x4, matrix products, on_device(): lax.dot_general(widened, updates, (((0,), (0,)), ((), ())), precision=lax...  12.9 us
    all_to_all x3, waiting for transfers between devices, copy_for_each(): return lax.all_to_all(copies, axis, split_axis=0, concat_axis=0, tiled=True)  12.8 us
    all_to_all x1, blocking collectives, copy_for_each(): return lax.all_to_all(copies, axis, split_axis=0, concat_axis=0, tiled=True)  11.5 us
    dot_general x4, matrix products, on_device(): jnp.dot(widened, current, precision=lax.Precision.HIGHEST, preferred_elem...  11.2 us
  transfers between devices with their start and end apart: 6, of which 6 were waited for; matrix products, arithmetic and copies ran while one was open for 6% of the time, Pallas kernels for 0%

commit v1 on v0

v1 whole, which is shorter than its diff:
```python
import jax
import jax.numpy as jnp
from jax import lax
from jax.sharding import Mesh
from jax.sharding import PartitionSpec as P

PCOL = ("pcol_0", "pcol_1", "pcol_2")


def exchange(parts, axis):
    return lax.all_to_all(parts, axis, split_axis=0, concat_axis=0, tiled=True)


def copy_for_each(x, axis, devices):
    return exchange(jnp.broadcast_to(x, (devices, *x.shape)), axis)


def from_partner(x):
    return lax.ppermute(x, "pcol_2", [(0, 1), (1, 0)])


def two_terms(x):
    high = lax.reduce_precision(x, exponent_bits=8, mantissa_bits=7)
    return high.astype(jnp.bfloat16), (x - high).astype(jnp.bfloat16)


def products(half, terms):
    both = jnp.dot(half, terms, preferred_element_type=jnp.float32)
    columns = terms.shape[1] // 2
    return both[:, :columns] + both[:, columns:]


def spread(half, image):
    high, low = two_terms(image)
    dims = (((0,), (0,)), ((), ()))
    return lax.dot_general(half, high, dims, preferred_element_type=jnp.float32) + lax.dot_general(
        half, low, dims, preferred_element_type=jnp.float32
    )


def sum_everywhere(x, axis):
    devices = lax.axis_size(axis)
    arrived = exchange(x.reshape(devices, x.shape[0] // devices, x.shape[1]), axis)
    return copy_for_each(arrived.sum(axis=0), axis, devices).reshape(x.shape)


def reordered(tri_factor, outer, core, inner):
    size = tri_factor.shape[0]
    place = lax.broadcasted_iota(jnp.int32, (size, size), 0)
    source = lax.broadcasted_iota(jnp.int32, (size, size), 1)
    part, rest = place // (outer * inner), place % (outer * inner)
    owner = jnp.where(part == 0, core, 1 - core)
    wanted = ((rest // inner) * 2 + owner) * inner + rest % inner
    choose = (wanted == source).astype(jnp.float32)
    turned = jnp.dot(choose, tri_factor, precision=lax.Precision.HIGHEST)
    return lax.dot_general(turned, choose, (((1,), (1,)), ((), ())), precision=lax.Precision.HIGHEST)


def on_device(vectors, reflectors, tau_diag, coupling):
    count, each, rows = reflectors.shape
    high_axis, low_axis, core_axis = PCOL
    wide, deep = lax.axis_size(high_axis), lax.axis_size(low_axis)
    core = lax.axis_index(core_axis)
    last = count - 1

    early = copy_for_each(reflectors[:last], low_axis, deep)
    early = early.transpose(1, 0, 2, 3).reshape(last, deep * each, rows)
    later = lax.all_gather(early, high_axis, axis=0, tiled=False)

    first = copy_for_each(reflectors[last], (high_axis, low_axis), wide * deep)
    first = first.reshape(wide * deep * each, rows)

    current = vectors
    for position in range(last, -1, -1):
        own = first if position == last else later[:, position].reshape(-1, rows)
        other = from_partner(own)
        tri_factor = jnp.diag(tau_diag[position]) + jnp.triu(coupling[position], 1)
        tri_factor = reordered(tri_factor, wide * deep, core, each)
        terms = jnp.concatenate(two_terms(current), axis=1)
        partial_sum = jnp.concatenate([products(own, terms), products(other, terms)], axis=0)
        total = sum_everywhere(partial_sum, "prow")
        image = jnp.dot(tri_factor, total, precision=lax.Precision.HIGHEST)
        split = image.shape[0] // 2
        current = current - spread(own, image[:split]) - spread(other, image[split:])
    return current


def solution(mesh):
    finer = Mesh(
        mesh.devices.reshape(mesh.shape["prow"], 8, 4, 2), ("prow", "pcol_0", "pcol_1", "pcol_2")
    )
    placed = (P("prow", PCOL), P(None, PCOL, "prow"), P(), P())
    return jax.shard_map(
        on_device, mesh=finer, in_specs=placed, out_specs=P("prow", PCOL), check_vma=False
    )
```

time: 268 us -> 233 us (0.87)
  the two profiles are of different devices: /device:TPU:2 before, /device:TPU:4 now
where the time goes in v1:
time: 233 us; the launch traced here: 231 us
  waiting for transfers between devices  85.2 us (37%)
  starting transfers between devices  62.2 us (27%)
  matrix products  47.2 us (20%)
  local copies, waits for them, and re-layouts  17.9 us (8%)
  between operations  14 us (6%)
  other arithmetic  4.46 us (2%)
    all_to_all x10, waiting for transfers between devices, exchange(): return lax.all_to_all(parts, axis, split_axis=0, concat_axis=0, tiled=True)  85.2 us
    all_to_all x10, starting transfers between devices, exchange(): return lax.all_to_all(parts, axis, split_axis=0, concat_axis=0, tiled=True)  54.2 us
    dot_general x8, matrix products, products(): both = jnp.dot(half, terms, preferred_element_type=jnp.float32)  11.3 us
    dot_general x8, matrix products, spread(): lax.dot_general(half, high, dims, preferred_element_type=jnp.float32)  10.7 us
    dot_general x8, matrix products, spread(): lax.dot_general(half, low, dims, preferred_element_type=jnp.float32)  8.97 us
    dot_general x4, matrix products, reordered(): turned = jnp.dot(choose, tri_factor, precision=lax.Precision.HIGHEST)  8.01 us
    ppermute x4, starting transfers between devices, from_partner(): return lax.ppermute(x, 'pcol_2', [(0, 1), (1, 0)])  8 us
    dot_general x4, matrix products, reordered(): lax.dot_general(turned, choose, (((1,), (1,)), ((), ())), precision=lax.P...  5.82 us
  transfers between devices with their start and end apart: 15, of which 10 were waited for; matrix products, arithmetic and copies ran while one was open for 20% of the time, Pallas kernels for 0%

profile of v1, /device:TPU:4, one launch (start us, length us, event | category | flops | bytes accessed | tf_op | source)
XLA Modules:
  0.0 231.0 jit_solution(6790258901450145832)
XLA Ops:
  8.3 9.3 %all-to-all-start.3 = ((bf16[4,3,4,4096]{3,2,1,0:T(4,128)(2,1)}), bf16[4,3,4,4096]{3,2,1,0:T(4,128)(2,1)S(1)}, u32[]{:S(2)}, u32[]{:S(2)}) async-start(bf16[4,3,4,4096]{3,2,1,0:T(4,128)(2,1)} %broadcast_in_dim.93), calls=%async_computation.3 | async-start | bytes 786432 | tf_op jit(solution)/shard_map/all_to_all | solution.py:11
  18.4 3.6 %all-to-all-done.3 = bf16[4,3,4,4096]{3,2,1,0:T(4,128)(2,1)S(1)} async-done(((bf16[4,3,4,4096]{3,2,1,0:T(4,128)(2,1)}), bf16[4,3,4,4096]{3,2,1,0:T(4,128)(2,1)S(1)}, u32[]{:S(2)}, u32[]{:S(2)}) %all-to-all-start.3) | async-done | bytes 393248 | tf_op jit(solution)/shard_map/all_to_all | solution.py:11
  22.0 1.4 broadcast_in_dim.89
  23.5 7.2 %all-to-all-start = ((bf16[32,4,4096]{2,1,0:T(4,128)(2,1)}), bf16[32,4,4096]{2,1,0:T(4,128)(2,1)}, u32[]{:S(2)}, u32[]{:S(2)}) async-start(bf16[32,4,4096]{2,1,0:T(4,128)(2,1)} %broadcast_in_dim.89), calls=%async_computation | async-start | bytes 2097152 | tf_op jit(solution)/shard_map/all_to_all | solution.py:11
  31.8 25.5 %all-to-all-done = bf16[32,4,4096]{2,1,0:T(4,128)(2,1)} async-done(((bf16[32,4,4096]{2,1,0:T(4,128)(2,1)}), bf16[32,4,4096]{2,1,0:T(4,128)(2,1)}, u32[]{:S(2)}, u32[]{:S(2)}) %all-to-all-start) | async-done | bytes 1048608 | tf_op jit(solution)/shard_map/all_to_all | solution.py:11
  58.7 1.9 collective-permute-start
  60.6 1.7 reduce-precision_convert_fusion.3
  62.3 1.9 copy.9
  64.9 2.1 fusion.29
  67.1 1.7 fusion.28
  69.5 14.1 %all-to-all-start.1 = ((f32[8,32,128]{2,1,0:T(8,128)}), f32[8,32,128]{2,1,0:T(8,128)S(1)}, u32[]{:S(2)}, u32[]{:S(2)}) async-start(f32[8,32,128]{2,1,0:T(8,128)} %bitcast.5), calls=%async_computation.1 | async-start | bytes 262144 | tf_op jit(solution)/shard_map/all_to_all | solution.py:11
  83.6 2.2 fusion.54
  85.8 7.6 %all-to-all-done.1 = f32[8,32,128]{2,1,0:T(8,128)S(1)} async-done(((f32[8,32,128]{2,1,0:T(8,128)}), f32[8,32,128]{2,1,0:T(8,128)S(1)}, u32[]{:S(2)}, u32[]{:S(2)}) %all-to-all-start.1) | async-done | bytes 131104 | tf_op jit(solution)/shard_map/all_to_all | solution.py:11
  94.0 3.4 %all-to-all-start.2 = ((f32[8,32,128]{2,1,0:T(8,128)}), f32[8,32,128]{2,1,0:T(8,128)S(1)}, u32[]{:S(2)}, u32[]{:S(2)}) async-start(f32[8,32,128]{2,1,0:T(8,128)} %broadcast_in_dim.90), calls=%async_computation.2 | async-start | bytes 262144 | tf_op jit(solution)/shard_map/all_to_all | solution.py:11
  97.4 2.2 fusion.120
  99.6 6.8 %all-to-all-done.2 = f32[8,32,128]{2,1,0:T(8,128)S(1)} async-done(((f32[8,32,128]{2,1,0:T(8,128)}), f32[8,32,128]{2,1,0:T(8,128)S(1)}, u32[]{:S(2)}, u32[]{:S(2)}) %all-to-all-start.2) | async-done | bytes 131104 | tf_op jit(solution)/shard_map/all_to_all | solution.py:11
  108.2 1.9 fusion.15
  110.1 2.1 fusion.123
  112.2 2.1 collective-permute-start.1
  114.3 1.7 fusion.90
  115.9 3.2 %reduce-precision_convert_fusion.2 = (bf16[4096,128]{0,1:T(8,128)(2,1)S(1)}, bf16[4096,128]{0,1:T(8,128)(2,1)S(1)}, f32[4096,128]{0,1:T(8,128)}) fusion(f32[4096,128]{0,1:T(8,128)S(1)} %copy-done.3, f32[128,4096]{1,0:T(8,128)S(1)} %fusion.90, bf16[128,4096]{1,0:T(8,128)(2,1)} %collective-permute-done, f32[256,128]{1,0:T(8,128)S(1)} %fusion.125), kind=kOutput, calls=%fused_computation.29 | convolution fusion | flops 137396224 | bytes 9502720 | tf_op jit(solution)/shard_map/dot_general | solution.py:36
  121.7 3.4 %all-to-all-start.4 = ((f32[8,32,128]{2,1,0:T(8,128)}), f32[8,32,128]{2,1,0:T(8,128)S(1)}, u32[]{:S(2)}, u32[]{:S(2)}) async-start(f32[8,32,128]{2,1,0:T(8,128)} %bitcast.15), calls=%async_computation.4 | async-start | bytes 262144 | tf_op jit(solution)/shard_map/all_to_all | solution.py:11
  125.1 2.2 fusion.51
  127.3 7.7 %all-to-all-done.4 = f32[8,32,128]{2,1,0:T(8,128)S(1)} async-done(((f32[8,32,128]{2,1,0:T(8,128)}), f32[8,32,128]{2,1,0:T(8,128)S(1)}, u32[]{:S(2)}, u32[]{:S(2)}) %all-to-all-start.4) | async-done | bytes 131104 | tf_op jit(solution)/shard_map/all_to_all | solution.py:11
  135.7 3.4 %all-to-all-start.5 = ((f32[8,32,128]{2,1,0:T(8,128)}), f32[8,32,128]{2,1,0:T(8,128)S(1)}, u32[]{:S(2)}, u32[]{:S(2)}) async-start(f32[8,32,128]{2,1,0:T(8,128)} %broadcast_in_dim.94), calls=%async_computation.5 | async-start | bytes 262144 | tf_op jit(solution)/shard_map/all_to_all | solution.py:11
  139.0 1.5 fusion.117
  140.6 2.1 collective-permute-start.2
  142.7 5.7 %all-to-all-done.5 = f32[8,32,128]{2,1,0:T(8,128)S(1)} async-done(((f32[8,32,128]{2,1,0:T(8,128)}), f32[8,32,128]{2,1,0:T(8,128)S(1)}, u32[]{:S(2)}, u32[]{:S(2)}) %all-to-all-start.5) | async-done | bytes 131104 | tf_op jit(solution)/shard_map/all_to_all | solution.py:11
  151.7 2.0 reduce-precision_convert_fusion.1
  154.6 2.1 fusion.33
  157.3 3.4 %all-to-all-start.6 = ((f32[8,32,128]{2,1,0:T(8,128)}), f32[8,32,128]{2,1,0:T(8,128)S(1)}, u32[]{:S(2)}, u32[]{:S(2)}) async-start(f32[8,32,128]{2,1,0:T(8,128)} %bitcast.24), calls=%async_computation.6 | async-start | bytes 262144 | tf_op jit(solution)/shard_map/all_to_all | solution.py:11
  160.8 1.5 fusion.48
  162.2 7.5 %all-to-all-done.6 = f32[8,32,128]{2,1,0:T(8,128)S(1)} async-done(((f32[8,32,128]{2,1,0:T(8,128)}), f32[8,32,128]{2,1,0:T(8,128)S(1)}, u32[]{:S(2)}, u32[]{:S(2)}) %all-to-all-start.6) | async-done | bytes 131104 | tf_op jit(solution)/shard_map/all_to_all | solution.py:11
  170.4 3.4 %all-to-all-start.7 = ((f32[8,32,128]{2,1,0:T(8,128)}), f32[8,32,128]{2,1,0:T(8,128)S(1)}, u32[]{:S(2)}, u32[]{:S(2)}) async-start(f32[8,32,128]{2,1,0:T(8,128)} %broadcast_in_dim.97), calls=%async_computation.7 | async-start | bytes 262144 | tf_op jit(solution)/shard_map/all_to_all | solution.py:11
  174.3 1.9 collective-permute-start.3
  176.3 6.5 %all-to-all-done.7 = f32[8,32,128]{2,1,0:T(8,128)S(1)} async-done(((f32[8,32,128]{2,1,0:T(8,128)}), f32[8,32,128]{2,1,0:T(8,128)S(1)}, u32[]{:S(2)}, u32[]{:S(2)}) %all-to-all-start.7) | async-done | bytes 131104 | tf_op jit(solution)/shard_map/all_to_all | solution.py:11
  184.8 1.7 fusion.84
  186.5 1.9 reduce-precision_convert_fusion
  189.3 2.1 fusion.35
  192.1 3.4 %all-to-all-start.8 = ((f32[8,32,128]{2,1,0:T(8,128)}), f32[8,32,128]{2,1,0:T(8,128)S(1)}, u32[]{:S(2)}, u32[]{:S(2)}) async-start(f32[8,32,128]{2,1,0:T(8,128)} %bitcast.33), calls=%async_computation.8 | async-start | bytes 262144 | tf_op jit(solution)/shard_map/all_to_all | solution.py:11
  195.4 2.2 fusion.45
  197.6 6.8 %all-to-all-done.8 = f32[8,32,128]{2,1,0:T(8,128)S(1)} async-done(((f32[8,32,128]{2,1,0:T(8,128)}), f32[8,32,128]{2,1,0:T(8,128)S(1)}, u32[]{:S(2)}, u32[]{:S(2)}) %all-to-all-start.8) | async-done | bytes 131104 | tf_op jit(solution)/shard_map/all_to_all | solution.py:11
  205.1 3.4 %all-to-all-start.9 = ((f32[8,32,128]{2,1,0:T(8,128)}), f32[8,32,128]{2,1,0:T(8,128)S(1)}, u32[]{:S(2)}, u32[]{:S(2)}) async-start(f32[8,32,128]{2,1,0:T(8,128)} %broadcast_in_dim.100), calls=%async_computation.9 | async-start | bytes 262144 | tf_op jit(solution)/shard_map/all_to_all | solution.py:11
  208.5 1.5 fusion.111
  210.0 7.5 %all-to-all-done.9 = f32[8,32,128]{2,1,0:T(8,128)S(1)} async-done(((f32[8,32,128]{2,1,0:T(8,128)}), f32[8,32,128]{2,1,0:T(8,128)S(1)}, u32[]{:S(2)}, u32[]{:S(2)}) %all-to-all-start.9) | async-done | bytes 131104 | tf_op jit(solution)/shard_map/all_to_all | solution.py:11
  218.9 1.7 fusion.81
  220.6 1.7 fusion.1
  222.3 1.8 copy.11
  (84 shorter events, 23.6 us)
Async XLA Ops:
  8.3 13.7 %all-to-all-start.3 = ((bf16[4,3,4,4096]{3,2,1,0:T(4,128)(2,1)}), bf16[4,3,4,4096]{3,2,1,0:T(4,128)(2,1)S(1)}, u32[]{:S(2)}, u32[]{:S(2)}) async-start(bf16[4,3,4,4096]{3,2,1,0:T(4,128)(2,1)} %broadcast_in_dim.93), calls=%async_computation.3 | async-start | bytes 786432 | tf_op jit(solution)/shard_map/all_to_all | solution.py:11
  23.5 33.9 %all-to-all-start = ((bf16[32,4,4096]{2,1,0:T(4,128)(2,1)}), bf16[32,4,4096]{2,1,0:T(4,128)(2,1)}, u32[]{:S(2)}, u32[]{:S(2)}) async-start(bf16[32,4,4096]{2,1,0:T(4,128)(2,1)} %broadcast_in_dim.89), calls=%async_computation | async-start | bytes 2097152 | tf_op jit(solution)/shard_map/all_to_all | solution.py:11
  30.7 29.9 %copy-start = (f32[4096,128]{1,0:T(8,128)S(1)}, f32[4096,128]{1,0:T(8,128)}, u32[]{:S(2)}) copy-start(f32[4096,128]{1,0:T(8,128)} %param.4) | copy-start | bytes 6291460
  30.7 79.3 %all-gather.2.cloned.1.call-start = ((), (), s32[]{:S(2)}) async-start(), calls=%async_computation.10 | async-start | bytes 3538944 | tf_op jit(solution)/shard_map/all_gather | solution.py:68
  58.7 8.4 %collective-permute-start = (bf16[128,4096]{1,0:T(8,128)(2,1)S(1)}, bf16[128,4096]{1,0:T(8,128)(2,1)}, u32[]{:S(2)}, u32[]{:S(2)}) collective-permute-start(bf16[128,4096]{1,0:T(8,128)(2,1)S(1)} %reshape.35), channel_id=1, source_target_pairs={{0,1},{1,0},{2,3},{3,2},{4,5},{5,4},{6,7},{7,6},{8,9},{9,8},{10,11... | collective-permute-start | bytes 3145736 | tf_op jit(solution)/shard_map/ppermute | solution.py:19
  62.3 2.0 copy-start.8
  64.3 60.8 %copy-start.11 = (pred[256]{0:T(512)(128)(4,1)}, pred[256]{0:T(512)(128)(4,1)S(1)}, u32[]{:S(2)}) copy-start(pred[256]{0:T(512)(128)(4,1)S(1)} %get-tuple-element.23) | copy-start | bytes 772
  64.3 60.8 %copy-start.13 = (pred[256]{0:T(512)(128)(4,1)}, pred[256]{0:T(512)(128)(4,1)S(1)}, u32[]{:S(2)}) copy-start(pred[256]{0:T(512)(128)(4,1)S(1)} %get-tuple-element.24) | copy-start | bytes 772
  64.9 2.2 copy-start.6
  64.9 2.2 copy-start.7
  69.5 23.8 %all-to-all-start.1 = ((f32[8,32,128]{2,1,0:T(8,128)}), f32[8,32,128]{2,1,0:T(8,128)S(1)}, u32[]{:S(2)}, u32[]{:S(2)}) async-start(f32[8,32,128]{2,1,0:T(8,128)} %bitcast.5), calls=%async_computation.1 | async-start | bytes 262144 | tf_op jit(solution)/shard_map/all_to_all | solution.py:11
  94.0 12.4 %all-to-all-start.2 = ((f32[8,32,128]{2,1,0:T(8,128)}), f32[8,32,128]{2,1,0:T(8,128)S(1)}, u32[]{:S(2)}, u32[]{:S(2)}) async-start(f32[8,32,128]{2,1,0:T(8,128)} %broadcast_in_dim.90), calls=%async_computation.2 | async-start | bytes 262144 | tf_op jit(solution)/shard_map/all_to_all | solution.py:11
  112.2 3.8 %copy-start.3 = (f32[4096,128]{0,1:T(8,128)S(1)}, f32[4096,128]{0,1:T(8,128)}, u32[]{:S(2)}) copy-start(f32[4096,128]{0,1:T(8,128)} %fusion.15) | copy-start | bytes 6291460
  112.2 7.8 %collective-permute-start.1 = (bf16[128,4096]{1,0:T(8,128)(2,1)S(1)}, bf16[128,4096]{1,0:T(8,128)(2,1)S(1)}, u32[]{:S(2)}, u32[]{:S(2)}) collective-permute-start(bf16[128,4096]{1,0:T(8,128)(2,1)S(1)} %bitcast.130), channel_id=1, source_target_pairs={{0,1},{1,0},{2,3},{3,2},{4,5},{5,4},{6,7},{7,6},{8,9},{9,8},{10,11... | collective-permute-start | bytes 3145736 | tf_op jit(solution)/shard_map/ppermute | solution.py:19
  120.0 1.0 copy-start.4
  121.7 13.3 %all-to-all-start.4 = ((f32[8,32,128]{2,1,0:T(8,128)}), f32[8,32,128]{2,1,0:T(8,128)S(1)}, u32[]{:S(2)}, u32[]{:S(2)}) async-start(f32[8,32,128]{2,1,0:T(8,128)} %bitcast.15), calls=%async_computation.4 | async-start | bytes 262144 | tf_op jit(solution)/shard_map/all_to_all | solution.py:11
  135.7 12.8 %all-to-all-start.5 = ((f32[8,32,128]{2,1,0:T(8,128)}), f32[8,32,128]{2,1,0:T(8,128)S(1)}, u32[]{:S(2)}, u32[]{:S(2)}) async-start(f32[8,32,128]{2,1,0:T(8,128)} %broadcast_in_dim.94), calls=%async_computation.5 | async-start | bytes 262144 | tf_op jit(solution)/shard_map/all_to_all | solution.py:11
  140.6 14.0 %collective-permute-start.2 = (bf16[128,4096]{1,0:T(8,128)(2,1)S(1)}, bf16[128,4096]{1,0:T(8,128)(2,1)}, u32[]{:S(2)}, u32[]{:S(2)}) collective-permute-start(bf16[128,4096]{1,0:T(8,128)(2,1)S(1)} %bitcast.126), channel_id=1, source_target_pairs={{0,1},{1,0},{2,3},{3,2},{4,5},{5,4},{6,7},{7,6},{8,9},{9,8},{10,11... | collective-permute-start | bytes 3145736 | tf_op jit(solution)/shard_map/ppermute | solution.py:19
  148.4 1.6 copy-start.2
  150.0 1.2 copy-start.5
  154.6 6.2 %copy-start.10 = (f32[1,256]{1,0:T(1,128)S(1)}, f32[1,256]{1,0:T(1,128)}, u32[]{:S(2)}) copy-start(f32[1,256]{1,0:T(1,128)} %get-tuple-element.19) | copy-start | bytes 3076
  154.6 6.2 %copy-start.12 = (pred[256]{0:T(512)(128)(4,1)S(1)}, pred[256]{0:T(512)(128)(4,1)}, u32[]{:S(2)}) copy-start(pred[256]{0:T(512)(128)(4,1)} %copy-done.11) | copy-start | bytes 772
  154.6 6.2 %copy-start.14 = (pred[256]{0:T(512)(128)(4,1)S(1)}, pred[256]{0:T(512)(128)(4,1)}, u32[]{:S(2)}) copy-start(pred[256]{0:T(512)(128)(4,1)} %copy-done.13) | copy-start | bytes 772
  157.3 12.4 %all-to-all-start.6 = ((f32[8,32,128]{2,1,0:T(8,128)}), f32[8,32,128]{2,1,0:T(8,128)S(1)}, u32[]{:S(2)}, u32[]{:S(2)}) async-start(f32[8,32,128]{2,1,0:T(8,128)} %bitcast.24), calls=%async_computation.6 | async-start | bytes 262144 | tf_op jit(solution)/shard_map/all_to_all | solution.py:11
  170.4 12.4 %all-to-all-start.7 = ((f32[8,32,128]{2,1,0:T(8,128)}), f32[8,32,128]{2,1,0:T(8,128)S(1)}, u32[]{:S(2)}, u32[]{:S(2)}) async-start(f32[8,32,128]{2,1,0:T(8,128)} %broadcast_in_dim.97), calls=%async_computation.7 | async-start | bytes 262144 | tf_op jit(solution)/shard_map/all_to_all | solution.py:11
  174.3 15.0 %collective-permute-start.3 = (bf16[128,4096]{1,0:T(8,128)(2,1)S(1)}, bf16[128,4096]{1,0:T(8,128)(2,1)}, u32[]{:S(2)}, u32[]{:S(2)}) collective-permute-start(bf16[128,4096]{1,0:T(8,128)(2,1)S(1)} %bitcast.122), channel_id=1, source_target_pairs={{0,1},{1,0},{2,3},{3,2},{4,5},{5,4},{6,7},{7,6},{8,9},{9,8},{10,11... | collective-permute-start | bytes 3145736 | tf_op jit(solution)/shard_map/ppermute | solution.py:19
  182.7 1.6 copy-start.1
  189.3 6.2 %copy-start.9 = (f32[1,256]{1,0:T(1,128)S(1)}, f32[1,256]{1,0:T(1,128)}, u32[]{:S(2)}) copy-start(f32[1,256]{1,0:T(1,128)} %get-tuple-element.16) | copy-start | bytes 3076
  192.1 12.4 %all-to-all-start.8 = ((f32[8,32,128]{2,1,0:T(8,128)}), f32[8,32,128]{2,1,0:T(8,128)S(1)}, u32[]{:S(2)}, u32[]{:S(2)}) async-start(f32[8,32,128]{2,1,0:T(8,128)} %bitcast.33), calls=%async_computation.8 | async-start | bytes 262144 | tf_op jit(solution)/shard_map/all_to_all | solution.py:11
  205.1 12.4 %all-to-all-start.9 = ((f32[8,32,128]{2,1,0:T(8,128)}), f32[8,32,128]{2,1,0:T(8,128)S(1)}, u32[]{:S(2)}, u32[]{:S(2)}) async-start(f32[8,32,128]{2,1,0:T(8,128)} %broadcast_in_dim.100), calls=%async_computation.9 | async-start | bytes 262144 | tf_op jit(solution)/shard_map/all_to_all | solution.py:11
Sparse Core Ops, SparseCore 0:
  33.6 51.8 all-gather.1

commit v2 on v1

v2 whole, which is shorter than its diff:
```python
import functools

import jax
import jax.numpy as jnp
from jax import lax
from jax.experimental import pallas as pl
from jax.experimental.pallas import tpu as pltpu
from jax.sharding import Mesh
from jax.sharding import PartitionSpec as P

PCOL = ("pcol_0", "pcol_1", "pcol_2")
CHUNK = 512
ROWS_BY_LANES = (((1,), (1,)), ((), ()))


def exchange(parts, axis):
    return lax.all_to_all(parts, axis, split_axis=0, concat_axis=0, tiled=True)


def copy_for_each(x, axis, devices):
    return exchange(jnp.broadcast_to(x, (devices, *x.shape)), axis)


def from_partner(x):
    return lax.ppermute(x, "pcol_2", [(0, 1), (1, 0)])


def two_terms(x):
    high = x.astype(jnp.bfloat16)
    low = (x - high.astype(jnp.float32)).astype(jnp.bfloat16)
    return jnp.concatenate([high, low], axis=0)


def folded(x):
    half = x.shape[0] // 2
    return x[:half] + x[half:]


def lanes(step):
    return pl.ds(pl.multiple_of(step * CHUNK, CHUNK), CHUNK)


def local_call(kernel, shapes, flops, *operands):
    whole = pl.BlockSpec(memory_space=pltpu.VMEM)
    moved = sum(x.size * x.dtype.itemsize for x in operands)
    single = not isinstance(shapes, (list, tuple))
    return pl.pallas_call(
        kernel,
        out_shape=shapes,
        in_specs=[whole] * len(operands),
        out_specs=whole if single else [whole] * len(shapes),
        cost_estimate=pl.CostEstimate(flops=flops, bytes_accessed=moved, transcendentals=0),
        compiler_params=pltpu.CompilerParams(vmem_limit_bytes=24 << 20),
    )(*operands)


def product_kernel(z_ref, half_ref, sums_ref):
    def step(i, total):
        terms = two_terms(z_ref[:, lanes(i)])
        return total + lax.dot_general(
            terms, half_ref[:, lanes(i)], ROWS_BY_LANES, preferred_element_type=jnp.float32
        )

    rows, depth = z_ref.shape
    start = jnp.zeros((2 * rows, half_ref.shape[0]), jnp.float32)
    sums_ref[...] = folded(lax.fori_loop(0, depth // CHUNK, step, start))


def second_product_kernel(z_ref, half_ref, before_ref, sums_ref):
    width = half_ref.shape[0]
    sums_ref[:, :width] = before_ref[...]
    product_kernel(z_ref, half_ref, sums_ref.at[:, width:])


def joined(refs, i):
    return jnp.concatenate([ref[:, lanes(i)] for ref in refs], axis=0)


def step_kernel(z_ref, image_ref, *refs):
    *used_refs, next_ref, new_ref, sums_ref = refs
    image = two_terms(image_ref[...])

    def step(i, total):
        change = jnp.dot(image, joined(used_refs, i), preferred_element_type=jnp.float32)
        current = z_ref[:, lanes(i)] - folded(change)
        new_ref[:, lanes(i)] = current
        return total + lax.dot_general(
            two_terms(current), next_ref[:, lanes(i)], ROWS_BY_LANES, preferred_element_type=jnp.float32
        )

    rows, depth = z_ref.shape
    start = jnp.zeros((2 * rows, next_ref.shape[0]), jnp.float32)
    sums_ref[...] = folded(lax.fori_loop(0, depth // CHUNK, step, start))


def last_kernel(z_ref, image_ref, used_ref, result_ref):
    image = two_terms(image_ref[...])

    def step(i, carry):
        change = jnp.dot(image, used_ref[:, lanes(i)], preferred_element_type=jnp.float32)
        result_ref[lanes(i), :] = (z_ref[:, lanes(i)] - folded(change)).T
        return carry

    lax.fori_loop(0, z_ref.shape[1] // CHUNK, step, 0)


def share_kernel(parts_ref, tri_ref, copies_ref):
    devices = parts_ref.shape[0]
    total = parts_ref[0]
    for device in range(1, devices):
        total = total + parts_ref[device]
    image = lax.dot_general(
        total,
        tri_ref[...],
        ROWS_BY_LANES,
        precision=lax.Precision.HIGHEST,
        preferred_element_type=jnp.float32,
    )
    for device in range(devices):
        copies_ref[device] = image


def share_copies(sums, tri_factor, axis):
    devices = lax.axis_size(axis)
    columns, size = sums.shape
    shape = jax.ShapeDtypeStruct((devices, columns // devices, size), jnp.float32)
    arrived = exchange(sums.reshape(shape.shape), axis)
    flops = 2 * columns // devices * size * size
    return local_call(share_kernel, shape, flops, arrived, tri_factor)


def after(x, *earlier):
    return lax.optimization_barrier((x, *earlier))[0]


def reordered(tri_factor, wanted):
    size = tri_factor.shape[0]
    source = lax.broadcasted_iota(jnp.int32, (size, size), 1)
    choose = (wanted == source).astype(jnp.float32)
    turned = jnp.dot(choose, tri_factor, precision=lax.Precision.HIGHEST)
    return lax.dot_general(turned, choose, ROWS_BY_LANES, precision=lax.Precision.HIGHEST)


def on_device(vectors, reflectors, tau_diag, coupling):
    count, each, rows = reflectors.shape
    high_axis, low_axis, core_axis = PCOL
    wide, deep = lax.axis_size(high_axis), lax.axis_size(low_axis)
    core = lax.axis_index(core_axis)
    last = count - 1
    half = wide * deep * each
    columns = vectors.shape[1]

    early = copy_for_each(reflectors[:last], low_axis, deep)
    early = early.transpose(1, 0, 2, 3).reshape(last, deep * each, rows)
    later = lax.all_gather(early, (high_axis, core_axis), axis=0, tiled=False)

    start = after(reflectors[last], early)
    first = copy_for_each(start, (high_axis, low_axis), wide * deep).reshape(half, rows)
    partner = from_partner(first)

    place = lax.broadcasted_iota(jnp.int32, (2 * half, 2 * half), 0)
    parity = jnp.where(place // half == 0, core, 1 - core)
    rest = place % half
    alone = (rest // each * 2 + parity) * each + rest % each
    spot, inner = place // each, place % each
    high, mid, low = spot // (2 * deep), spot // deep % 2, spot % deep
    together = ((high * deep + low) * 2 + mid) * each + inner

    def factor(position):
        tri_factor = jnp.diag(tau_diag[position]) + jnp.triu(coupling[position], 1)
        return reordered(tri_factor, alone if position == last else together)

    factors = [factor(position) for position in range(count)]
    current = after(vectors.T, *factors)
    pass_flops = 4 * columns * half * rows
    sums_shape = jax.ShapeDtypeStruct((columns, 2 * half), jnp.float32)
    own_shape = jax.ShapeDtypeStruct((columns, half), jnp.float32)
    z_shape = jax.ShapeDtypeStruct(current.shape, jnp.float32)
    sums = local_call(product_kernel, own_shape, pass_flops, current, first)
    sums = local_call(second_product_kernel, sums_shape, pass_flops, current, partner, sums)

    panels = None
    used = [first, partner]
    for k in range(last, -1, -1):
        copies = share_copies(sums, factors[k], "prow")
        if panels is None:
            gathered = after(later, copies)
            panels = [gathered[:, p].reshape(2 * half, rows) for p in range(last)]
        image = exchange(copies, "prow").reshape(columns, 2 * half)
        if k > 0:
            following = panels[k - 1]
            current, sums = local_call(
                step_kernel, [z_shape, sums_shape], 4 * pass_flops, current, image, *used, following
            )
            used = [following]
    result = jax.ShapeDtypeStruct(vectors.shape, jnp.float32)
    return local_call(last_kernel, result, 2 * pass_flops, current, image, *used)


def solution(mesh):
    finer = Mesh(
        mesh.devices.reshape(mesh.shape["prow"], 8, 4, 2), ("prow", "pcol_0", "pcol_1", "pcol_2")
    )
    placed = (P("prow", PCOL), P(None, PCOL, "prow"), P(), P())
    return jax.shard_map(
        on_device, mesh=finer, in_specs=placed, out_specs=P("prow", PCOL), check_vma=False
    )
```

time: 233 us -> 216 us (0.927)
  the two profiles are of different devices: /device:TPU:4 before, /device:TPU:2 now
where the time goes in v2:
time: 216 us; the launch traced here: 215 us
  blocking collectives  107 us (50%)
  waiting for transfers between devices  34.9 us (16%)
  Pallas kernels  23 us (11%)
  local copies, waits for them, and re-layouts  14 us (6%)
  between operations  13.7 us (6%)
  starting transfers between devices  11.7 us (5%)
  matrix products  10.9 us (5%)
    all_to_all x8, blocking collectives, exchange(): return lax.all_to_all(parts, axis, split_axis=0, concat_axis=0, tiled=True)  107 us
    all_to_all x2, waiting for transfers between devices, exchange(): return lax.all_to_all(parts, axis, split_axis=0, concat_axis=0, tiled=True)  34.9 us
    pallas_call x10, Pallas kernels, local_call(): pl.pallas_call(kernel, out_shape=shapes, in_specs=[whole] * len(operands)...  23 us
    all_to_all x2, starting transfers between devices, exchange(): return lax.all_to_all(parts, axis, split_axis=0, concat_axis=0, tiled=True)  9.73 us
    dot_general x4, matrix products, reordered(): turned = jnp.dot(choose, tri_factor, precision=lax.Precision.HIGHEST)  6.26 us
    slice x1, local copies, waits for them, and re-layouts, on_device(): panels = [gathered[:, p].reshape(2 * half, rows) for p in range(last)]  5.87 us
    dot_general x4, matrix products, reordered(): lax.dot_general(turned, choose, ROWS_BY_LANES, precision=lax.Precision.HI...  4.64 us
  transfers between devices with their start and end apart: 4, of which 2 were waited for; matrix products, arithmetic and copies ran while one was open for 10% of the time, Pallas kernels for 3%

profile of v2, /device:TPU:2, one launch (start us, length us, event | category | flops | bytes accessed | tf_op | source)
XLA Modules:
  0.0 215.0 jit_solution(12439868177254655233)
XLA Ops:
  6.5 0.9 slice.48
  7.5 0.1 broadcast_in_dim.78
  7.6 14.2 %all_to_all.50 = bf16[4,3,4,4096]{3,2,1,0:T(4,128)(2,1)S(1)} all-to-all(bf16[4,3,4,4096]{3,2,1,0:T(4,128)(2,1)S(1)} %broadcast_in_dim.78), channel_id=1, replica_groups=mesh['prow'=8,'pcol_0'=8,'pcol_1'=4,'pcol_2'=2] {'pcol_1'}, dimensions={0} | all-to-all | bytes 786432 | tf_op jit(solution)/shard_map/all_to_all | solution.py:17
  21.8 0.2 copy.10
  22.0 0.0 copy-start.7
  22.0 0.8 all_gather_reshape.3
  22.9 0.0 all-gather.2.cloned.1.call-update
  22.9 0.8 slice_bitcast_fusion
  23.7 1.4 broadcast_in_dim.77
  25.1 6.4 %all-to-all-start = ((bf16[32,4,4096]{2,1,0:T(4,128)(2,1)}), bf16[32,4,4096]{2,1,0:T(4,128)(2,1)S(1)}, u32[]{:S(2)}, u32[]{:S(2)}) async-start(bf16[32,4,4096]{2,1,0:T(4,128)(2,1)} %broadcast_in_dim.77), calls=%async_computation | async-start | bytes 2097152 | tf_op jit(solution)/shard_map/all_to_all | solution.py:17
  31.6 1.6 fusion.29
  33.2 0.7 fusion.69.tri_ref
  33.8 1.5 fusion.23
  35.3 31.8 %all-to-all-done = bf16[32,4,4096]{2,1,0:T(4,128)(2,1)S(1)} async-done(((bf16[32,4,4096]{2,1,0:T(4,128)(2,1)}), bf16[32,4,4096]{2,1,0:T(4,128)(2,1)S(1)}, u32[]{:S(2)}, u32[]{:S(2)}) %all-to-all-start) | async-done | bytes 1048608 | tf_op jit(solution)/shard_map/all_to_all | solution.py:17
  67.1 0.3 reshape.36.half_ref.refs_0_
  67.4 1.9 collective-permute-start
  69.3 1.3 fusion.63.tri_ref
  70.5 1.9 copy.9
  72.5 1.6 fusion.32
  74.1 1.4 fusion.72.tri_ref
  75.4 1.6 fusion.26
  77.0 1.4 fusion.66.tri_ref
  78.4 1.9 shard_map.46.before_ref
  80.3 0.0 copy-start.6
  80.3 0.0 collective-permute-done.half_ref.refs_1_
  80.3 3.2 %shard_map.47 = f32[128,256]{1,0:T(8,128)S(1)} custom-call(f32[128,4096]{1,0:T(8,128)S(1)} %bitcast.44, bf16[128,4096]{1,0:T(8,128)(2,1)} %collective-permute-done.half_ref.refs_1_, f32[128,128]{1,0:T(8,128)S(1)} %shard_map.46.before_ref), custom_call_target="tpu_custom_call" | custom-call | flops 268435456 | bytes 3211264 | tf_op jit(solution)/shard_map/pallas_call | solution.py:47
  83.6 22.3 %all_to_all.51.parts_ref = f32[8,16,256]{2,1,0:T(8,128)S(1)} all-to-all(f32[8,16,256]{2,1,0:T(8,128)S(1)} %bitcast.56), channel_id=1, replica_groups=mesh['prow'=8,'pcol_0'=8,'pcol_1'=4,'pcol_2'=2] {'prow'}, dimensions={0} | all-to-all | bytes 262144 | tf_op jit(solution)/shard_map/all_to_all | solution.py:17
  105.9 1.0 shard_map.48
  106.9 3.4 %all-to-all-start.2 = ((f32[8,16,256]{2,1,0:T(8,128)}), f32[8,16,256]{2,1,0:T(8,128)S(1)}, u32[]{:S(2)}, u32[]{:S(2)}) async-start(f32[8,16,256]{2,1,0:T(8,128)} %shard_map.48), calls=%async_computation.2 | async-start | bytes 262144 | tf_op jit(solution)/shard_map/all_to_all | solution.py:17
  110.3 0.0 all-gather.2.cloned.1.call-done
  110.3 5.9 %fusion.75 = (bf16[16,1,16,4096]{3,2,1,0:T(8,128)(2,1)}, bf16[16,1,16,4096]{3,2,1,0:T(8,128)(2,1)}, bf16[16,1,16,4096]{3,2,1,0:T(8,128)(2,1)}) fusion(bf16[16,3,16,4096]{3,2,1,0:T(8,128)(2,1)} %all-gather.2.cloned.1.call-done), kind=kLoop, calls=%fused_computation.102 | loop fusion | bytes 12582912 | tf_op jit(solution)/shard_map/slice | solution.py:188
  116.2 3.1 %all-to-all-done.2 = f32[8,16,256]{2,1,0:T(8,128)S(1)} async-done(((f32[8,16,256]{2,1,0:T(8,128)}), f32[8,16,256]{2,1,0:T(8,128)S(1)}, u32[]{:S(2)}, u32[]{:S(2)}) %all-to-all-start.2) | async-done | bytes 131104 | tf_op jit(solution)/shard_map/all_to_all | solution.py:17
  119.3 1.6 copy-done.2
  120.9 4.9 %shard_map.49 = (f32[128,4096]{1,0:T(8,128)S(1)}, f32[128,256]{1,0:T(8,128)S(1)}) custom-call(f32[128,4096]{1,0:T(8,128)S(1)} %bitcast.45, f32[128,256]{1,0:T(8,128)S(1)} %bitcast.52, bf16[128,4096]{1,0:T(8,128)(2,1)S(1)} %reshape.36.half_ref.refs_0_, bf16[128,4096]{1,0:T(8,128)(2,1)} %collective-permute-done.half_ref.refs_1_, bf16[256,4096]{1,0:T(8,128)(2,1)S(1)} %bitcast.50), custom_call_target="tpu_custom_call" | custom-call | flops 1073741824 | bytes 6422528 | tf_op jit(solution)/shard_map/pallas_call | solution.py:47
  125.7 12.9 %all_to_all.52.parts_ref = f32[8,16,256]{2,1,0:T(8,128)S(1)} all-to-all(f32[8,16,256]{2,1,0:T(8,128)S(1)} %bitcast.57), channel_id=1, replica_groups=mesh['prow'=8,'pcol_0'=8,'pcol_1'=4,'pcol_2'=2] {'prow'}, dimensions={0} | all-to-all | bytes 262144 | tf_op jit(solution)/shard_map/all_to_all | solution.py:17
  138.6 0.3 shard_map.50
  138.9 11.5 %all_to_all.53 = f32[8,16,256]{2,1,0:T(8,128)S(1)} all-to-all(f32[8,16,256]{2,1,0:T(8,128)S(1)} %shard_map.50), channel_id=1, replica_groups=mesh['prow'=8,'pcol_0'=8,'pcol_1'=4,'pcol_2'=2] {'prow'}, dimensions={0} | all-to-all | bytes 262144 | tf_op jit(solution)/shard_map/all_to_all | solution.py:17
  150.4 3.5 %shard_map.51 = (f32[128,4096]{1,0:T(8,128)S(1)}, f32[128,256]{1,0:T(8,128)S(1)}) custom-call(f32[128,4096]{1,0:T(8,128)S(1)} %get-tuple-element.15.z_ref, f32[128,256]{1,0:T(8,128)S(1)} %bitcast.54, bf16[256,4096]{1,0:T(8,128)(2,1)S(1)} %bitcast.51, bf16[256,4096]{1,0:T(8,128)(2,1)S(1)} %bitcast.48), custom_call_target="tpu_custom_call" | custom-call | flops 1073741824 | bytes 6422528 | tf_op jit(solution)/shard_map/pallas_call | solution.py:47
  154.0 11.5 %all_to_all.54.parts_ref = f32[8,16,256]{2,1,0:T(8,128)S(1)} all-to-all(f32[8,16,256]{2,1,0:T(8,128)S(1)} %bitcast.58), channel_id=1, replica_groups=mesh['prow'=8,'pcol_0'=8,'pcol_1'=4,'pcol_2'=2] {'prow'}, dimensions={0} | all-to-all | bytes 262144 | tf_op jit(solution)/shard_map/all_to_all | solution.py:17
  165.4 0.3 shard_map.52
  165.8 11.5 %all_to_all.55 = f32[8,16,256]{2,1,0:T(8,128)S(1)} all-to-all(f32[8,16,256]{2,1,0:T(8,128)S(1)} %shard_map.52), channel_id=1, replica_groups=mesh['prow'=8,'pcol_0'=8,'pcol_1'=4,'pcol_2'=2] {'prow'}, dimensions={0} | all-to-all | bytes 262144 | tf_op jit(solution)/shard_map/all_to_all | solution.py:17
  177.2 0.0 copy-done
  177.2 3.5 %shard_map.53 = (f32[128,4096]{1,0:T(8,128)S(1)}, f32[128,256]{1,0:T(8,128)S(1)}) custom-call(f32[128,4096]{1,0:T(8,128)S(1)} %get-tuple-element.17.z_ref, f32[128,256]{1,0:T(8,128)S(1)} %bitcast.53, bf16[256,4096]{1,0:T(8,128)(2,1)S(1)} %bitcast.49, bf16[256,4096]{1,0:T(8,128)(2,1)S(1)} %bitcast.46), custom_call_target="tpu_custom_call" | custom-call | flops 1073741824 | bytes 6422528 | tf_op jit(solution)/shard_map/pallas_call | solution.py:47
  180.8 11.6 %all_to_all.56.parts_ref = f32[8,16,256]{2,1,0:T(8,128)S(1)} all-to-all(f32[8,16,256]{2,1,0:T(8,128)S(1)} %bitcast.59), channel_id=1, replica_groups=mesh['prow'=8,'pcol_0'=8,'pcol_1'=4,'pcol_2'=2] {'prow'}, dimensions={0} | all-to-all | bytes 262144 | tf_op jit(solution)/shard_map/all_to_all | solution.py:17
  192.3 0.0 copy-done.4
  192.3 0.3 shard_map.54
  192.7 11.5 %all_to_all.57 = f32[8,16,256]{2,1,0:T(8,128)S(1)} all-to-all(f32[8,16,256]{2,1,0:T(8,128)S(1)} %shard_map.54), channel_id=1, replica_groups=mesh['prow'=8,'pcol_0'=8,'pcol_1'=4,'pcol_2'=2] {'prow'}, dimensions={0} | all-to-all | bytes 262144 | tf_op jit(solution)/shard_map/all_to_all | solution.py:17
  204.1 4.0 %shard_map.55 = f32[4096,128]{1,0:T(8,128)} custom-call(f32[128,4096]{1,0:T(8,128)S(1)} %get-tuple-element.19.z_ref, f32[128,256]{1,0:T(8,128)S(1)} %bitcast.55, bf16[256,4096]{1,0:T(8,128)(2,1)S(1)} %bitcast.47), custom_call_target="tpu_custom_call" | custom-call | flops 536870912 | bytes 4325376 | tf_op jit(solution)/shard_map/pallas_call | solution.py:47
  (19 shorter events, 0.1 us)
Async XLA Ops:
  6.5 103.8 %all-gather.2.cloned.1.call-start = ((), (), s32[]{:S(2)}) async-start(), calls=%async_computation.10 | async-start | bytes 6684672 | tf_op jit(solution)/shard_map/all_gather | solution.py:155
  22.0 9.6 %copy-start.7 = (f32[4,256]{1,0:T(4,128)S(1)}, f32[4,256]{1,0:T(4,128)}, u32[]{:S(2)}) copy-start(f32[4,256]{1,0:T(4,128)} %param.6) | copy-start | bytes 12292
  25.1 42.0 %all-to-all-start = ((bf16[32,4,4096]{2,1,0:T(4,128)(2,1)}), bf16[32,4,4096]{2,1,0:T(4,128)(2,1)S(1)}, u32[]{:S(2)}, u32[]{:S(2)}) async-start(bf16[32,4,4096]{2,1,0:T(4,128)(2,1)} %broadcast_in_dim.77), calls=%async_computation | async-start | bytes 2097152 | tf_op jit(solution)/shard_map/all_to_all | solution.py:17
  67.4 13.0 %collective-permute-start = (bf16[128,4096]{1,0:T(8,128)(2,1)S(1)}, bf16[128,4096]{1,0:T(8,128)(2,1)}, u32[]{:S(2)}, u32[]{:S(2)}) collective-permute-start(bf16[128,4096]{1,0:T(8,128)(2,1)S(1)} %reshape.36.half_ref.refs_0_), channel_id=1, source_target_pairs={{0,1},{1,0},{2,3},{3,2},{4,5},{5,4},{6,7},{7,6},{8,9},{9,8},{10,11... | collective-permute-start | bytes 3145736 | tf_op jit(solution)/shard_map/ppermute | solution.py:25
  80.3 25.6 %copy-start.6 = (f32[256,256]{1,0:T(8,128)S(1)}, f32[256,256]{1,0:T(8,128)}, u32[]{:S(2)}) copy-start(f32[256,256]{1,0:T(8,128)} %fusion.63.tri_ref) | copy-start | bytes 786436
  106.9 12.4 %all-to-all-start.2 = ((f32[8,16,256]{2,1,0:T(8,128)}), f32[8,16,256]{2,1,0:T(8,128)S(1)}, u32[]{:S(2)}, u32[]{:S(2)}) async-start(f32[8,16,256]{2,1,0:T(8,128)} %shard_map.48), calls=%async_computation.2 | async-start | bytes 262144 | tf_op jit(solution)/shard_map/all_to_all | solution.py:17
  119.3 1.6 copy-start.2
  120.9 17.8 %copy-start.5 = (f32[256,256]{1,0:T(8,128)S(1)}, f32[256,256]{1,0:T(8,128)}, u32[]{:S(2)}) copy-start(f32[256,256]{1,0:T(8,128)} %fusion.66.tri_ref) | copy-start | bytes 786436
  120.9 29.6 %copy-start.1 = (bf16[16,1,16,4096]{3,2,1,0:T(8,128)(2,1)S(1)}, bf16[16,1,16,4096]{3,2,1,0:T(8,128)(2,1)}, u32[]{:S(2)}) copy-start(bf16[16,1,16,4096]{3,2,1,0:T(8,128)(2,1)} %get-tuple-element.22) | copy-start | bytes 6291460
  120.9 29.6 %copy-start.3 = (bf16[16,1,16,4096]{3,2,1,0:T(8,128)(2,1)S(1)}, bf16[16,1,16,4096]{3,2,1,0:T(8,128)(2,1)}, u32[]{:S(2)}) copy-start(bf16[16,1,16,4096]{3,2,1,0:T(8,128)(2,1)} %get-tuple-element.23) | copy-start | bytes 6291460
  150.4 26.8 %copy-start = (bf16[16,1,16,4096]{3,2,1,0:T(8,128)(2,1)S(1)}, bf16[16,1,16,4096]{3,2,1,0:T(8,128)(2,1)}, u32[]{:S(2)}) copy-start(bf16[16,1,16,4096]{3,2,1,0:T(8,128)(2,1)} %get-tuple-element.21) | copy-start | bytes 6291460
  177.2 15.1 %copy-start.4 = (f32[256,256]{1,0:T(8,128)S(1)}, f32[256,256]{1,0:T(8,128)}, u32[]{:S(2)}) copy-start(f32[256,256]{1,0:T(8,128)} %fusion.72.tri_ref) | copy-start | bytes 786436
Sparse Core Ops, SparseCore 0:
  23.0 63.8 all-gather.1

commit v3 on v1

v3 whole, which is shorter than its diff:
```python
import jax
import jax.numpy as jnp
from jax import lax
from jax.experimental import pallas as pl
from jax.experimental.pallas import tpu as pltpu
from jax.sharding import Mesh
from jax.sharding import PartitionSpec as P


PCOL = ("pcol_0", "pcol_1", "pcol_2")
CHUNK = 512
ROWS_BY_LANES = (((1,), (1,)), ((), ()))


def exchange(parts, axis):
    return lax.all_to_all(parts, axis, split_axis=0, concat_axis=0, tiled=True)


def copy_for_each(x, axis, devices):
    return exchange(jnp.broadcast_to(x, (devices, *x.shape)), axis)


def from_partner(x):
    return lax.ppermute(x, "pcol_2", [(0, 1), (1, 0)])


def shifted(x, axis, by):
    devices = lax.axis_size(axis)
    return lax.ppermute(x, axis, [(i, (i + by) % devices) for i in range(devices)])


def after(x, *earlier):
    return lax.optimization_barrier((x, *earlier))[0]


def two_terms(x):
    high = x.astype(jnp.bfloat16)
    low = (x - high.astype(jnp.float32)).astype(jnp.bfloat16)
    return jnp.concatenate([high, low], axis=0)


def lanes(step):
    return pl.ds(pl.multiple_of(step * CHUNK, CHUNK), CHUNK)


def local_call(kernel, shapes, flops, *operands, scratch=()):
    whole = pl.BlockSpec(memory_space=pltpu.VMEM)
    moved = sum(x.size * x.dtype.itemsize for x in operands)
    single = not isinstance(shapes, (list, tuple))
    return pl.pallas_call(
        kernel,
        out_shape=shapes,
        in_specs=[whole] * len(operands),
        out_specs=whole if single else [whole] * len(shapes),
        scratch_shapes=scratch,
        cost_estimate=pl.CostEstimate(flops=flops, bytes_accessed=moved, transcendentals=0),
        compiler_params=pltpu.CompilerParams(vmem_limit_bytes=24 << 20),
    )(*operands)


def products(half_ref, terms_ref):
    both = lax.dot_general(
        half_ref[...], terms_ref[...], ROWS_BY_LANES, preferred_element_type=jnp.float32
    )
    columns = both.shape[1] // 2
    return both[:, :columns] + both[:, columns:]


def split_kernel(z_ref, turned_ref, terms_ref):
    def step(i, carry):
        turned = z_ref[lanes(i), :].T
        turned_ref[:, lanes(i)] = turned
        terms_ref[:, lanes(i)] = two_terms(turned)
        return carry

    lax.fori_loop(0, z_ref.shape[0] // CHUNK, step, 0)


def first_kernel(terms_ref, half_ref, sums_ref):
    sums_ref[...] = products(half_ref, terms_ref)


def second_kernel(terms_ref, half_ref, before_ref, sums_ref):
    size = before_ref.shape[0]
    sums_ref[:size, :] = before_ref[...]
    sums_ref[size:, :] = products(half_ref, terms_ref)


def image_terms(tri_ref, total_ref):
    image = jnp.dot(
        tri_ref[...], total_ref[...], precision=lax.Precision.HIGHEST, preferred_element_type=jnp.float32
    )
    return two_terms(image.T)


def changed(z_ref, image, own_ref, other_ref, i):
    used = jnp.concatenate([own_ref[:, lanes(i)], other_ref[:, lanes(i)]], axis=0)
    change = jnp.dot(image, used, preferred_element_type=jnp.float32)
    rows = z_ref.shape[0]
    return z_ref[:, lanes(i)] - (change[:rows] + change[rows:])


def step_kernel(
    z_ref, tri_ref, total_ref, own_ref, other_ref, next_own_ref, next_other_ref, new_ref, sums_ref, terms_ref
):
    image = image_terms(tri_ref, total_ref)

    def step(i, carry):
        current = changed(z_ref, image, own_ref, other_ref, i)
        new_ref[:, lanes(i)] = current
        terms_ref[:, lanes(i)] = two_terms(current)
        return carry

    lax.fori_loop(0, z_ref.shape[1] // CHUNK, step, 0)
    size = next_own_ref.shape[0]
    sums_ref[:size, :] = products(next_own_ref, terms_ref)
    sums_ref[size:, :] = products(next_other_ref, terms_ref)


def last_kernel(z_ref, tri_ref, total_ref, own_ref, other_ref, result_ref):
    image = image_terms(tri_ref, total_ref)

    def step(i, carry):
        result_ref[lanes(i), :] = changed(z_ref, image, own_ref, other_ref, i).T
        return carry

    lax.fori_loop(0, z_ref.shape[1] // CHUNK, step, 0)


def share_kernel(parts_ref, copies_ref):
    devices = parts_ref.shape[0]
    total = parts_ref[0]
    for device in range(1, devices):
        total = total + parts_ref[device]
    for device in range(devices):
        copies_ref[device] = total


def reordered(tri_factor, wanted):
    size = tri_factor.shape[0]
    source = lax.broadcasted_iota(jnp.int32, (size, size), 1)
    choose = (wanted == source).astype(jnp.float32)
    turned = jnp.dot(choose, tri_factor, precision=lax.Precision.HIGHEST)
    return lax.dot_general(turned, choose, ROWS_BY_LANES, precision=lax.Precision.HIGHEST)


def on_device(vectors, reflectors, tau_diag, coupling):
    count, each, rows = reflectors.shape
    high_axis, low_axis, core_axis = PCOL
    wide, deep = lax.axis_size(high_axis), lax.axis_size(low_axis)
    core, low = lax.axis_index(core_axis), lax.axis_index(low_axis)
    last = count - 1
    group = wide * each
    half = deep * group
    columns = vectors.shape[1]
    f32 = jnp.float32

    place = lax.broadcasted_iota(jnp.int32, (2 * half, 2 * half), 0)
    parity = jnp.where(place // half == 0, core, 1 - core)
    piece, spot, inner = place % half // group, place % group // each, place % each

    def factor(position):
        tri_factor = jnp.diag(tau_diag[position]) + jnp.triu(coupling[position], 1)
        offset = jnp.where(piece == 1, deep - 1, jnp.where(piece == 2, 1, jnp.where(piece == 3, 2, 0)))
        source = piece if position == last else (low + offset) % deep
        return reordered(tri_factor, ((spot * deep + source) * 2 + parity) * each + inner)

    factors = [factor(position) for position in range(count)]
    z_shape = jax.ShapeDtypeStruct((columns, rows), f32)
    terms_shape = jax.ShapeDtypeStruct((2 * columns, rows), jnp.bfloat16)
    current, terms = local_call(split_kernel, [z_shape, terms_shape], 1 << 24, vectors)

    def along_high(reflectors):
        arrived = copy_for_each(reflectors, high_axis, wide)
        return [arrived[:, k].reshape(group, rows) for k in range(reflectors.shape[0])]

    groups = {}
    groups[last - 1], groups[last] = along_high(reflectors[last - 1 :])
    start = after(groups[last], current, terms, *factors)
    first = copy_for_each(start, low_axis, deep).reshape(half, rows)
    groups[0], groups[1] = along_high(after(reflectors[: last - 1], first))
    partner = from_partner(first)

    pass_flops = 4 * columns * half * rows
    sums_shape = jax.ShapeDtypeStruct((2 * half, columns), f32)
    own_shape = jax.ShapeDtypeStruct((half, columns), f32)
    own_sums = local_call(first_kernel, own_shape, pass_flops, terms, first)
    sums = local_call(second_kernel, sums_shape, pass_flops, terms, partner, own_sums)
    sums = after(sums, groups[0], groups[1])

    def along_low(position, earlier):
        x = after(groups[position], earlier)
        pieces = [x]
        for by in (1, -1, 2):
            pieces.append(shifted(x, low_axis, by))
        return pieces

    devices = lax.axis_size("prow")
    parts_shape = jax.ShapeDtypeStruct((devices, 2 * half // devices, columns), f32)
    sent = {last - 1: along_low(last - 1, first)}
    used = (first, partner)
    for k in range(last, -1, -1):
        if k > 1:
            sent[k - 2] = along_low(k - 2, sums)
        if k > 0:
            own = jnp.concatenate(lax.optimization_barrier((*sent[k - 1], sums))[:-1])
        arrived = exchange(sums.reshape(parts_shape.shape), "prow")
        copies = local_call(share_kernel, parts_shape, 1 << 20, arrived)
        if k > 0:
            following = (own, from_partner(after(own, copies)))
        total = exchange(copies, "prow").reshape(2 * half, columns)
        if k > 0:
            current, sums = local_call(
                step_kernel,
                [z_shape, sums_shape],
                4 * pass_flops,
                current,
                factors[k],
                total,
                *used,
                *following,
                scratch=[pltpu.VMEM(terms_shape.shape, jnp.bfloat16)],
            )
            used = following
    result = jax.ShapeDtypeStruct(vectors.shape, f32)
    return local_call(last_kernel, result, 2 * pass_flops, current, factors[0], total, *used)


def solution(mesh):
    finer = Mesh(
        mesh.devices.reshape(mesh.shape["prow"], 8, 4, 2), ("prow", "pcol_0", "pcol_1", "pcol_2")
    )
    placed = (P("prow", PCOL), P(None, PCOL, "prow"), P(), P())

    return jax.shard_map(
        on_device, mesh=finer, in_specs=placed, out_specs=P("prow", PCOL), check_vma=False
    )
```

time: 233 us -> 230 us (0.987)
  the two profiles are of different devices: /device:TPU:4 before, /device:TPU:8 now
where the time goes in v3:
time: 230 us; the launch traced here: 228 us
  starting transfers between devices  84.7 us (37%)
  blocking collectives  52.7 us (23%)
  local copies, waits for them, and re-layouts  36.3 us (16%)
  Pallas kernels  25.8 us (11%)
  waiting for transfers between devices  17.7 us (8%)
  matrix products  10.6 us (5%)
    all_to_all x4, blocking collectives, exchange(): return lax.all_to_all(parts, axis, split_axis=0, concat_axis=0, tiled=True)  52.7 us
    all_to_all x7, starting transfers between devices, exchange(): return lax.all_to_all(parts, axis, split_axis=0, concat_axis=0, tiled=True)  47.6 us
    ppermute x9, starting transfers between devices, shifted(): lax.ppermute(x, axis, [(i, (i + by) % devices) for i in range(devices)])  29.4 us
    pallas_call x11, Pallas kernels, local_call(): pl.pallas_call(kernel, out_shape=shapes, in_specs=[whole] * len(operands)...  25.8 us
    unnamed x37, local copies, waits for them, and re-layouts  22.2 us
    all_to_all x7, waiting for transfers between devices, exchange(): return lax.all_to_all(parts, axis, split_axis=0, concat_axis=0, tiled=True)  17.6 us
    ppermute x4, starting transfers between devices, from_partner(): return lax.ppermute(x, 'pcol_2', [(0, 1), (1, 0)])  7.65 us
    dot_general x4, matrix products, reordered(): lax.dot_general(turned, choose, ROWS_BY_LANES, precision=lax.Precision.HI...  6.6 us
  transfers between devices with their start and end apart: 20, of which 5 were waited for; matrix products, arithmetic and copies ran while one was open for 13% of the time, Pallas kernels for 7%

profile of v3, /device:TPU:8, one launch (start us, length us, event | category | flops | bytes accessed | tf_op | source)
XLA Modules:
  0.0 228.2 jit_solution(13336836490438751504)
XLA Ops:
  1.9 9.2 %all-to-all-start = ((bf16[8,2,4,4096]{3,2,1,0:T(4,128)(2,1)}), bf16[8,2,4,4096]{3,2,1,0:T(4,128)(2,1)S(1)}, u32[]{:S(2)}, u32[]{:S(2)}) async-start(bf16[8,2,4,4096]{3,2,1,0:T(4,128)(2,1)} %broadcast_in_dim.89), calls=%async_computation | async-start | bytes 1048576 | tf_op jit(solution)/shard_map/all_to_all | solution.py:16
  11.2 1.6 copy-done.6
  13.9 1.3 copy-done
  15.2 1.8 fusion.26
  19.3 2.0 fusion.54.tri_ref
  21.3 1.9 fusion.60.tri_ref
  24.0 2.0 fusion.57.tri_ref
  27.0 17.0 %all_to_all.55 = bf16[4,32,4096]{2,1,0:T(8,128)(2,1)S(1)} all-to-all(bf16[4,32,4096]{2,1,0:T(8,128)(2,1)S(1)} %broadcast_in_dim.96), channel_id=1, replica_groups=mesh['prow'=8,'pcol_0'=8,'pcol_1'=4,'pcol_2'=2] {'pcol_1'}, dimensions={0} | all-to-all | bytes 2097152 | tf_op jit(solution)/shard_map/all_to_all | solution.py:16
  45.0 7.5 %all-to-all-start.2 = ((bf16[8,2,4,4096]{3,2,1,0:T(4,128)(2,1)}), bf16[8,2,4,4096]{3,2,1,0:T(4,128)(2,1)}, u32[]{:S(2)}, u32[]{:S(2)}) async-start(bf16[8,2,4,4096]{3,2,1,0:T(4,128)(2,1)} %broadcast_in_dim.97), calls=%async_computation.2 | async-start | bytes 1048576 | tf_op jit(solution)/shard_map/all_to_all | solution.py:16
  52.5 1.9 collective-permute-start
  54.4 1.7 reshape_squeeze.15
  56.1 2.5 %collective-permute-start.1 = (bf16[32,4096]{1,0:T(8,128)(2,1)}, bf16[32,4096]{1,0:T(8,128)(2,1)}, u32[]{:S(2)}, u32[]{:S(2)}) collective-permute-start(bf16[32,4096]{1,0:T(8,128)(2,1)} %reshape_squeeze.15), channel_id=1, source_target_pairs={{0,2},{2,4},{4,6},{6,0},{1,3},{3,5},{5,7},{7,1},{8,10},{10,12},{12... | collective-permute-start | bytes 786440 | tf_op jit(solution)/shard_map/ppermute | solution.py:29
  58.6 4.6 %collective-permute-start.2 = (bf16[32,4096]{1,0:T(8,128)(2,1)}, bf16[32,4096]{1,0:T(8,128)(2,1)}, u32[]{:S(2)}, u32[]{:S(2)}) collective-permute-start(bf16[32,4096]{1,0:T(8,128)(2,1)} %reshape_squeeze.15), channel_id=1, source_target_pairs={{0,6},{2,0},{4,2},{6,4},{1,7},{3,1},{5,3},{7,5},{8,14},{10,8},{12,... | collective-permute-start | bytes 786440 | tf_op jit(solution)/shard_map/ppermute | solution.py:29
  63.2 1.9 collective-permute-start.3
  65.9 1.8 all-to-all-done.2
  67.7 2.0 fusion.67
  69.7 1.7 reshape_squeeze.13
  71.4 1.7 reshape_squeeze.14
  73.1 2.7 %shard_map.48 = f32[256,128]{1,0:T(8,128)} custom-call(bf16[256,4096]{1,0:T(8,128)(2,1)S(1)} %get-tuple-element.35.terms_ref, bf16[128,4096]{1,0:T(8,128)(2,1)} %collective-permute-done.half_ref.other_ref, f32[128,128]{1,0:T(8,128)S(1)} %shard_map.47.before_ref), custom_call_target="tpu_custom_call" | custom-call | flops 268435456 | bytes 3211264 | tf_op jit(solution)/shard_map/pallas_call | solution.py:50
  75.8 10.3 %all-to-all-start.3 = ((f32[8,32,128]{2,1,0:T(8,128)}), f32[8,32,128]{2,1,0:T(8,128)S(1)}, u32[]{:S(2)}, u32[]{:S(2)}) async-start(f32[8,32,128]{2,1,0:T(8,128)} %bitcast.9), calls=%async_computation.3 | async-start | bytes 262144 | tf_op jit(solution)/shard_map/all_to_all | solution.py:16
  90.1 5.2 %all-to-all-done.3.parts_ref = f32[8,32,128]{2,1,0:T(8,128)S(1)} async-done(((f32[8,32,128]{2,1,0:T(8,128)}), f32[8,32,128]{2,1,0:T(8,128)S(1)}, u32[]{:S(2)}, u32[]{:S(2)}) %all-to-all-start.3) | async-done | bytes 131104 | tf_op jit(solution)/shard_map/all_to_all | solution.py:16
  95.9 1.9 collective-permute-start.4
  97.8 3.4 %all-to-all-start.4 = ((f32[8,32,128]{2,1,0:T(8,128)}), f32[8,32,128]{2,1,0:T(8,128)S(1)}, u32[]{:S(2)}, u32[]{:S(2)}) async-start(f32[8,32,128]{2,1,0:T(8,128)} %shard_map.49), calls=%async_computation.4 | async-start | bytes 262144 | tf_op jit(solution)/shard_map/all_to_all | solution.py:16
  101.2 2.5 %collective-permute-start.5 = (bf16[32,4096]{1,0:T(8,128)(2,1)}, bf16[32,4096]{1,0:T(8,128)(2,1)}, u32[]{:S(2)}, u32[]{:S(2)}) collective-permute-start(bf16[32,4096]{1,0:T(8,128)(2,1)} %reshape_squeeze.14), channel_id=1, source_target_pairs={{0,2},{2,4},{4,6},{6,0},{1,3},{3,5},{5,7},{7,1},{8,10},{10,12},{12... | collective-permute-start | bytes 786440 | tf_op jit(solution)/shard_map/ppermute | solution.py:29
  103.7 4.6 %collective-permute-start.6 = (bf16[32,4096]{1,0:T(8,128)(2,1)}, bf16[32,4096]{1,0:T(8,128)(2,1)}, u32[]{:S(2)}, u32[]{:S(2)}) collective-permute-start(bf16[32,4096]{1,0:T(8,128)(2,1)} %reshape_squeeze.14), channel_id=1, source_target_pairs={{0,6},{2,0},{4,2},{6,4},{1,7},{3,1},{5,3},{7,5},{8,14},{10,8},{12,... | collective-permute-start | bytes 786440 | tf_op jit(solution)/shard_map/ppermute | solution.py:29
  108.3 2.5 %collective-permute-start.7 = (bf16[32,4096]{1,0:T(8,128)(2,1)}, bf16[32,4096]{1,0:T(8,128)(2,1)}, u32[]{:S(2)}, u32[]{:S(2)}) collective-permute-start(bf16[32,4096]{1,0:T(8,128)(2,1)} %reshape_squeeze.14), channel_id=1, source_target_pairs={{0,4},{2,6},{4,0},{6,2},{1,5},{3,7},{5,1},{7,3},{8,12},{10,14},{12... | collective-permute-start | bytes 786440 | tf_op jit(solution)/shard_map/ppermute | solution.py:29
  111.1 1.6 copy-done.1
  113.7 5.1 %shard_map.50 = (f32[128,4096]{1,0:T(8,128)S(1)}, f32[256,128]{1,0:T(8,128)S(1)}) custom-call(f32[128,4096]{1,0:T(8,128)S(1)} %copy-done.1, f32[256,256]{1,0:T(8,128)S(1)} %copy-done.9, f32[256,128]{1,0:T(8,128)S(1)} %bitcast.41, bf16[128,4096]{1,0:T(8,128)(2,1)S(1)} %bitcast.39, bf16[128,4096]{1,0:T(8,128)(2,1)} %collective-permute-done.half_ref.other_ref, ...), custom_call_target="tpu_custom_call" | custom-call | flops 1073741824 | bytes 6684672 | tf_op jit(solution)/shard_map/pallas_call | solution.py:50
  118.8 1.3 copy-done.2
  120.8 6.8 %all-to-all-start.5 = ((f32[8,32,128]{2,1,0:T(8,128)}), f32[8,32,128]{2,1,0:T(8,128)S(1)}, u32[]{:S(2)}, u32[]{:S(2)}) async-start(f32[8,32,128]{2,1,0:T(8,128)} %bitcast.44), calls=%async_computation.5 | async-start | bytes 262144 | tf_op jit(solution)/shard_map/all_to_all | solution.py:16
  131.5 5.2 %all-to-all-done.5.parts_ref = f32[8,32,128]{2,1,0:T(8,128)S(1)} async-done(((f32[8,32,128]{2,1,0:T(8,128)}), f32[8,32,128]{2,1,0:T(8,128)S(1)}, u32[]{:S(2)}, u32[]{:S(2)}) %all-to-all-start.5) | async-done | bytes 131104 | tf_op jit(solution)/shard_map/all_to_all | solution.py:16
  137.3 1.9 collective-permute-start.8
  139.2 3.4 %all-to-all-start.6 = ((f32[8,32,128]{2,1,0:T(8,128)}), f32[8,32,128]{2,1,0:T(8,128)S(1)}, u32[]{:S(2)}, u32[]{:S(2)}) async-start(f32[8,32,128]{2,1,0:T(8,128)} %shard_map.51), calls=%async_computation.6 | async-start | bytes 262144 | tf_op jit(solution)/shard_map/all_to_all | solution.py:16
  142.6 2.2 collective-permute-start.9
  144.8 4.8 %collective-permute-start.10 = (bf16[32,4096]{1,0:T(8,128)(2,1)}, bf16[32,4096]{1,0:T(8,128)(2,1)}, u32[]{:S(2)}, u32[]{:S(2)}) collective-permute-start(bf16[32,4096]{1,0:T(8,128)(2,1)} %reshape_squeeze.13), channel_id=1, source_target_pairs={{0,6},{2,0},{4,2},{6,4},{1,7},{3,1},{5,3},{7,5},{8,14},{10,8},{12,... | collective-permute-start | bytes 786440 | tf_op jit(solution)/shard_map/ppermute | solution.py:29
  149.7 3.8 %collective-permute-start.11 = (bf16[32,4096]{1,0:T(8,128)(2,1)}, bf16[32,4096]{1,0:T(8,128)(2,1)}, u32[]{:S(2)}, u32[]{:S(2)}) collective-permute-start(bf16[32,4096]{1,0:T(8,128)(2,1)} %reshape_squeeze.13), channel_id=1, source_target_pairs={{0,4},{2,6},{4,0},{6,2},{1,5},{3,7},{5,1},{7,3},{8,12},{10,14},{12... | collective-permute-start | bytes 786440 | tf_op jit(solution)/shard_map/ppermute | solution.py:29
  153.6 1.6 copy-done.3
  156.1 5.1 %shard_map.52 = (f32[128,4096]{1,0:T(8,128)S(1)}, f32[256,128]{1,0:T(8,128)S(1)}) custom-call(f32[128,4096]{1,0:T(8,128)S(1)} %copy-done.3, f32[256,256]{1,0:T(8,128)S(1)} %copy-done.8, f32[256,128]{1,0:T(8,128)S(1)} %bitcast.40, bf16[128,4096]{1,0:T(8,128)(2,1)S(1)} %constant_dynamic-update-slice_fusion.next_own_ref.own_ref, ...), custom_call_target="tpu_custom_call" | custom-call | flops 1073741824 | bytes 6684672 | tf_op jit(solution)/shard_map/pallas_call | solution.py:50
  161.2 1.3 copy-done.4
  163.2 7.1 %all-to-all-start.7 = ((f32[8,32,128]{2,1,0:T(8,128)}), f32[8,32,128]{2,1,0:T(8,128)S(1)}, u32[]{:S(2)}, u32[]{:S(2)}) async-start(f32[8,32,128]{2,1,0:T(8,128)} %bitcast.45), calls=%async_computation.7 | async-start | bytes 262144 | tf_op jit(solution)/shard_map/all_to_all | solution.py:16
  174.2 5.2 %all-to-all-done.7.parts_ref = f32[8,32,128]{2,1,0:T(8,128)S(1)} async-done(((f32[8,32,128]{2,1,0:T(8,128)}), f32[8,32,128]{2,1,0:T(8,128)S(1)}, u32[]{:S(2)}, u32[]{:S(2)}) %all-to-all-start.7) | async-done | bytes 131104 | tf_op jit(solution)/shard_map/all_to_all | solution.py:16
  179.4 1.9 collective-permute-start.12
  181.3 12.4 %all_to_all.56 = f32[8,32,128]{2,1,0:T(8,128)S(1)} all-to-all(f32[8,32,128]{2,1,0:T(8,128)S(1)} %shard_map.53), channel_id=1, replica_groups=mesh['prow'=8,'pcol_0'=8,'pcol_1'=4,'pcol_2'=2] {'prow'}, dimensions={0} | all-to-all | bytes 262144 | tf_op jit(solution)/shard_map/all_to_all | solution.py:16
  193.7 1.6 copy-done.5
  195.3 5.1 %shard_map.54 = (f32[128,4096]{1,0:T(8,128)S(1)}, f32[256,128]{1,0:T(8,128)S(1)}) custom-call(f32[128,4096]{1,0:T(8,128)S(1)} %copy-done.5, f32[256,256]{1,0:T(8,128)S(1)} %copy-done.7, f32[256,128]{1,0:T(8,128)S(1)} %bitcast.42, bf16[128,4096]{1,0:T(8,128)(2,1)S(1)} %constant_dynamic-update-slice_fusion.4.next_own_ref.own_ref, ...), custom_call_target="tpu_custom_call" | custom-call | flops 1073741824 | bytes 6684672 | tf_op jit(solution)/shard_map/pallas_call | solution.py:50
  200.4 11.9 %all_to_all.57.parts_ref = f32[8,32,128]{2,1,0:T(8,128)S(1)} all-to-all(f32[8,32,128]{2,1,0:T(8,128)S(1)} %bitcast.46), channel_id=1, replica_groups=mesh['prow'=8,'pcol_0'=8,'pcol_1'=4,'pcol_2'=2] {'prow'}, dimensions={0} | all-to-all | bytes 262144 | tf_op jit(solution)/shard_map/all_to_all | solution.py:16
  212.3 11.5 %all_to_all.58 = f32[8,32,128]{2,1,0:T(8,128)S(1)} all-to-all(f32[8,32,128]{2,1,0:T(8,128)S(1)} %shard_map.55), channel_id=1, replica_groups=mesh['prow'=8,'pcol_0'=8,'pcol_1'=4,'pcol_2'=2] {'prow'}, dimensions={0} | all-to-all | bytes 262144 | tf_op jit(solution)/shard_map/all_to_all | solution.py:16
  223.8 4.5 %shard_map.56 = f32[4096,128]{1,0:T(8,128)} custom-call(f32[128,4096]{1,0:T(8,128)S(1)} %get-tuple-element.61.z_ref, f32[256,256]{1,0:T(8,128)S(1)} %fusion.63.tri_ref, f32[256,128]{1,0:T(8,128)S(1)} %bitcast.43, bf16[128,4096]{1,0:T(8,128)(2,1)S(1)} %constant_dynamic-update-slice_fusion.8.next_own_ref.own_ref, ...), custom_call_target="tpu_custom_call" | custom-call | flops 536870912 | bytes 4587520 | tf_op jit(solution)/shard_map/pallas_call | solution.py:50
  (72 shorter events, 25.6 us)
Async XLA Ops:
  0.0 15.2 %copy-start.12 = (f32[4,256]{1,0:T(4,128)S(1)}, f32[4,256]{1,0:T(4,128)}, u32[]{:S(2)}) copy-start(f32[4,256]{1,0:T(4,128)} %param.6) | copy-start | bytes 12292
  1.9 24.0 %all-to-all-start = ((bf16[8,2,4,4096]{3,2,1,0:T(4,128)(2,1)}), bf16[8,2,4,4096]{3,2,1,0:T(4,128)(2,1)S(1)}, u32[]{:S(2)}, u32[]{:S(2)}) async-start(bf16[8,2,4,4096]{3,2,1,0:T(4,128)(2,1)} %broadcast_in_dim.89), calls=%async_computation | async-start | bytes 1048576 | tf_op jit(solution)/shard_map/all_to_all | solution.py:16
  11.2 1.6 copy-start.6
  13.9 1.3 copy-start
  15.2 1.8 copy-start.13
  45.0 22.7 %all-to-all-start.2 = ((bf16[8,2,4,4096]{3,2,1,0:T(4,128)(2,1)}), bf16[8,2,4,4096]{3,2,1,0:T(4,128)(2,1)}, u32[]{:S(2)}, u32[]{:S(2)}) async-start(bf16[8,2,4,4096]{3,2,1,0:T(4,128)(2,1)} %broadcast_in_dim.97), calls=%async_computation.2 | async-start | bytes 1048576 | tf_op jit(solution)/shard_map/all_to_all | solution.py:16
  52.5 20.7 %collective-permute-start = (bf16[128,4096]{1,0:T(8,128)(2,1)S(1)}, bf16[128,4096]{1,0:T(8,128)(2,1)}, u32[]{:S(2)}, u32[]{:S(2)}) collective-permute-start(bf16[128,4096]{1,0:T(8,128)(2,1)S(1)} %bitcast.37), channel_id=1, source_target_pairs={{0,1},{1,0},{2,3},{3,2},{4,5},{5,4},{6,7},{7,6},{8,9},{9,8},{10,11... | collective-permute-start | bytes 3145736 | tf_op jit(solution)/shard_map/ppermute | solution.py:24
  56.1 30.0 %collective-permute-start.1 = (bf16[32,4096]{1,0:T(8,128)(2,1)}, bf16[32,4096]{1,0:T(8,128)(2,1)}, u32[]{:S(2)}, u32[]{:S(2)}) collective-permute-start(bf16[32,4096]{1,0:T(8,128)(2,1)} %reshape_squeeze.15), channel_id=1, source_target_pairs={{0,2},{2,4},{4,6},{6,0},{1,3},{3,5},{5,7},{7,1},{8,10},{10,12},{12... | collective-permute-start | bytes 786440 | tf_op jit(solution)/shard_map/ppermute | solution.py:29
  58.6 27.6 %collective-permute-start.2 = (bf16[32,4096]{1,0:T(8,128)(2,1)}, bf16[32,4096]{1,0:T(8,128)(2,1)}, u32[]{:S(2)}, u32[]{:S(2)}) collective-permute-start(bf16[32,4096]{1,0:T(8,128)(2,1)} %reshape_squeeze.15), channel_id=1, source_target_pairs={{0,6},{2,0},{4,2},{6,4},{1,7},{3,1},{5,3},{7,5},{8,14},{10,8},{12,... | collective-permute-start | bytes 786440 | tf_op jit(solution)/shard_map/ppermute | solution.py:29
  63.2 23.0 %collective-permute-start.3 = (bf16[32,4096]{1,0:T(8,128)(2,1)}, bf16[32,4096]{1,0:T(8,128)(2,1)}, u32[]{:S(2)}, u32[]{:S(2)}) collective-permute-start(bf16[32,4096]{1,0:T(8,128)(2,1)} %reshape_squeeze.15), channel_id=1, source_target_pairs={{0,4},{2,6},{4,0},{6,2},{1,5},{3,7},{5,1},{7,3},{8,12},{10,14},{12... | collective-permute-start | bytes 786440 | tf_op jit(solution)/shard_map/ppermute | solution.py:29
  75.8 19.4 %all-to-all-start.3 = ((f32[8,32,128]{2,1,0:T(8,128)}), f32[8,32,128]{2,1,0:T(8,128)S(1)}, u32[]{:S(2)}, u32[]{:S(2)}) async-start(f32[8,32,128]{2,1,0:T(8,128)} %bitcast.9), calls=%async_computation.3 | async-start | bytes 262144 | tf_op jit(solution)/shard_map/all_to_all | solution.py:16
  95.9 15.2 %collective-permute-start.4 = (bf16[128,4096]{1,0:T(8,128)(2,1)S(1)}, bf16[128,4096]{1,0:T(8,128)(2,1)S(1)}, u32[]{:S(2)}, u32[]{:S(2)}) collective-permute-start(bf16[128,4096]{1,0:T(8,128)(2,1)S(1)} %constant_dynamic-update-slice_fusion.next_own_ref.own_ref), channel_id=1, source_target_pairs={{0,1},{1,0},{2,3},{3,2},{4,5},{5,4},{6,7},{7,6},{8,9},{9,8},{10,11... | collective-permute-start | bytes 3145736 | tf_op jit(solution)/shard_map/ppermute | solution.py:24
  97.8 13.3 %all-to-all-start.4 = ((f32[8,32,128]{2,1,0:T(8,128)}), f32[8,32,128]{2,1,0:T(8,128)S(1)}, u32[]{:S(2)}, u32[]{:S(2)}) async-start(f32[8,32,128]{2,1,0:T(8,128)} %shard_map.49), calls=%async_computation.4 | async-start | bytes 262144 | tf_op jit(solution)/shard_map/all_to_all | solution.py:16
  101.2 26.3 %collective-permute-start.5 = (bf16[32,4096]{1,0:T(8,128)(2,1)}, bf16[32,4096]{1,0:T(8,128)(2,1)}, u32[]{:S(2)}, u32[]{:S(2)}) collective-permute-start(bf16[32,4096]{1,0:T(8,128)(2,1)} %reshape_squeeze.14), channel_id=1, source_target_pairs={{0,2},{2,4},{4,6},{6,0},{1,3},{3,5},{5,7},{7,1},{8,10},{10,12},{12... | collective-permute-start | bytes 786440 | tf_op jit(solution)/shard_map/ppermute | solution.py:29
  103.7 23.9 %collective-permute-start.6 = (bf16[32,4096]{1,0:T(8,128)(2,1)}, bf16[32,4096]{1,0:T(8,128)(2,1)}, u32[]{:S(2)}, u32[]{:S(2)}) collective-permute-start(bf16[32,4096]{1,0:T(8,128)(2,1)} %reshape_squeeze.14), channel_id=1, source_target_pairs={{0,6},{2,0},{4,2},{6,4},{1,7},{3,1},{5,3},{7,5},{8,14},{10,8},{12,... | collective-permute-start | bytes 786440 | tf_op jit(solution)/shard_map/ppermute | solution.py:29
  108.3 19.3 %collective-permute-start.7 = (bf16[32,4096]{1,0:T(8,128)(2,1)}, bf16[32,4096]{1,0:T(8,128)(2,1)}, u32[]{:S(2)}, u32[]{:S(2)}) collective-permute-start(bf16[32,4096]{1,0:T(8,128)(2,1)} %reshape_squeeze.14), channel_id=1, source_target_pairs={{0,4},{2,6},{4,0},{6,2},{1,5},{3,7},{5,1},{7,3},{8,12},{10,14},{12... | collective-permute-start | bytes 786440 | tf_op jit(solution)/shard_map/ppermute | solution.py:29
  111.1 1.6 copy-start.1
  112.7 0.9 copy-start.9
  118.8 1.3 copy-start.2
  120.1 0.6 copy-start.10
  120.8 15.8 %all-to-all-start.5 = ((f32[8,32,128]{2,1,0:T(8,128)}), f32[8,32,128]{2,1,0:T(8,128)S(1)}, u32[]{:S(2)}, u32[]{:S(2)}) async-start(f32[8,32,128]{2,1,0:T(8,128)} %bitcast.44), calls=%async_computation.5 | async-start | bytes 262144 | tf_op jit(solution)/shard_map/all_to_all | solution.py:16
  137.3 16.2 %collective-permute-start.8 = (bf16[128,4096]{1,0:T(8,128)(2,1)S(1)}, bf16[128,4096]{1,0:T(8,128)(2,1)}, u32[]{:S(2)}, u32[]{:S(2)}) collective-permute-start(bf16[128,4096]{1,0:T(8,128)(2,1)S(1)} %constant_dynamic-update-slice_fusion.4.next_own_ref.own_ref), channel_id=1, source_target_pairs={{0,1},{1,0},{2,3},{3,2},{4,5},{5,4},{6,7},{7,6},{8,9},{9,8},{10,11... | collective-permute-start | bytes 3145736 | tf_op jit(solution)/shard_map/ppermute | solution.py:24
  139.2 14.3 %all-to-all-start.6 = ((f32[8,32,128]{2,1,0:T(8,128)}), f32[8,32,128]{2,1,0:T(8,128)S(1)}, u32[]{:S(2)}, u32[]{:S(2)}) async-start(f32[8,32,128]{2,1,0:T(8,128)} %shard_map.51), calls=%async_computation.6 | async-start | bytes 262144 | tf_op jit(solution)/shard_map/all_to_all | solution.py:16
  142.6 27.7 %collective-permute-start.9 = (bf16[32,4096]{1,0:T(8,128)(2,1)}, bf16[32,4096]{1,0:T(8,128)(2,1)}, u32[]{:S(2)}, u32[]{:S(2)}) collective-permute-start(bf16[32,4096]{1,0:T(8,128)(2,1)} %reshape_squeeze.13), channel_id=1, source_target_pairs={{0,2},{2,4},{4,6},{6,0},{1,3},{3,5},{5,7},{7,1},{8,10},{10,12},{12... | collective-permute-start | bytes 786440 | tf_op jit(solution)/shard_map/ppermute | solution.py:29
  144.8 25.5 %collective-permute-start.10 = (bf16[32,4096]{1,0:T(8,128)(2,1)}, bf16[32,4096]{1,0:T(8,128)(2,1)}, u32[]{:S(2)}, u32[]{:S(2)}) collective-permute-start(bf16[32,4096]{1,0:T(8,128)(2,1)} %reshape_squeeze.13), channel_id=1, source_target_pairs={{0,6},{2,0},{4,2},{6,4},{1,7},{3,1},{5,3},{7,5},{8,14},{10,8},{12,... | collective-permute-start | bytes 786440 | tf_op jit(solution)/shard_map/ppermute | solution.py:29
  149.7 20.6 %collective-permute-start.11 = (bf16[32,4096]{1,0:T(8,128)(2,1)}, bf16[32,4096]{1,0:T(8,128)(2,1)}, u32[]{:S(2)}, u32[]{:S(2)}) collective-permute-start(bf16[32,4096]{1,0:T(8,128)(2,1)} %reshape_squeeze.13), channel_id=1, source_target_pairs={{0,4},{2,6},{4,0},{6,2},{1,5},{3,7},{5,1},{7,3},{8,12},{10,14},{12... | collective-permute-start | bytes 786440 | tf_op jit(solution)/shard_map/ppermute | solution.py:29
  153.5 1.6 copy-start.3
  155.1 0.9 copy-start.8
  161.2 1.3 copy-start.4
  162.5 0.6 copy-start.11
  162.5 31.2 %copy-start.7 = (f32[256,256]{1,0:T(8,128)S(1)}, f32[256,256]{1,0:T(8,128)}, u32[]{:S(2)}) copy-start(f32[256,256]{1,0:T(8,128)} %fusion.60.tri_ref) | copy-start | bytes 786436
  163.2 16.2 %all-to-all-start.7 = ((f32[8,32,128]{2,1,0:T(8,128)}), f32[8,32,128]{2,1,0:T(8,128)S(1)}, u32[]{:S(2)}, u32[]{:S(2)}) async-start(f32[8,32,128]{2,1,0:T(8,128)} %bitcast.45), calls=%async_computation.7 | async-start | bytes 262144 | tf_op jit(solution)/shard_map/all_to_all | solution.py:16
  179.4 14.3 %collective-permute-start.12 = (bf16[128,4096]{1,0:T(8,128)(2,1)S(1)}, bf16[128,4096]{1,0:T(8,128)(2,1)S(1)}, u32[]{:S(2)}, u32[]{:S(2)}) collective-permute-start(bf16[128,4096]{1,0:T(8,128)(2,1)S(1)} %constant_dynamic-update-slice_fusion.8.next_own_ref.own_ref), channel_id=1, source_target_pairs={{0,1},{1,0},{2,3},{3,2},{4,5},{5,4},{6,7},{7,6},{8,9},{9,8},{10,11... | collective-permute-start | bytes 3145736 | tf_op jit(solution)/shard_map/ppermute | solution.py:24
  193.7 1.6 copy-start.5

commit v4 on v2

--- a/solution.py
+++ b/solution.py
@@ -40,7 +40,7 @@
     return pl.ds(pl.multiple_of(step * CHUNK, CHUNK), CHUNK)
 
 
-def local_call(kernel, shapes, flops, *operands):
+def local_call(kernel, shapes, flops, *operands, scratch=()):
     whole = pl.BlockSpec(memory_space=pltpu.VMEM)
     moved = sum(x.size * x.dtype.itemsize for x in operands)
     single = not isinstance(shapes, (list, tuple))
@@ -49,27 +49,38 @@
         out_shape=shapes,
         in_specs=[whole] * len(operands),
         out_specs=whole if single else [whole] * len(shapes),
+        scratch_shapes=scratch,
         cost_estimate=pl.CostEstimate(flops=flops, bytes_accessed=moved, transcendentals=0),
         compiler_params=pltpu.CompilerParams(vmem_limit_bytes=24 << 20),
     )(*operands)
 
 
-def product_kernel(z_ref, half_ref, sums_ref):
-    def step(i, total):
-        terms = two_terms(z_ref[:, lanes(i)])
-        return total + lax.dot_general(
-            terms, half_ref[:, lanes(i)], ROWS_BY_LANES, preferred_element_type=jnp.float32
-        )
-
-    rows, depth = z_ref.shape
-    start = jnp.zeros((2 * rows, half_ref.shape[0]), jnp.float32)
-    sums_ref[...] = folded(lax.fori_loop(0, depth // CHUNK, step, start))
-
-
-def second_product_kernel(z_ref, half_ref, before_ref, sums_ref):
-    width = half_ref.shape[0]
-    sums_ref[:, :width] = before_ref[...]
-    product_kernel(z_ref, half_ref, sums_ref.at[:, width:])
+def products(half_ref, terms_ref):
+    both = lax.dot_general(
+        half_ref[...], terms_ref[...], ROWS_BY_LANES, preferred_element_type=jnp.float32
+    )
+    columns = both.shape[1] // 2
+    return (both[:, :columns] + both[:, columns:]).T
+
+
+def split_kernel(z_ref, turned_ref, terms_ref):
+    def step(i, carry):
+        turned = z_ref[lanes(i), :].T
+        turned_ref[:, lanes(i)] = turned
+        terms_ref[:, lanes(i)] = two_terms(turned)
+        return carry
+
+    lax.fori_loop(0, z_ref.shape[0] // CHUNK, step, 0)
+
+
+def first_kernel(terms_ref, half_ref, sums_ref):
+    sums_ref[...] = products(half_ref, terms_ref)
+
+
+def second_kernel(terms_ref, half_ref, before_ref, sums_ref):
+    size = before_ref.shape[1]
+    sums_ref[:, :size] = before_ref[...]
+    sums_ref[:, size:] = products(half_ref, terms_ref)
 
 
 def joined(refs, i):
@@ -77,20 +88,18 @@
 
 
 def step_kernel(z_ref, image_ref, *refs):
-    *used_refs, next_ref, new_ref, sums_ref = refs
+    *used_refs, next_ref, new_ref, sums_ref, terms_ref = refs
     image = two_terms(image_ref[...])
 
-    def step(i, total):
+    def step(i, carry):
         change = jnp.dot(image, joined(used_refs, i), preferred_element_type=jnp.float32)
         current = z_ref[:, lanes(i)] - folded(change)
         new_ref[:, lanes(i)] = current
-        return total + lax.dot_general(
-            two_terms(current), next_ref[:, lanes(i)], ROWS_BY_LANES, preferred_element_type=jnp.float32
-        )
-
-    rows, depth = z_ref.shape
-    start = jnp.zeros((2 * rows, next_ref.shape[0]), jnp.float32)
-    sums_ref[...] = folded(lax.fori_loop(0, depth // CHUNK, step, start))
+        terms_ref[:, lanes(i)] = two_terms(current)
+        return carry
+
+    lax.fori_loop(0, z_ref.shape[1] // CHUNK, step, 0)
+    sums_ref[...] = products(next_ref, terms_ref)
 
 
 def last_kernel(z_ref, image_ref, used_ref, result_ref):
@@ -154,14 +163,12 @@
     early = early.transpose(1, 0, 2, 3).reshape(last, deep * each, rows)
     later = lax.all_gather(early, (high_axis, core_axis), axis=0, tiled=False)
 
-    start = after(reflectors[last], early)
-    first = copy_for_each(start, (high_axis, low_axis), wide * deep).reshape(half, rows)
-    partner = from_partner(first)
+    group = copy_for_each(after(reflectors[last], early), high_axis, wide).reshape(wide * each, rows)
 
     place = lax.broadcasted_iota(jnp.int32, (2 * half, 2 * half), 0)
     parity = jnp.where(place // half == 0, core, 1 - core)
-    rest = place % half
-    alone = (rest // each * 2 + parity) * each + rest % each
+    across, along = place % half // (wide * each), place % (wide * each) // each
+    alone = ((along * deep + across) * 2 + parity) * each + place % each
     spot, inner = place // each, place % each
     high, mid, low = spot // (2 * deep), spot // deep % 2, spot % deep
     together = ((high * deep + low) * 2 + mid) * each + inner
@@ -171,13 +178,17 @@
         return reordered(tri_factor, alone if position == last else together)
 
     factors = [factor(position) for position in range(count)]
-    current = after(vectors.T, *factors)
     pass_flops = 4 * columns * half * rows
     sums_shape = jax.ShapeDtypeStruct((columns, 2 * half), jnp.float32)
     own_shape = jax.ShapeDtypeStruct((columns, half), jnp.float32)
-    z_shape = jax.ShapeDtypeStruct(current.shape, jnp.float32)
-    sums = local_call(product_kernel, own_shape, pass_flops, current, first)
-    sums = local_call(second_product_kernel, sums_shape, pass_flops, current, partner, sums)
+    z_shape = jax.ShapeDtypeStruct((columns, rows), jnp.float32)
+    terms_shape = jax.ShapeDtypeStruct((2 * columns, rows), jnp.bfloat16)
+    current, terms = local_call(split_kernel, [z_shape, terms_shape], 1 << 24, vectors)
+    start = after(group, current, terms, *factors)
+    first = copy_for_each(start, low_axis, deep).reshape(half, rows)
+    partner = from_partner(first)
+    sums = local_call(first_kernel, own_shape, pass_flops, terms, first)
+    sums = local_call(second_kernel, sums_shape, pass_flops, terms, partner, sums)
 
     panels = None
     used = [first, partner]
@@ -190,7 +201,14 @@
         if k > 0:
             following = panels[k - 1]
             current, sums = local_call(
-                step_kernel, [z_shape, sums_shape], 4 * pass_flops, current, image, *used, following
+                step_kernel,
+                [z_shape, sums_shape],
+                4 * pass_flops,
+                current,
+                image,
+                *used,
+                following,
+                scratch=[pltpu.VMEM(terms_shape.shape, jnp.bfloat16)],
             )
             used = [following]
     result = jax.ShapeDtypeStruct(vectors.shape, jnp.float32)

time: 216 us -> 193 us (0.89)
  the two profiles are of different devices: /device:TPU:2 before, /device:TPU:8 now
where the time goes in v4:
time: 193 us; the launch traced here: 192 us
  blocking collectives  118 us (61%)
  Pallas kernels  17.3 us (9%)
  local copies, waits for them, and re-layouts  15.6 us (8%)
  between operations  13.6 us (7%)
  starting transfers between devices  12.8 us (7%)
  matrix products  9.07 us (5%)
  waiting for transfers between devices  5.39 us (3%)
    all_to_all x9, blocking collectives, exchange(): return lax.all_to_all(parts, axis, split_axis=0, concat_axis=0, tiled=True)  118 us
    pallas_call x11, Pallas kernels, local_call(): pl.pallas_call(kernel, out_shape=shapes, in_specs=[whole] * len(operands)...  17.3 us
    all_to_all x2, starting transfers between devices, exchange(): return lax.all_to_all(parts, axis, split_axis=0, concat_axis=0, tiled=True)  10.9 us
    unnamed x24, local copies, waits for them, and re-layouts  6.14 us
    slice x1, local copies, waits for them, and re-layouts, on_device(): panels = [gathered[:, p].reshape(2 * half, rows) for p in range(last)]  5.59 us
    dot_general x4, matrix products, reordered(): lax.dot_general(turned, choose, ROWS_BY_LANES, precision=lax.Precision.HI...  5.29 us
  transfers between devices with their start and end apart: 4, of which 2 were waited for; matrix products, arithmetic and copies ran while one was open for 9% of the time, Pallas kernels for 2%

profile of v4, /device:TPU:8, one launch (start us, length us, event | category | flops | bytes accessed | tf_op | source)
XLA Modules:
  0.0 191.7 jit_solution(2600534348785481239)
XLA Ops:
  6.5 0.9 slice.48
  7.5 0.1 broadcast_in_dim.82
  7.6 12.2 %all_to_all.55 = bf16[4,3,4,4096]{3,2,1,0:T(4,128)(2,1)S(1)} all-to-all(bf16[4,3,4,4096]{3,2,1,0:T(4,128)(2,1)S(1)} %broadcast_in_dim.82), channel_id=1, replica_groups=mesh['prow'=8,'pcol_0'=8,'pcol_1'=4,'pcol_2'=2] {'pcol_1'}, dimensions={0} | all-to-all | bytes 786432 | tf_op jit(solution)/shard_map/all_to_all | solution.py:17
  19.8 0.2 copy.6
  20.0 0.9 all_gather_reshape.3
  20.9 0.8 slice_bitcast_fusion
  21.6 0.8 broadcast_in_dim.69
  22.4 7.5 %all-to-all-start = ((bf16[8,4,4096]{2,1,0:T(4,128)(2,1)}), bf16[8,4,4096]{2,1,0:T(4,128)(2,1)S(1)}, u32[]{:S(2)}, u32[]{:S(2)}) async-start(bf16[8,4,4096]{2,1,0:T(4,128)(2,1)} %broadcast_in_dim.69), calls=%async_computation | async-start | bytes 524288 | tf_op jit(solution)/shard_map/all_to_all | solution.py:17
  30.0 1.6 copy-done.6
  31.6 1.1 shard_map.46
  32.8 1.8 fusion.34
  34.6 1.4 fusion.76.tri_ref
  36.0 0.6 fusion.37
  36.6 0.7 fusion.79.tri_ref
  37.3 0.6 fusion.31
  37.9 0.7 fusion.28
  38.7 1.4 fusion.73.tri_ref
  40.0 1.9 fusion.70.tri_ref
  41.9 0.1 reshape.39
  42.0 0.1 broadcast_in_dim.81
  42.1 16.1 %all_to_all.56 = bf16[4,32,4096]{2,1,0:T(8,128)(2,1)S(1)} all-to-all(bf16[4,32,4096]{2,1,0:T(8,128)(2,1)S(1)} %broadcast_in_dim.81), channel_id=1, replica_groups=mesh['prow'=8,'pcol_0'=8,'pcol_1'=4,'pcol_2'=2] {'pcol_1'}, dimensions={0} | all-to-all | bytes 2097152 | tf_op jit(solution)/shard_map/all_to_all | solution.py:17
  58.2 1.9 collective-permute-start
  60.1 0.9 shard_map.47.before_ref
  61.0 2.0 %collective-permute-done.half_ref.refs_1_ = bf16[128,4096]{1,0:T(8,128)(2,1)S(1)} collective-permute-done((bf16[128,4096]{1,0:T(8,128)(2,1)S(1)}, bf16[128,4096]{1,0:T(8,128)(2,1)S(1)}, u32[]{:S(2)}, u32[]{:S(2)}) %collective-permute-start) | collective-permute-done | bytes 1048608 | tf_op jit(solution)/shard_map/ppermute | solution.py:25
  63.0 0.9 shard_map.48
  63.9 0.1 copy-done.2
  64.0 19.6 %all_to_all.57.parts_ref = f32[8,16,256]{2,1,0:T(8,128)S(1)} all-to-all(f32[8,16,256]{2,1,0:T(8,128)S(1)} %bitcast.56), channel_id=1, replica_groups=mesh['prow'=8,'pcol_0'=8,'pcol_1'=4,'pcol_2'=2] {'prow'}, dimensions={0} | all-to-all | bytes 262144 | tf_op jit(solution)/shard_map/all_to_all | solution.py:17
  83.6 1.0 shard_map.49
  84.6 3.4 %all-to-all-start.3 = ((f32[8,16,256]{2,1,0:T(8,128)}), f32[8,16,256]{2,1,0:T(8,128)S(1)}, u32[]{:S(2)}, u32[]{:S(2)}) async-start(f32[8,16,256]{2,1,0:T(8,128)} %shard_map.49), calls=%async_computation.3 | async-start | bytes 262144 | tf_op jit(solution)/shard_map/all_to_all | solution.py:17
  88.0 0.0 all-gather.2.cloned.1.call-done
  88.0 5.6 %fusion.82 = (bf16[16,1,16,4096]{3,2,1,0:T(8,128)(2,1)S(1)}, bf16[16,1,16,4096]{3,2,1,0:T(8,128)(2,1)}, bf16[16,1,16,4096]{3,2,1,0:T(8,128)(2,1)}) fusion(bf16[16,3,16,4096]{3,2,1,0:T(8,128)(2,1)} %all-gather.2.cloned.1.call-done), kind=kLoop, calls=%fused_computation.119 | loop fusion | bytes 12582912 | tf_op jit(solution)/shard_map/slice | solution.py:199
  93.6 3.4 %all-to-all-done.3 = f32[8,16,256]{2,1,0:T(8,128)S(1)} async-done(((f32[8,16,256]{2,1,0:T(8,128)}), f32[8,16,256]{2,1,0:T(8,128)S(1)}, u32[]{:S(2)}, u32[]{:S(2)}) %all-to-all-start.3) | async-done | bytes 131104 | tf_op jit(solution)/shard_map/all_to_all | solution.py:17
  97.0 1.6 copy-done.1
  98.5 1.2 copy-done.3
  99.8 1.6 copy-done.5
  101.4 2.8 %shard_map.50 = (f32[128,4096]{1,0:T(8,128)S(1)}, f32[128,256]{1,0:T(8,128)S(1)}) custom-call(f32[128,4096]{1,0:T(8,128)S(1)} %copy-done.5, f32[128,256]{1,0:T(8,128)S(1)} %bitcast.52, bf16[128,4096]{1,0:T(8,128)(2,1)S(1)} %bitcast.51, bf16[128,4096]{1,0:T(8,128)(2,1)S(1)} %copy-done.3, bf16[256,4096]{1,0:T(8,128)(2,1)S(1)} %bitcast.47), custom_call_target="tpu_custom_call" | custom-call | flops 1073741824 | bytes 6422528 | tf_op jit(solution)/shard_map/pallas_call | solution.py:47
  104.2 12.6 %all_to_all.58.parts_ref = f32[8,16,256]{2,1,0:T(8,128)S(1)} all-to-all(f32[8,16,256]{2,1,0:T(8,128)S(1)} %bitcast.57), channel_id=1, replica_groups=mesh['prow'=8,'pcol_0'=8,'pcol_1'=4,'pcol_2'=2] {'prow'}, dimensions={0} | all-to-all | bytes 262144 | tf_op jit(solution)/shard_map/all_to_all | solution.py:17
  116.8 0.3 shard_map.51
  117.1 11.5 %all_to_all.59 = f32[8,16,256]{2,1,0:T(8,128)S(1)} all-to-all(f32[8,16,256]{2,1,0:T(8,128)S(1)} %shard_map.51), channel_id=1, replica_groups=mesh['prow'=8,'pcol_0'=8,'pcol_1'=4,'pcol_2'=2] {'prow'}, dimensions={0} | all-to-all | bytes 262144 | tf_op jit(solution)/shard_map/all_to_all | solution.py:17
  128.6 2.8 %shard_map.52 = (f32[128,4096]{1,0:T(8,128)S(1)}, f32[128,256]{1,0:T(8,128)S(1)}) custom-call(f32[128,4096]{1,0:T(8,128)S(1)} %get-tuple-element.19.z_ref, f32[128,256]{1,0:T(8,128)S(1)} %bitcast.54, bf16[256,4096]{1,0:T(8,128)(2,1)S(1)} %bitcast.48, bf16[256,4096]{1,0:T(8,128)(2,1)S(1)} %bitcast.45), custom_call_target="tpu_custom_call" | custom-call | flops 1073741824 | bytes 6422528 | tf_op jit(solution)/shard_map/pallas_call | solution.py:47
  131.4 11.5 %all_to_all.60.parts_ref = f32[8,16,256]{2,1,0:T(8,128)S(1)} all-to-all(f32[8,16,256]{2,1,0:T(8,128)S(1)} %bitcast.58), channel_id=1, replica_groups=mesh['prow'=8,'pcol_0'=8,'pcol_1'=4,'pcol_2'=2] {'prow'}, dimensions={0} | all-to-all | bytes 262144 | tf_op jit(solution)/shard_map/all_to_all | solution.py:17
  142.8 0.3 shard_map.53
  143.2 11.5 %all_to_all.61 = f32[8,16,256]{2,1,0:T(8,128)S(1)} all-to-all(f32[8,16,256]{2,1,0:T(8,128)S(1)} %shard_map.53), channel_id=1, replica_groups=mesh['prow'=8,'pcol_0'=8,'pcol_1'=4,'pcol_2'=2] {'prow'}, dimensions={0} | all-to-all | bytes 262144 | tf_op jit(solution)/shard_map/all_to_all | solution.py:17
  154.6 2.8 %shard_map.54 = (f32[128,4096]{1,0:T(8,128)S(1)}, f32[128,256]{1,0:T(8,128)S(1)}) custom-call(f32[128,4096]{1,0:T(8,128)S(1)} %get-tuple-element.21.z_ref, f32[128,256]{1,0:T(8,128)S(1)} %bitcast.53, bf16[256,4096]{1,0:T(8,128)(2,1)S(1)} %bitcast.46, bf16[256,4096]{1,0:T(8,128)(2,1)S(1)} %bitcast.43), custom_call_target="tpu_custom_call" | custom-call | flops 1073741824 | bytes 6422528 | tf_op jit(solution)/shard_map/pallas_call | solution.py:47
  157.4 11.6 %all_to_all.62.parts_ref = f32[8,16,256]{2,1,0:T(8,128)S(1)} all-to-all(f32[8,16,256]{2,1,0:T(8,128)S(1)} %bitcast.59), channel_id=1, replica_groups=mesh['prow'=8,'pcol_0'=8,'pcol_1'=4,'pcol_2'=2] {'prow'}, dimensions={0} | all-to-all | bytes 262144 | tf_op jit(solution)/shard_map/all_to_all | solution.py:17
  169.0 0.3 shard_map.55
  169.3 11.5 %all_to_all.63 = f32[8,16,256]{2,1,0:T(8,128)S(1)} all-to-all(f32[8,16,256]{2,1,0:T(8,128)S(1)} %shard_map.55), channel_id=1, replica_groups=mesh['prow'=8,'pcol_0'=8,'pcol_1'=4,'pcol_2'=2] {'prow'}, dimensions={0} | all-to-all | bytes 262144 | tf_op jit(solution)/shard_map/all_to_all | solution.py:17
  180.8 4.0 %shard_map.56 = f32[4096,128]{1,0:T(8,128)} custom-call(f32[128,4096]{1,0:T(8,128)S(1)} %get-tuple-element.23.z_ref, f32[128,256]{1,0:T(8,128)S(1)} %bitcast.55, bf16[256,4096]{1,0:T(8,128)(2,1)S(1)} %bitcast.44), custom_call_target="tpu_custom_call" | custom-call | flops 536870912 | bytes 4325376 | tf_op jit(solution)/shard_map/pallas_call | solution.py:47
  (31 shorter events, 0.1 us)
Async XLA Ops:
  6.5 81.4 %all-gather.2.cloned.1.call-start = ((), (), s32[]{:S(2)}) async-start(), calls=%async_computation.11 | async-start | bytes 6684672 | tf_op jit(solution)/shard_map/all_gather | solution.py:164
  20.0 12.8 %copy-start.10 = (f32[4,256]{1,0:T(4,128)S(1)}, f32[4,256]{1,0:T(4,128)}, u32[]{:S(2)}) copy-start(f32[4,256]{1,0:T(4,128)} %param.6) | copy-start | bytes 12292
  22.4 19.5 %all-to-all-start = ((bf16[8,4,4096]{2,1,0:T(4,128)(2,1)}), bf16[8,4,4096]{2,1,0:T(4,128)(2,1)S(1)}, u32[]{:S(2)}, u32[]{:S(2)}) async-start(bf16[8,4,4096]{2,1,0:T(4,128)(2,1)} %broadcast_in_dim.69), calls=%async_computation | async-start | bytes 524288 | tf_op jit(solution)/shard_map/all_to_all | solution.py:17
  30.0 1.6 copy-start.6
  32.7 1.9 %copy-start.4 = (f32[128,4096]{1,0:T(8,128)}, f32[128,4096]{1,0:T(8,128)S(1)}, u32[]{:S(2)}) copy-start(f32[128,4096]{1,0:T(8,128)S(1)} %get-tuple-element.15.z_ref) | copy-start | bytes 6291460
  34.6 1.4 copy-start.11
  58.2 4.8 %collective-permute-start = (bf16[128,4096]{1,0:T(8,128)(2,1)S(1)}, bf16[128,4096]{1,0:T(8,128)(2,1)S(1)}, u32[]{:S(2)}, u32[]{:S(2)}) collective-permute-start(bf16[128,4096]{1,0:T(8,128)(2,1)S(1)} %bitcast.49), channel_id=1, source_target_pairs={{0,1},{1,0},{2,3},{3,2},{4,5},{5,4},{6,7},{7,6},{8,9},{9,8},{10,11... | collective-permute-start | bytes 3145736 | tf_op jit(solution)/shard_map/ppermute | solution.py:25
  61.0 22.6 %copy-start.9 = (f32[256,256]{1,0:T(8,128)S(1)}, f32[256,256]{1,0:T(8,128)}, u32[]{:S(2)}) copy-start(f32[256,256]{1,0:T(8,128)} %fusion.70.tri_ref) | copy-start | bytes 786436
  63.0 1.0 copy-start.2
  84.6 12.4 %all-to-all-start.3 = ((f32[8,16,256]{2,1,0:T(8,128)}), f32[8,16,256]{2,1,0:T(8,128)S(1)}, u32[]{:S(2)}, u32[]{:S(2)}) async-start(f32[8,16,256]{2,1,0:T(8,128)} %shard_map.49), calls=%async_computation.3 | async-start | bytes 262144 | tf_op jit(solution)/shard_map/all_to_all | solution.py:17
  96.9 1.6 copy-start.1
  98.5 1.2 copy-start.3
  99.8 1.6 copy-start.5
  101.4 15.4 %copy-start.8 = (f32[256,256]{1,0:T(8,128)S(1)}, f32[256,256]{1,0:T(8,128)}, u32[]{:S(2)}) copy-start(f32[256,256]{1,0:T(8,128)} %fusion.73.tri_ref) | copy-start | bytes 786436
  101.4 27.2 %copy-start = (bf16[16,1,16,4096]{3,2,1,0:T(8,128)(2,1)S(1)}, bf16[16,1,16,4096]{3,2,1,0:T(8,128)(2,1)}, u32[]{:S(2)}) copy-start(bf16[16,1,16,4096]{3,2,1,0:T(8,128)(2,1)} %get-tuple-element.26) | copy-start | bytes 6291460
  128.6 14.3 %copy-start.7 = (f32[256,256]{1,0:T(8,128)S(1)}, f32[256,256]{1,0:T(8,128)}, u32[]{:S(2)}) copy-start(f32[256,256]{1,0:T(8,128)} %fusion.76.tri_ref) | copy-start | bytes 786436
Sparse Core Ops, SparseCore 0:
  21.0 50.7 all-gather.1

commit v5 on v1

v5 whole, which is shorter than its diff:
```python
import functools

import jax
import jax.numpy as jnp
from jax import lax
from jax.experimental import pallas as pl
from jax.experimental.pallas import tpu as pltpu
from jax.sharding import Mesh
from jax.sharding import PartitionSpec as P

PCOL = ("pcol_0", "pcol_1", "pcol_2")
CHUNK = 1024
F32 = jnp.float32
BF16 = jnp.bfloat16
ROWS_BY_LANES = (((1,), (1,)), ((), ()))
LIMIT = 24 << 20


def exchange(parts, axis):
    return lax.all_to_all(parts, axis, split_axis=0, concat_axis=0, tiled=True)


def copy_for_each(x, axis, devices):
    return exchange(jnp.broadcast_to(x, (devices, *x.shape)), axis)


def from_partner(x):
    return lax.ppermute(x, "pcol_2", [(0, 1), (1, 0)])


def after(x, *earlier):
    return lax.optimization_barrier((x, *earlier))[0]


def two_terms(x):
    high = x.astype(BF16)
    low = (x - high.astype(F32)).astype(BF16)
    return jnp.concatenate([high, low], axis=0)


def folded(x):
    half = x.shape[0] // 2
    return x[:half] + x[half:]


def cost(flops, *operands):
    moved = sum(x.size * x.dtype.itemsize for x in operands)
    return pl.CostEstimate(flops=flops, bytes_accessed=moved, transcendentals=0)


def whole(memory_space=pltpu.VMEM):
    return pl.BlockSpec(memory_space=memory_space)


def local_call(kernel, shapes, flops, *operands, scalars=0):
    single = not isinstance(shapes, (list, tuple))
    return pl.pallas_call(
        kernel,
        out_shape=shapes,
        in_specs=[whole(pltpu.SMEM)] * scalars + [whole()] * (len(operands) - scalars),
        out_specs=whole() if single else [whole()] * len(shapes),
        cost_estimate=cost(flops, *operands),
        compiler_params=pltpu.CompilerParams(vmem_limit_bytes=LIMIT),
    )(*operands)


def fixed(*shape):
    return pl.BlockSpec(shape, lambda i: (0,) * len(shape))


def by_lanes(rows):
    return pl.BlockSpec((rows, CHUNK), lambda i: (0, i))


def panel_of(gathered, position):
    owners, _, inner, _ = gathered.shape
    return pl.BlockSpec((owners, None, inner, CHUNK), lambda i: (0, position, 0, i))


def streamed_call(kernel, shapes, in_specs, out_specs, scratch, flops, *operands):
    return pl.pallas_call(
        kernel,
        grid=(4096 // CHUNK,),
        out_shape=shapes,
        in_specs=in_specs,
        out_specs=out_specs,
        scratch_shapes=scratch,
        cost_estimate=cost(flops, *operands),
        compiler_params=pltpu.CompilerParams(
            vmem_limit_bytes=LIMIT, dimension_semantics=("arbitrary",)
        ),
    )(*operands)


def rows_of(ref):
    owners, inner, width = ref.shape
    return ref[...].reshape(owners * inner, width)


def products(reflectors, terms):
    return lax.dot_general(reflectors, terms, ROWS_BY_LANES, preferred_element_type=F32)


def settled(both):
    columns = both.shape[1] // 2
    return (both[:, :columns] + both[:, columns:]).T


def split_kernel(z_ref, turned_ref, terms_ref):
    for i in range(z_ref.shape[0] // CHUNK):
        part = slice(i * CHUNK, (i + 1) * CHUNK)
        turned = z_ref[part, :].T
        turned_ref[:, part] = turned
        terms_ref[:, part] = two_terms(turned)


def first_kernel(terms_ref, half_ref, sums_ref):
    sums_ref[...] = settled(products(half_ref[...], terms_ref[...]))


def second_kernel(terms_ref, half_ref, before_ref, sums_ref):
    size = before_ref.shape[1]
    sums_ref[:, :size] = before_ref[...]
    sums_ref[:, size:] = settled(products(half_ref[...], terms_ref[...]))


def gram_kernel(core_ref, half_ref, other_ref, gram_ref):
    @pl.when(pl.program_id(0) == 0)
    def _():
        gram_ref[...] = jnp.zeros_like(gram_ref)

    gram_ref[...] += products(rows_of(half_ref), rows_of(other_ref))


def updated(z_ref, image, used):
    change = jnp.dot(two_terms(image), used, preferred_element_type=F32)
    return z_ref[...] - folded(change)


def accumulated(total_ref, part):
    @pl.when(pl.program_id(0) == 0)
    def _():
        total_ref[...] = part

    @pl.when(pl.program_id(0) > 0)
    def _():
        total_ref[...] += part


def ended():
    return pl.program_id(0) == pl.num_programs(0) - 1


def step_kernel(z_ref, image_ref, own_ref, partner_ref, next_ref, gram_ref, new_ref, parts_ref, total_ref):
    used = jnp.concatenate([own_ref[...], partner_ref[...]], axis=0)
    current = updated(z_ref, image_ref[...], used)
    new_ref[...] = current
    accumulated(total_ref, products(rows_of(next_ref), two_terms(current)))

    @pl.when(ended())
    def _():
        devices, both, size = parts_ref.shape
        parts_ref[:, : both // 2, :] = settled(total_ref[...]).reshape(devices, both // 2, size)
        parts_ref[:, both // 2 :, :] = gram_ref[...].reshape(devices, both // 2, size)


def pair_kernel(z_ref, copies_ref, used_ref, high_ref, low_ref, new_ref, sums_ref, total_ref):
    devices, both, size = copies_ref.shape
    image = copies_ref[:, : both // 2, :].reshape(devices * both // 2, size)
    current = updated(z_ref, image, rows_of(used_ref))
    new_ref[...] = current
    following = jnp.concatenate([rows_of(high_ref), rows_of(low_ref)], axis=0)
    accumulated(total_ref, products(following, two_terms(current)))

    @pl.when(ended())
    def _():
        sums_ref[...] = settled(total_ref[...])


def last_kernel(z_ref, image_ref, high_ref, low_ref, result_ref):
    used = jnp.concatenate([rows_of(high_ref), rows_of(low_ref)], axis=0)
    result_ref[...] = updated(z_ref, image_ref[...], used).T


def applied(x, matrix):
    return lax.dot_general(
        x, matrix, ROWS_BY_LANES, precision=lax.Precision.HIGHEST, preferred_element_type=F32
    )


def summed(parts_ref):
    total = parts_ref[0]
    for device in range(1, parts_ref.shape[0]):
        total = total + parts_ref[device]
    return total


def share_kernel(parts_ref, tri_ref, copies_ref):
    image = applied(summed(parts_ref), tri_ref[...])
    for device in range(parts_ref.shape[0]):
        copies_ref[device] = image


def gram_share_kernel(parts_ref, tri_ref, copies_ref):
    total = summed(parts_ref)
    rows = total.shape[0] // 2
    image = applied(total[:rows], tri_ref[...])
    for device in range(parts_ref.shape[0]):
        copies_ref[device, :rows] = image
        copies_ref[device, rows:] = total[rows:]


def pair_share_kernel(parts_ref, high_ref, low_ref, gram_ref, copies_ref):
    total = summed(parts_ref)
    size = total.shape[1] // 2
    high = applied(total[:, :size], high_ref[...])
    low = applied(total[:, size:] - applied(high, gram_ref[...]), low_ref[...])
    for device in range(parts_ref.shape[0]):
        copies_ref[device, :, :size] = high
        copies_ref[device, :, size:] = low


def factor_kernel(wide, deep, each, core_ref, tau_ref, coupling_ref, *factor_refs):
    size = tau_ref.shape[1]
    row = lax.broadcasted_iota(jnp.int32, (size, size), 0)
    column = lax.broadcasted_iota(jnp.int32, (size, size), 1)
    spot, inner = row // each, row % each
    high, mid, low = spot // (2 * deep), spot // deep % 2, spot % deep
    together = ((high * deep + low) * 2 + mid) * each + inner
    core = core_ref[0]
    part, rest = row // (size // 2), row % (size // 2)
    parity = jnp.where(part == 0, core, 1 - core)
    across, along = rest // (wide * each), rest % (wide * each) // each
    alone = ((along * deep + across) * 2 + parity) * each + inner
    for position, factor_ref in enumerate(factor_refs):
        wanted = alone if position == len(factor_refs) - 1 else together
        choose = (wanted == column).astype(F32)
        upper = jnp.where(column > row, coupling_ref[position], 0.0)
        factor = jnp.where(column == row, tau_ref[position : position + 1, :], upper)
        turned = jnp.dot(choose, factor, precision=lax.Precision.HIGHEST, preferred_element_type=F32)
        factor_ref[...] = applied(turned, choose)


def on_device(vectors, reflectors, tau_diag, coupling):
    count, each, rows = reflectors.shape
    high_axis, low_axis, core_axis = PCOL
    wide, deep = lax.axis_size(high_axis), lax.axis_size(low_axis)
    devices = lax.axis_size("prow")
    core = lax.axis_index(core_axis)
    last = count - 1
    half = wide * deep * each
    size = 2 * half
    columns = vectors.shape[1]
    share = columns // devices

    def shape(*lengths, dtype=F32):
        return jax.ShapeDtypeStruct(lengths, dtype)

    early = copy_for_each(reflectors[:last], low_axis, deep)
    early = early.transpose(1, 0, 2, 3).reshape(last, deep * each, rows)
    later = lax.all_gather(early, (high_axis, core_axis), axis=0, tiled=False)

    group = copy_for_each(after(reflectors[last], early), high_axis, wide).reshape(wide * each, rows)

    where_core = core.astype(jnp.int32).reshape(1)
    factors = local_call(
        functools.partial(factor_kernel, wide, deep, each),
        [shape(size, size)] * count,
        count * 24 * size**3,
        where_core,
        tau_diag,
        coupling,
        scalars=1,
    )
    current, terms = local_call(
        split_kernel, [shape(columns, rows), shape(2 * columns, rows, dtype=BF16)], 1 << 24, vectors
    )
    start = after(group, current, terms, *factors)
    first = copy_for_each(start, low_axis, deep).reshape(half, rows)
    partner = from_partner(first)

    once = 4 * columns * half * rows
    sums = local_call(first_kernel, shape(columns, half), once, terms, first)
    sums = local_call(second_kernel, shape(columns, size), once, terms, partner, sums)
    arrived = exchange(sums.reshape(devices, share, size), "prow")
    copies = local_call(share_kernel, shape(devices, share, size), 1 << 24, arrived, factors[3])

    gathered = after(later, copies)
    owners, _, inner, _ = gathered.shape
    gram_half = pl.pallas_call(
        gram_kernel,
        grid_spec=pltpu.PrefetchScalarGridSpec(
            num_scalar_prefetch=1,
            grid=(rows // CHUNK,),
            in_specs=[
                pl.BlockSpec((owners // 2, None, inner, CHUNK), lambda i, core: (core[0], 0, 0, i)),
                pl.BlockSpec((owners, None, inner, CHUNK), lambda i, core: (0, 1, 0, i)),
            ],
            out_specs=pl.BlockSpec((half, size), lambda i, core: (0, 0)),
        ),
        out_shape=shape(half, size),
        cost_estimate=cost(2 * half * size * rows, gathered),
        compiler_params=pltpu.CompilerParams(
            vmem_limit_bytes=LIMIT, dimension_semantics=("arbitrary",)
        ),
    )(where_core, gathered, gathered)

    image = exchange(copies, "prow").reshape(columns, size)
    current, parts = streamed_call(
        step_kernel,
        [shape(columns, rows), shape(devices, 2 * share, size)],
        [
            by_lanes(columns),
            fixed(columns, size),
            by_lanes(half),
            by_lanes(half),
            panel_of(gathered, 2),
            fixed(half, size),
        ],
        [by_lanes(columns), fixed(devices, 2 * share, size)],
        [pltpu.VMEM((size, 2 * columns), F32)],
        4 * once,
        current,
        image,
        first,
        partner,
        gathered,
        gram_half,
    )
    arrived = exchange(parts, "prow")
    copies = local_call(gram_share_kernel, shape(*parts.shape), 1 << 24, arrived, factors[2])
    copies = exchange(copies, "prow")
    gram_own = copies[:, share:].reshape(half, size)
    gram_other = from_partner(gram_own)
    gram = jnp.where(
        core == 0,
        jnp.concatenate([gram_own, gram_other]),
        jnp.concatenate([gram_other, gram_own]),
    )
    current, sums = streamed_call(
        pair_kernel,
        [shape(columns, rows), shape(columns, 2 * size)],
        [
            by_lanes(columns),
            fixed(devices, 2 * share, size),
            panel_of(gathered, 2),
            panel_of(gathered, 1),
            panel_of(gathered, 0),
        ],
        [by_lanes(columns), fixed(columns, 2 * size)],
        [pltpu.VMEM((2 * size, 2 * columns), F32)],
        6 * once,
        current,
        copies,
        gathered,
        gathered,
        gathered,
    )
    arrived = exchange(sums.reshape(devices, share, 2 * size), "prow")
    copies = local_call(
        pair_share_kernel, shape(*arrived.shape), 1 << 24, arrived, factors[1], factors[0], gram
    )
    image = exchange(copies, "prow").reshape(columns, 2 * size)
    return streamed_call(
        last_kernel,
        shape(*vectors.shape),
        [by_lanes(columns), fixed(columns, 2 * size), panel_of(gathered, 1), panel_of(gathered, 0)],
        pl.BlockSpec((CHUNK, columns), lambda i: (i, 0)),
        [],
        4 * once,
        current,
        image,
        gathered,
        gathered,
    )


def solution(mesh):
    finer = Mesh(
        mesh.devices.reshape(mesh.shape["prow"], 8, 4, 2), ("prow", "pcol_0", "pcol_1", "pcol_2")
    )
    placed = (P("prow", PCOL), P(None, PCOL, "prow"), P(), P())
    return jax.shard_map(
        on_device, mesh=finer, in_specs=placed, out_specs=P("prow", PCOL), check_vma=False
    )
```

time: 233 us -> 175 us (0.75)
  the two profiles are of different devices: /device:TPU:4 before, /device:TPU:2 now
where the time goes in v5:
time: 175 us; the launch traced here: 174 us
  blocking collectives  87.8 us (50%)
  Pallas kernels  20.6 us (12%)
  local copies, waits for them, and re-layouts  19.9 us (11%)
  waiting for transfers between devices  17.7 us (10%)
  starting transfers between devices  14.8 us (8%)
  between operations  13.6 us (8%)
    all_to_all x6, blocking collectives, exchange(): return lax.all_to_all(parts, axis, split_axis=0, concat_axis=0, tiled=True)  87.8 us
    unnamed x34, local copies, waits for them, and re-layouts  15.1 us
    all_to_all x3, waiting for transfers between devices, exchange(): return lax.all_to_all(parts, axis, split_axis=0, concat_axis=0, tiled=True)  14.4 us
    pallas_call x3, Pallas kernels, streamed_call(): pl.pallas_call(kernel, grid=(4096 // CHUNK,), out_shape=shapes, in_specs=...  11.8 us
    all_to_all x3, starting transfers between devices, exchange(): return lax.all_to_all(parts, axis, split_axis=0, concat_axis=0, tiled=True)  10.9 us
    pallas_call x7, Pallas kernels, local_call(): pl.pallas_call(kernel, out_shape=shapes, in_specs=[whole(pltpu.SMEM)] * s...  7.31 us
    ppermute x2, starting transfers between devices, from_partner(): return lax.ppermute(x, 'pcol_2', [(0, 1), (1, 0)])  3.83 us
  transfers between devices with their start and end apart: 6, of which 5 were waited for; matrix products, arithmetic and copies ran while one was open for 2% of the time, Pallas kernels for 4%

profile of v5, /device:TPU:2, one launch (start us, length us, event | category | flops | bytes accessed | tf_op | source)
XLA Modules:
  0.0 174.4 jit_solution(11303618700495823124)
XLA Ops:
  6.5 0.9 slice.10
  7.5 0.1 broadcast_in_dim.11
  7.6 14.2 %all_to_all.45 = bf16[4,3,4,4096]{3,2,1,0:T(4,128)(2,1)S(1)} all-to-all(bf16[4,3,4,4096]{3,2,1,0:T(4,128)(2,1)S(1)} %broadcast_in_dim.11), channel_id=1, replica_groups=mesh['prow'=8,'pcol_0'=8,'pcol_1'=4,'pcol_2'=2] {'pcol_1'}, dimensions={0} | all-to-all | bytes 786432 | tf_op jit(solution)/shard_map/all_to_all | solution.py:20
  21.8 0.2 copy.5
  22.0 0.0 copy-start.16
  22.0 0.8 all_gather_reshape.3
  22.8 0.0 all-gather.2.cloned.1.call-update
  22.9 0.8 slice_bitcast_fusion
  23.6 0.8 broadcast_in_dim.9
  24.4 4.1 %all-to-all-start = ((bf16[8,4,4096]{2,1,0:T(4,128)(2,1)}), bf16[8,4,4096]{2,1,0:T(4,128)(2,1)}, u32[]{:S(2)}, u32[]{:S(2)}) async-start(bf16[8,4,4096]{2,1,0:T(4,128)(2,1)} %broadcast_in_dim.9), calls=%async_computation | async-start | bytes 524288 | tf_op jit(solution)/shard_map/all_to_all | solution.py:20
  28.6 1.6 copy-done.6
  30.2 0.6 shard_map.46
  30.8 1.3 copy-done.7
  32.1 2.4 %shard_map.47 = (f32[256,256]{1,0:T(8,128)S(1)}, f32[256,256]{1,0:T(8,128)S(1)}, f32[256,256]{1,0:T(8,128)S(1)}, f32[256,256]{1,0:T(8,128)S(1)}) custom-call(s32[1]{0:T(128)} %bitcast.1.core_ref, f32[4,256]{1,0:T(4,128)S(1)} %copy-done.16, f32[4,256,256]{2,1,0:T(8,128)S(1)} %copy-done.15), custom_call_target="tpu_custom_call" | custom-call | flops 1610612736 | bytes 1052676 | tf_op jit(solution)/shard_map/pallas_call | solution.py:57
  34.5 0.7 copy-done.9
  35.3 0.7 copy-done.11
  36.0 0.7 copy-done.13
  36.7 2.7 %all-to-all-done = bf16[8,4,4096]{2,1,0:T(4,128)(2,1)} async-done(((bf16[8,4,4096]{2,1,0:T(4,128)(2,1)}), bf16[8,4,4096]{2,1,0:T(4,128)(2,1)}, u32[]{:S(2)}, u32[]{:S(2)}) %all-to-all-start) | async-done | bytes 262176 | tf_op jit(solution)/shard_map/all_to_all | solution.py:20
  39.4 1.0 reshape.25
  40.4 0.1 broadcast_in_dim.10
  40.6 14.9 %all_to_all.46 = bf16[4,32,4096]{2,1,0:T(8,128)(2,1)S(1)} all-to-all(bf16[4,32,4096]{2,1,0:T(8,128)(2,1)S(1)} %broadcast_in_dim.10), channel_id=1, replica_groups=mesh['prow'=8,'pcol_0'=8,'pcol_1'=4,'pcol_2'=2] {'pcol_1'}, dimensions={0} | all-to-all | bytes 2097152 | tf_op jit(solution)/shard_map/all_to_all | solution.py:20
  55.5 1.9 %collective-permute-start = (bf16[128,4096]{1,0:T(8,128)(2,1)S(1)}, bf16[128,4096]{1,0:T(8,128)(2,1)S(1)}, u32[]{:S(2)}, u32[]{:S(2)}) collective-permute-start(bf16[128,4096]{1,0:T(8,128)(2,1)S(1)} %bitcast.10), channel_id=1, source_target_pairs={{0,1},{1,0},{2,3},{3,2},{4,5},{5,4},{6,7},{7,6},{8,9},{9,8},{10,11... | collective-permute-start | bytes 3145736 | tf_op jit(solution)/shard_map/ppermute | solution.py:28
  57.4 0.9 shard_map.48.before_ref
  58.3 1.9 %collective-permute-done.half_ref.partner_ref = bf16[128,4096]{1,0:T(8,128)(2,1)S(1)} collective-permute-done((bf16[128,4096]{1,0:T(8,128)(2,1)S(1)}, bf16[128,4096]{1,0:T(8,128)(2,1)S(1)}, u32[]{:S(2)}, u32[]{:S(2)}) %collective-permute-start) | collective-permute-done | bytes 1048608 | tf_op jit(solution)/shard_map/ppermute | solution.py:28
  60.2 0.9 shard_map.49
  61.1 0.1 copy-done.4
  61.2 20.0 %all_to_all.47.parts_ref = f32[8,16,256]{2,1,0:T(8,128)S(1)} all-to-all(f32[8,16,256]{2,1,0:T(8,128)S(1)} %bitcast.15), channel_id=1, replica_groups=mesh['prow'=8,'pcol_0'=8,'pcol_1'=4,'pcol_2'=2] {'prow'}, dimensions={0} | all-to-all | bytes 262144 | tf_op jit(solution)/shard_map/all_to_all | solution.py:20
  81.2 1.0 shard_map.50
  82.2 3.4 %all-to-all-start.3 = ((f32[8,16,256]{2,1,0:T(8,128)}), f32[8,16,256]{2,1,0:T(8,128)S(1)}, u32[]{:S(2)}, u32[]{:S(2)}) async-start(f32[8,16,256]{2,1,0:T(8,128)} %shard_map.50), calls=%async_computation.3 | async-start | bytes 262144 | tf_op jit(solution)/shard_map/all_to_all | solution.py:20
  85.6 0.0 all-gather.2.cloned.1.call-done.half_ref.other_ref.next_ref.used_ref.high_ref.low_ref
  85.6 2.8 %copy-done = bf16[16,3,16,4096]{3,2,1,0:T(8,128)(2,1)S(1)} copy-done((bf16[16,3,16,4096]{3,2,1,0:T(8,128)(2,1)S(1)}, bf16[16,3,16,4096]{3,2,1,0:T(8,128)(2,1)}, u32[]{:S(2)}) %copy-start) | copy-done | bytes 6291480
  88.4 1.5 shard_map.51.gram_ref
  89.9 4.6 %all-to-all-done.3 = f32[8,16,256]{2,1,0:T(8,128)S(1)} async-done(((f32[8,16,256]{2,1,0:T(8,128)}), f32[8,16,256]{2,1,0:T(8,128)S(1)}, u32[]{:S(2)}, u32[]{:S(2)}) %all-to-all-start.3) | async-done | bytes 131104 | tf_op jit(solution)/shard_map/all_to_all | solution.py:20
  94.6 2.8 %copy-done.1 = bf16[16,3,16,4096]{3,2,1,0:T(8,128)(2,1)S(1)} copy-done((bf16[16,3,16,4096]{3,2,1,0:T(8,128)(2,1)S(1)}, bf16[16,3,16,4096]{3,2,1,0:T(8,128)(2,1)}, u32[]{:S(2)}) %copy-start.1) | copy-done | bytes 6291480
  97.3 1.6 copy-done.8
  98.9 3.5 %shard_map.52 = (f32[128,4096]{1,0:T(8,128)S(1)}, f32[8,32,256]{2,1,0:T(8,128)S(1)}) custom-call(f32[128,4096]{1,0:T(8,128)S(1)} %copy-done.8, f32[128,256]{1,0:T(8,128)S(1)} %bitcast.14, bf16[128,4096]{1,0:T(8,128)(2,1)S(1)} %bitcast.12, bf16[128,4096]{1,0:T(8,128)(2,1)S(1)} %copy-done.5, bf16[16,3,16,4096]{3,2,1,0:T(8,128)(2,1)S(1)} %copy-done.1, ...), custom_call_target="tpu_custom_call" | custom-call | flops 1073741824 | bytes 10747904 | tf_op jit(solution)/shard_map/pallas_call | solution.py:81
  102.4 12.9 %all_to_all.48.parts_ref = f32[8,32,256]{2,1,0:T(8,128)S(1)} all-to-all(f32[8,32,256]{2,1,0:T(8,128)S(1)} %get-tuple-element.26), channel_id=1, replica_groups=mesh['prow'=8,'pcol_0'=8,'pcol_1'=4,'pcol_2'=2] {'prow'}, dimensions={0} | all-to-all | bytes 524288 | tf_op jit(solution)/shard_map/all_to_all | solution.py:20
  115.3 0.3 shard_map.53
  115.6 12.9 %all_to_all.49.copies_ref = f32[8,32,256]{2,1,0:T(8,128)S(1)} all-to-all(f32[8,32,256]{2,1,0:T(8,128)S(1)} %shard_map.53), channel_id=1, replica_groups=mesh['prow'=8,'pcol_0'=8,'pcol_1'=4,'pcol_2'=2] {'prow'}, dimensions={0} | all-to-all | bytes 524288 | tf_op jit(solution)/shard_map/all_to_all | solution.py:20
  128.5 4.7 %shard_map.54 = (f32[128,4096]{1,0:T(8,128)S(1)}, f32[128,512]{1,0:T(8,128)}) custom-call(f32[128,4096]{1,0:T(8,128)S(1)} %get-tuple-element.25.z_ref, f32[8,32,256]{2,1,0:T(8,128)S(1)} %all_to_all.49.copies_ref, bf16[16,3,16,4096]{3,2,1,0:T(8,128)(2,1)S(1)} %copy-done.2, bf16[16,3,16,4096]{3,2,1,0:T(8,128)(2,1)S(1)} %copy-done.2, ...), custom_call_target="tpu_custom_call" | custom-call | flops 1610612736 | bytes 21233664 | tf_op jit(solution)/shard_map/pallas_call | solution.py:81
  133.2 3.4 %all-to-all-start.7 = ((f32[8,16,512]{2,1,0:T(8,128)}), f32[8,16,512]{2,1,0:T(8,128)S(1)}, u32[]{:S(2)}, u32[]{:S(2)}) async-start(f32[8,16,512]{2,1,0:T(8,128)} %bitcast.6), calls=%async_computation.7 | async-start | bytes 524288 | tf_op jit(solution)/shard_map/all_to_all | solution.py:20
  136.7 1.9 %collective-permute-start.1 = (f32[128,256]{1,0:T(8,128)S(1)}, f32[128,256]{1,0:T(8,128)S(1)}, u32[]{:S(2)}, u32[]{:S(2)}) collective-permute-start(f32[128,256]{1,0:T(8,128)S(1)} %bitcast.17), channel_id=1, source_target_pairs={{0,1},{1,0},{2,3},{3,2},{4,5},{5,4},{6,7},{7,6},{8,9},{9,8},{10,11... | collective-permute-start | bytes 393224 | tf_op jit(solution)/shard_map/ppermute | solution.py:28
  138.6 1.3 collective-permute-done.1
  140.0 7.1 %all-to-all-done.7.parts_ref = f32[8,16,512]{2,1,0:T(8,128)S(1)} async-done(((f32[8,16,512]{2,1,0:T(8,128)}), f32[8,16,512]{2,1,0:T(8,128)S(1)}, u32[]{:S(2)}, u32[]{:S(2)}) %all-to-all-start.7) | async-done | bytes 262176 | tf_op jit(solution)/shard_map/all_to_all | solution.py:20
  147.1 1.2 shard_map.55
  148.3 12.9 %all_to_all.50 = f32[8,16,512]{2,1,0:T(8,128)S(1)} all-to-all(f32[8,16,512]{2,1,0:T(8,128)S(1)} %shard_map.55), channel_id=1, replica_groups=mesh['prow'=8,'pcol_0'=8,'pcol_1'=4,'pcol_2'=2] {'prow'}, dimensions={0} | all-to-all | bytes 524288 | tf_op jit(solution)/shard_map/all_to_all | solution.py:20
  161.2 2.8 %copy-done.3 = bf16[16,3,16,4096]{3,2,1,0:T(8,128)(2,1)S(1)} copy-done((bf16[16,3,16,4096]{3,2,1,0:T(8,128)(2,1)S(1)}, bf16[16,3,16,4096]{3,2,1,0:T(8,128)(2,1)}, u32[]{:S(2)}) %copy-start.3) | copy-done | bytes 6291480
  164.0 3.6 %shard_map.56 = f32[4096,128]{1,0:T(8,128)} custom-call(f32[128,4096]{1,0:T(8,128)S(1)} %get-tuple-element.27.z_ref, f32[128,512]{1,0:T(8,128)S(1)} %bitcast.13, bf16[16,3,16,4096]{3,2,1,0:T(8,128)(2,1)S(1)} %copy-done.3, bf16[16,3,16,4096]{3,2,1,0:T(8,128)(2,1)S(1)} %copy-done.3), custom_call_target="tpu_custom_call" | custom-call | flops 1073741824 | bytes 14942208 | tf_op jit(solution)/shard_map/pallas_call | solution.py:81
  (26 shorter events, 0.1 us)
Async XLA Ops:
  6.5 79.0 %all-gather.2.cloned.1.call-start = ((), (), s32[]{:S(2)}) async-start(), calls=%async_computation.9 | async-start | bytes 6684672 | tf_op jit(solution)/shard_map/all_gather | solution.py:261
  22.0 10.1 %copy-start.15 = (f32[4,256,256]{2,1,0:T(8,128)S(1)}, f32[4,256,256]{2,1,0:T(8,128)}, u32[]{:S(2)}) copy-start(f32[4,256,256]{2,1,0:T(8,128)} %coupling_ref.1) | copy-start | bytes 3145732
  22.0 10.1 %copy-start.16 = (f32[4,256]{1,0:T(4,128)S(1)}, f32[4,256]{1,0:T(4,128)}, u32[]{:S(2)}) copy-start(f32[4,256]{1,0:T(4,128)} %tau_ref.1) | copy-start | bytes 12292
  24.4 15.0 %all-to-all-start = ((bf16[8,4,4096]{2,1,0:T(4,128)(2,1)}), bf16[8,4,4096]{2,1,0:T(4,128)(2,1)}, u32[]{:S(2)}, u32[]{:S(2)}) async-start(bf16[8,4,4096]{2,1,0:T(4,128)(2,1)} %broadcast_in_dim.9), calls=%async_computation | async-start | bytes 524288 | tf_op jit(solution)/shard_map/all_to_all | solution.py:20
  28.6 1.6 copy-start.6
  30.8 1.3 copy-start.7
  34.5 0.7 copy-start.9
  35.3 0.7 copy-start.11
  36.0 0.7 copy-start.13
  55.5 4.7 %collective-permute-start = (bf16[128,4096]{1,0:T(8,128)(2,1)S(1)}, bf16[128,4096]{1,0:T(8,128)(2,1)S(1)}, u32[]{:S(2)}, u32[]{:S(2)}) collective-permute-start(bf16[128,4096]{1,0:T(8,128)(2,1)S(1)} %bitcast.10), channel_id=1, source_target_pairs={{0,1},{1,0},{2,3},{3,2},{4,5},{5,4},{6,7},{7,6},{8,9},{9,8},{10,11... | collective-permute-start | bytes 3145736 | tf_op jit(solution)/shard_map/ppermute | solution.py:28
  58.3 22.9 %copy-start.14 = (f32[256,256]{1,0:T(8,128)S(1)}, f32[256,256]{1,0:T(8,128)}, u32[]{:S(2)}) copy-start(f32[256,256]{1,0:T(8,128)} %copy-done.13) | copy-start | bytes 786436
  60.2 1.0 copy-start.4
  82.2 12.4 %all-to-all-start.3 = ((f32[8,16,256]{2,1,0:T(8,128)}), f32[8,16,256]{2,1,0:T(8,128)S(1)}, u32[]{:S(2)}, u32[]{:S(2)}) async-start(f32[8,16,256]{2,1,0:T(8,128)} %shard_map.50), calls=%async_computation.3 | async-start | bytes 262144 | tf_op jit(solution)/shard_map/all_to_all | solution.py:20
  85.6 2.8 %copy-start = (bf16[16,3,16,4096]{3,2,1,0:T(8,128)(2,1)S(1)}, bf16[16,3,16,4096]{3,2,1,0:T(8,128)(2,1)}, u32[]{:S(2)}) copy-start(bf16[16,3,16,4096]{3,2,1,0:T(8,128)(2,1)} %all-gather.2.cloned.1.call-done.half_ref.other_ref.next_ref.used_ref.high_ref.low_ref) | copy-start | bytes 18874372
  88.4 6.2 %copy-start.5 = (bf16[128,4096]{1,0:T(8,128)(2,1)S(1)}, bf16[128,4096]{1,0:T(8,128)(2,1)}, u32[]{:S(2)}) copy-start(bf16[128,4096]{1,0:T(8,128)(2,1)} %copy-done.4) | copy-start | bytes 3145732
  94.6 2.8 %copy-start.1 = (bf16[16,3,16,4096]{3,2,1,0:T(8,128)(2,1)S(1)}, bf16[16,3,16,4096]{3,2,1,0:T(8,128)(2,1)}, u32[]{:S(2)}) copy-start(bf16[16,3,16,4096]{3,2,1,0:T(8,128)(2,1)} %all-gather.2.cloned.1.call-done.half_ref.other_ref.next_ref.used_ref.high_ref.low_ref) | copy-start | bytes 18874372
  97.3 1.6 copy-start.8
  98.9 16.4 %copy-start.12 = (f32[256,256]{1,0:T(8,128)S(1)}, f32[256,256]{1,0:T(8,128)}, u32[]{:S(2)}) copy-start(f32[256,256]{1,0:T(8,128)} %copy-done.11) | copy-start | bytes 786436
  98.9 29.6 %copy-start.2 = (bf16[16,3,16,4096]{3,2,1,0:T(8,128)(2,1)S(1)}, bf16[16,3,16,4096]{3,2,1,0:T(8,128)(2,1)}, u32[]{:S(2)}) copy-start(bf16[16,3,16,4096]{3,2,1,0:T(8,128)(2,1)} %all-gather.2.cloned.1.call-done.half_ref.other_ref.next_ref.used_ref.high_ref.low_ref) | copy-start | bytes 18874372
  128.5 18.5 %copy-start.10 = (f32[256,256]{1,0:T(8,128)S(1)}, f32[256,256]{1,0:T(8,128)}, u32[]{:S(2)}) copy-start(f32[256,256]{1,0:T(8,128)} %copy-done.9) | copy-start | bytes 786436
  133.2 13.8 %all-to-all-start.7 = ((f32[8,16,512]{2,1,0:T(8,128)}), f32[8,16,512]{2,1,0:T(8,128)S(1)}, u32[]{:S(2)}, u32[]{:S(2)}) async-start(f32[8,16,512]{2,1,0:T(8,128)} %bitcast.6), calls=%async_computation.7 | async-start | bytes 524288 | tf_op jit(solution)/shard_map/all_to_all | solution.py:20
  136.7 3.2 %collective-permute-start.1 = (f32[128,256]{1,0:T(8,128)S(1)}, f32[128,256]{1,0:T(8,128)S(1)}, u32[]{:S(2)}, u32[]{:S(2)}) collective-permute-start(f32[128,256]{1,0:T(8,128)S(1)} %bitcast.17), channel_id=1, source_target_pairs={{0,1},{1,0},{2,3},{3,2},{4,5},{5,4},{6,7},{7,6},{8,9},{9,8},{10,11... | collective-permute-start | bytes 393224 | tf_op jit(solution)/shard_map/ppermute | solution.py:28
  161.2 2.8 %copy-start.3 = (bf16[16,3,16,4096]{3,2,1,0:T(8,128)(2,1)S(1)}, bf16[16,3,16,4096]{3,2,1,0:T(8,128)(2,1)}, u32[]{:S(2)}) copy-start(bf16[16,3,16,4096]{3,2,1,0:T(8,128)(2,1)} %all-gather.2.cloned.1.call-done.half_ref.other_ref.next_ref.used_ref.high_ref.low_ref) | copy-start | bytes 18874372
Sparse Core Ops, SparseCore 0:
  23.0 49.3 all-gather.1

commit v6 on v5

--- a/solution.py
+++ b/solution.py
@@ -10,10 +10,13 @@
 
 PCOL = ("pcol_0", "pcol_1", "pcol_2")
 CHUNK = 1024
+PIECE = 512
 F32 = jnp.float32
 BF16 = jnp.bfloat16
 ROWS_BY_LANES = (((1,), (1,)), ((), ()))
 LIMIT = 24 << 20
+FETCH_LIMIT = 52 << 20
+GRAM_LIMIT = 60 << 20
 
 
 def exchange(parts, axis):
@@ -64,32 +67,16 @@
     )(*operands)
 
 
-def fixed(*shape):
-    return pl.BlockSpec(shape, lambda i: (0,) * len(shape))
-
-
-def by_lanes(rows):
-    return pl.BlockSpec((rows, CHUNK), lambda i: (0, i))
-
-
-def panel_of(gathered, position):
-    owners, _, inner, _ = gathered.shape
-    return pl.BlockSpec((owners, None, inner, CHUNK), lambda i: (0, position, 0, i))
-
-
-def streamed_call(kernel, shapes, in_specs, out_specs, scratch, flops, *operands):
+def fetching_call(kernel, shapes, out_spaces, scratch, flops, far, near):
     return pl.pallas_call(
         kernel,
-        grid=(4096 // CHUNK,),
         out_shape=shapes,
-        in_specs=in_specs,
-        out_specs=out_specs,
+        in_specs=[whole(pltpu.HBM)] * len(far) + [whole()] * len(near),
+        out_specs=[whole(space) for space in out_spaces],
         scratch_shapes=scratch,
-        cost_estimate=cost(flops, *operands),
-        compiler_params=pltpu.CompilerParams(
-            vmem_limit_bytes=LIMIT, dimension_semantics=("arbitrary",)
-        ),
-    )(*operands)
+        cost_estimate=cost(flops, *far, *near),
+        compiler_params=pltpu.CompilerParams(vmem_limit_bytes=FETCH_LIMIT),
+    )(*far, *near)
 
 
 def rows_of(ref):
@@ -132,54 +119,124 @@
     gram_ref[...] += products(rows_of(half_ref), rows_of(other_ref))
 
 
-def updated(z_ref, image, used):
-    change = jnp.dot(two_terms(image), used, preferred_element_type=F32)
-    return z_ref[...] - folded(change)
-
-
-def accumulated(total_ref, part):
-    @pl.when(pl.program_id(0) == 0)
-    def _():
-        total_ref[...] = part
-
-    @pl.when(pl.program_id(0) > 0)
-    def _():
-        total_ref[...] += part
-
-
-def ended():
-    return pl.program_id(0) == pl.num_programs(0) - 1
-
-
-def step_kernel(z_ref, image_ref, own_ref, partner_ref, next_ref, gram_ref, new_ref, parts_ref, total_ref):
-    used = jnp.concatenate([own_ref[...], partner_ref[...]], axis=0)
-    current = updated(z_ref, image_ref[...], used)
-    new_ref[...] = current
-    accumulated(total_ref, products(rows_of(next_ref), two_terms(current)))
-
-    @pl.when(ended())
-    def _():
-        devices, both, size = parts_ref.shape
-        parts_ref[:, : both // 2, :] = settled(total_ref[...]).reshape(devices, both // 2, size)
-        parts_ref[:, both // 2 :, :] = gram_ref[...].reshape(devices, both // 2, size)
-
-
-def pair_kernel(z_ref, copies_ref, used_ref, high_ref, low_ref, new_ref, sums_ref, total_ref):
+def stretch(i):
+    return slice(i * PIECE, (i + 1) * PIECE)
+
+
+def fetched(sources, buffers, arrivals):
+    copies = []
+    for i in range(buffers[0].shape[-1] // PIECE):
+        row = []
+        for k, (source, buffer) in enumerate(zip(sources, buffers)):
+            part = (slice(None),) * (len(buffer.shape) - 1) + (pl.ds(i * PIECE, PIECE),)
+            row.append(pltpu.make_async_copy(source.at[part], buffer.at[part], arrivals.at[k, i]))
+            row[-1].start()
+        copies.append(row)
+    return copies
+
+
+def returned(buffer, target, departures, i):
+    part = (slice(None), pl.ds(i * PIECE, PIECE))
+    return pltpu.make_async_copy(buffer.at[part], target.at[part], departures.at[i])
+
+
+def piece_of(buffer, i):
+    if len(buffer.shape) == 2:
+        return buffer[:, stretch(i)]
+    owners, inner, _ = buffer.shape
+    return buffer[:, :, stretch(i)].reshape(owners * inner, PIECE)
+
+
+def stacked(buffers, i):
+    return jnp.concatenate([piece_of(buffer, i) for buffer in buffers], axis=0)
+
+
+def advanced(image, sources, z_new, buffers, used, following, total, arrivals, departures):
+    z_buffer = buffers[0]
+    copies = fetched(sources, buffers, arrivals)
+    terms = two_terms(image)
+    for i, row in enumerate(copies):
+        for copy in row:
+            copy.wait()
+        change = jnp.dot(terms, stacked(used, i), preferred_element_type=F32)
+        current = z_buffer[:, stretch(i)] - folded(change)
+        z_buffer[:, stretch(i)] = current
+        part = products(stacked(following, i), two_terms(current))
+        if i == 0:
+            total[...] = part
+        else:
+            total[...] += part
+            returned(z_buffer, z_new, departures, i - 1).start()
+    returned(z_buffer, z_new, departures, len(copies) - 1).start()
+
+
+def drained(z_buffer, z_new, departures):
+    for i in range(z_buffer.shape[1] // PIECE):
+        returned(z_buffer, z_new, departures, i).wait()
+
+
+def step_kernel(
+    z, own, partner, gathered, image_ref, gram_ref, z_new, parts_ref,
+    z_buffer, own_buffer, partner_buffer, next_buffer, total, arrivals, departures,
+):
+    advanced(
+        image_ref[...],
+        [z, own, partner, gathered.at[:, 2]],
+        z_new,
+        [z_buffer, own_buffer, partner_buffer, next_buffer],
+        [own_buffer, partner_buffer],
+        [next_buffer],
+        total,
+        arrivals,
+        departures,
+    )
+    devices, both, size = parts_ref.shape
+    parts_ref[:, : both // 2, :] = settled(total[...]).reshape(devices, both // 2, size)
+    parts_ref[:, both // 2 :, :] = gram_ref[...].reshape(devices, both // 2, size)
+    drained(z_buffer, z_new, departures)
+
+
+def pair_kernel(
+    z, gathered, copies_ref, z_new, sums_ref,
+    z_buffer, used_buffer, high_buffer, low_buffer, total, arrivals, departures,
+):
     devices, both, size = copies_ref.shape
-    image = copies_ref[:, : both // 2, :].reshape(devices * both // 2, size)
-    current = updated(z_ref, image, rows_of(used_ref))
-    new_ref[...] = current
-    following = jnp.concatenate([rows_of(high_ref), rows_of(low_ref)], axis=0)
-    accumulated(total_ref, products(following, two_terms(current)))
-
-    @pl.when(ended())
-    def _():
-        sums_ref[...] = settled(total_ref[...])
-
-
-def last_kernel(z_ref, image_ref, high_ref, low_ref, result_ref):
-    used = jnp.concatenate([rows_of(high_ref), rows_of(low_ref)], axis=0)
-    result_ref[...] = updated(z_ref, image_ref[...], used).T
+    advanced(
+        copies_ref[:, : both // 2, :].reshape(devices * both // 2, size),
+        [z, gathered.at[:, 2], gathered.at[:, 1], gathered.at[:, 0]],
+        z_new,
+        [z_buffer, used_buffer, high_buffer, low_buffer],
+        [used_buffer],
+        [high_buffer, low_buffer],
+        total,
+        arrivals,
+        departures,
+    )
+    sums_ref[...] = settled(total[...])
+    drained(z_buffer, z_new, departures)
+
+
+def last_kernel(
+    z, gathered, image_ref, result, z_buffer, high_buffer, low_buffer, out_buffer, arrivals, departures
+):
+    buffers = [z_buffer, high_buffer, low_buffer]
+    copies = fetched([z, gathered.at[:, 1], gathered.at[:, 0]], buffers, arrivals)
+    terms = two_terms(image_ref[...])
+
+    def leaving(i):
+        part = pl.ds(i * PIECE, PIECE)
+        return pltpu.make_async_copy(out_buffer.at[part, :], result.at[part, :], departures.at[i])
+
+    for i, row in enumerate(copies):
+        for copy in row:
+            copy.wait()
+        change = jnp.dot(terms, stacked(buffers[1:], i), preferred_element_type=F32)
+        out_buffer[stretch(i), :] = (z_buffer[:, stretch(i)] - folded(change)).T
+        if i > 0:
+            leaving(i - 1).start()
+    leaving(len(copies) - 1).start()
+    for i in range(len(copies)):
+        leaving(i).wait()
 
 
 def applied(x, matrix):
@@ -256,11 +313,11 @@
     def shape(*lengths, dtype=F32):
         return jax.ShapeDtypeStruct(lengths, dtype)
 
-    early = copy_for_each(reflectors[:last], low_axis, deep)
-    early = early.transpose(1, 0, 2, 3).reshape(last, deep * each, rows)
+    hopped = copy_for_each(reflectors[:last], low_axis, deep)
+    early = hopped.transpose(1, 0, 2, 3).reshape(last, deep * each, rows)
     later = lax.all_gather(early, (high_axis, core_axis), axis=0, tiled=False)
 
-    group = copy_for_each(after(reflectors[last], early), high_axis, wide).reshape(wide * each, rows)
+    group = copy_for_each(after(reflectors[last], hopped), high_axis, wide).reshape(wide * each, rows)
 
     where_core = core.astype(jnp.int32).reshape(1)
     factors = local_call(
@@ -301,31 +358,32 @@
         out_shape=shape(half, size),
         cost_estimate=cost(2 * half * size * rows, gathered),
         compiler_params=pltpu.CompilerParams(
-            vmem_limit_bytes=LIMIT, dimension_semantics=("arbitrary",)
+            vmem_limit_bytes=GRAM_LIMIT, dimension_semantics=("arbitrary",)
         ),
     )(where_core, gathered, gathered)
 
     image = exchange(copies, "prow").reshape(columns, size)
-    current, parts = streamed_call(
+    pieces = rows // PIECE
+    z_scratch = pltpu.VMEM((columns, rows), F32)
+    half_scratch = pltpu.VMEM((half, rows), BF16)
+    panel_scratch = pltpu.VMEM((owners, inner, rows), BF16)
+    departures = pltpu.SemaphoreType.DMA((pieces,))
+
+    def arrivals(arrays):
+        return pltpu.SemaphoreType.DMA((arrays, pieces))
+
+    spaces = [pltpu.HBM, pltpu.VMEM]
+    current, parts = fetching_call(
         step_kernel,
         [shape(columns, rows), shape(devices, 2 * share, size)],
+        spaces,
         [
-            by_lanes(columns),
-            fixed(columns, size),
-            by_lanes(half),
-            by_lanes(half),
-            panel_of(gathered, 2),
-            fixed(half, size),
+            z_scratch, half_scratch, half_scratch, panel_scratch,
+            pltpu.VMEM((size, 2 * columns), F32), arrivals(4), departures,
         ],
-        [by_lanes(columns), fixed(devices, 2 * share, size)],
-        [pltpu.VMEM((size, 2 * columns), F32)],
         4 * once,
-        current,
-        image,
-        first,
-        partner,
-        gathered,
-        gram_half,
+        [current, first, partner, gathered],
+        [image, gram_half],
     )
     arrived = exchange(parts, "prow")
     copies = local_call(gram_share_kernel, shape(*parts.shape), 1 << 24, arrived, factors[2])
@@ -337,42 +395,35 @@
         jnp.concatenate([gram_own, gram_other]),
         jnp.concatenate([gram_other, gram_own]),
     )
-    current, sums = streamed_call(
+    current, sums = fetching_call(
         pair_kernel,
         [shape(columns, rows), shape(columns, 2 * size)],
+        spaces,
         [
-            by_lanes(columns),
-            fixed(devices, 2 * share, size),
-            panel_of(gathered, 2),
-            panel_of(gathered, 1),
-            panel_of(gathered, 0),
+            z_scratch, panel_scratch, panel_scratch, panel_scratch,
+            pltpu.VMEM((2 * size, 2 * columns), F32), arrivals(4), departures,
         ],
-        [by_lanes(columns), fixed(columns, 2 * size)],
-        [pltpu.VMEM((2 * size, 2 * columns), F32)],
         6 * once,
-        current,
-        copies,
-        gathered,
-        gathered,
-        gathered,
+        [current, gathered],
+        [copies],
     )
     arrived = exchange(sums.reshape(devices, share, 2 * size), "prow")
     copies = local_call(
         pair_share_kernel, shape(*arrived.shape), 1 << 24, arrived, factors[1], factors[0], gram
     )
     image = exchange(copies, "prow").reshape(columns, 2 * size)
-    return streamed_call(
+    return fetching_call(
         last_kernel,
-        shape(*vectors.shape),
-        [by_lanes(columns), fixed(columns, 2 * size), panel_of(gathered, 1), panel_of(gathered, 0)],
-        pl.BlockSpec((CHUNK, columns), lambda i: (i, 0)),
-        [],
+        [shape(*vectors.shape)],
+        [pltpu.HBM],
+        [
+            z_scratch, panel_scratch, panel_scratch, pltpu.VMEM(vectors.shape, F32),
+            arrivals(3), departures,
+        ],
         4 * once,
-        current,
-        image,
-        gathered,
-        gathered,
-    )
+        [current, gathered],
+        [image],
+    )[0]
 
 
 def solution(mesh):

time: 175 us -> 175 us (level)
  local copies, waits for them, and re-layouts: 19.9 us -> 10.8 us
  Pallas kernels: 20.6 us -> 29.4 us
    unnamed x34 -> x24, local copies, waits for them, and re-layouts: 15.1 us -> 6.05 us
    pallas_call x3, Pallas kernels: 11.8 us -> 18.1 us  [fetching_call(): pl.pallas_call(kernel, out_shape=shapes, in_specs=[whole(pltpu.HBM)] * le...]
    pallas_call x1, Pallas kernels: 1.55 us -> 3.97 us  [on_device(): pl.pallas_call(gram_kernel, grid_spec=pltpu.PrefetchScalarGridSpec(num_sc...]
  transfers between devices with their start and end apart: 6 -> 6, of which waited for: 5 -> 5; matrix products, arithmetic and copies ran while one was open for 2% -> 2% of each run, Pallas kernels for 4% -> 6%
where the time goes in v6:
time: 175 us
  blocking collectives  87.8 us (50%)
  Pallas kernels  29.4 us (17%)
  waiting for transfers between devices  18.1 us (10%)
  starting transfers between devices  14.8 us (8%)
  between operations  13.6 us (8%)
  local copies, waits for them, and re-layouts  10.8 us (6%)
    all_to_all x6, blocking collectives, exchange(): return lax.all_to_all(parts, axis, split_axis=0, concat_axis=0, tiled=True)  87.8 us
    pallas_call x3, Pallas kernels, fetching_call(): pl.pallas_call(kernel, out_shape=shapes, in_specs=[whole(pltpu.HBM)] * le...  18.1 us
    all_to_all x3, waiting for transfers between devices, exchange(): return lax.all_to_all(parts, axis, split_axis=0, concat_axis=0, tiled=True)  14.8 us
    all_to_all x3, starting transfers between devices, exchange(): return lax.all_to_all(parts, axis, split_axis=0, concat_axis=0, tiled=True)  10.9 us
    pallas_call x7, Pallas kernels, local_call(): pl.pallas_call(kernel, out_shape=shapes, in_specs=[whole(pltpu.SMEM)] * s...  7.33 us
    unnamed x24, local copies, waits for them, and re-layouts  6.05 us
    pallas_call x1, Pallas kernels, on_device(): pl.pallas_call(gram_kernel, grid_spec=pltpu.PrefetchScalarGridSpec(num_sc...  3.97 us
    ppermute x2, starting transfers between devices, from_partner(): return lax.ppermute(x, 'pcol_2', [(0, 1), (1, 0)])  3.83 us
  transfers between devices with their start and end apart: 6, of which 5 were waited for; matrix products, arithmetic and copies ran while one was open for 2% of the time, Pallas kernels for 6%

profile of v6, /device:TPU:2, one launch (start us, length us, event | category | flops | bytes accessed | tf_op | source)
XLA Modules:
  0.0 174.5 jit_solution(10783149501917120470)
XLA Ops:
  6.5 0.9 slice.10
  7.5 0.1 broadcast_in_dim.9
  7.6 14.2 %all_to_all.45 = bf16[4,3,4,4096]{3,2,1,0:T(4,128)(2,1)S(1)} all-to-all(bf16[4,3,4,4096]{3,2,1,0:T(4,128)(2,1)S(1)} %broadcast_in_dim.9), channel_id=1, replica_groups=mesh['prow'=8,'pcol_0'=8,'pcol_1'=4,'pcol_2'=2] {'pcol_1'}, dimensions={0} | all-to-all | bytes 786432 | tf_op jit(solution)/shard_map/all_to_all | solution.py:23
  21.8 0.2 copy.5
  22.0 0.0 copy-start.10
  22.0 0.0 copy-start.11
  22.0 0.8 all_gather_reshape.3
  22.9 0.0 all-gather.2.cloned.1.call-update
  22.9 0.8 slice_bitcast_fusion
  23.7 0.8 broadcast_in_dim.10
  24.4 4.1 %all-to-all-start.1 = ((bf16[8,4,4096]{2,1,0:T(4,128)(2,1)}), bf16[8,4,4096]{2,1,0:T(4,128)(2,1)}, u32[]{:S(2)}, u32[]{:S(2)}) async-start(bf16[8,4,4096]{2,1,0:T(4,128)(2,1)} %broadcast_in_dim.10), calls=%async_computation.1 | async-start | bytes 524288 | tf_op jit(solution)/shard_map/all_to_all | solution.py:23
  28.6 1.6 copy-done.1
  30.2 0.6 shard_map.46
  30.8 0.0 copy-start.2
  30.8 1.3 copy-done.2
  32.1 2.4 %shard_map.47 = (f32[256,256]{1,0:T(8,128)S(1)}, f32[256,256]{1,0:T(8,128)S(1)}, f32[256,256]{1,0:T(8,128)S(1)}, f32[256,256]{1,0:T(8,128)S(1)}) custom-call(s32[1]{0:T(128)} %bitcast.1.core_ref, f32[4,256]{1,0:T(4,128)S(1)} %copy-done.11, f32[4,256,256]{2,1,0:T(8,128)S(1)} %copy-done.10), custom_call_target="tpu_custom_call" | custom-call | flops 1610612736 | bytes 1052676 | tf_op jit(solution)/shard_map/pallas_call | solution.py:60
  34.5 0.7 copy-done.4
  35.2 0.7 copy-done.6
  36.0 0.7 copy-done.8
  36.7 2.7 %all-to-all-done.1 = bf16[8,4,4096]{2,1,0:T(4,128)(2,1)} async-done(((bf16[8,4,4096]{2,1,0:T(4,128)(2,1)}), bf16[8,4,4096]{2,1,0:T(4,128)(2,1)}, u32[]{:S(2)}, u32[]{:S(2)}) %all-to-all-start.1) | async-done | bytes 262176 | tf_op jit(solution)/shard_map/all_to_all | solution.py:23
  39.4 1.0 reshape.24
  40.4 0.1 broadcast_in_dim.11
  40.5 14.9 %all_to_all.46 = bf16[4,32,4096]{2,1,0:T(8,128)(2,1)S(1)} all-to-all(bf16[4,32,4096]{2,1,0:T(8,128)(2,1)S(1)} %broadcast_in_dim.11), channel_id=1, replica_groups=mesh['prow'=8,'pcol_0'=8,'pcol_1'=4,'pcol_2'=2] {'pcol_1'}, dimensions={0} | all-to-all | bytes 2097152 | tf_op jit(solution)/shard_map/all_to_all | solution.py:23
  55.4 1.9 %collective-permute-start = (bf16[128,4096]{1,0:T(8,128)(2,1)S(1)}, bf16[128,4096]{1,0:T(8,128)(2,1)S(1)}, u32[]{:S(2)}, u32[]{:S(2)}) collective-permute-start(bf16[128,4096]{1,0:T(8,128)(2,1)S(1)} %bitcast.10), channel_id=1, source_target_pairs={{0,1},{1,0},{2,3},{3,2},{4,5},{5,4},{6,7},{7,6},{8,9},{9,8},{10,11... | collective-permute-start | bytes 3145736 | tf_op jit(solution)/shard_map/ppermute | solution.py:31
  57.4 0.9 shard_map.48.before_ref
  58.2 0.0 copy-start.9
  58.3 1.9 %collective-permute-done.half_ref.partner = bf16[128,4096]{1,0:T(8,128)(2,1)S(1)} collective-permute-done((bf16[128,4096]{1,0:T(8,128)(2,1)S(1)}, bf16[128,4096]{1,0:T(8,128)(2,1)S(1)}, u32[]{:S(2)}, u32[]{:S(2)}) %collective-permute-start) | collective-permute-done | bytes 1048608 | tf_op jit(solution)/shard_map/ppermute | solution.py:31
  60.2 0.9 shard_map.49
  61.1 0.1 copy-done
  61.1 20.1 %all_to_all.47.parts_ref = f32[8,16,256]{2,1,0:T(8,128)S(1)} all-to-all(f32[8,16,256]{2,1,0:T(8,128)S(1)} %bitcast.15), channel_id=1, replica_groups=mesh['prow'=8,'pcol_0'=8,'pcol_1'=4,'pcol_2'=2] {'prow'}, dimensions={0} | all-to-all | bytes 262144 | tf_op jit(solution)/shard_map/all_to_all | solution.py:23
  81.2 1.0 shard_map.50
  82.2 3.4 %all-to-all-start.4 = ((f32[8,16,256]{2,1,0:T(8,128)}), f32[8,16,256]{2,1,0:T(8,128)S(1)}, u32[]{:S(2)}, u32[]{:S(2)}) async-start(f32[8,16,256]{2,1,0:T(8,128)} %shard_map.50), calls=%async_computation.4 | async-start | bytes 262144 | tf_op jit(solution)/shard_map/all_to_all | solution.py:23
  85.6 0.0 all-gather.2.cloned.1.call-done.half_ref.other_ref.gathered
  85.6 4.0 %shard_map.51.gram_ref = f32[128,256]{1,0:T(8,128)} custom-call(s32[1]{0:T(128)} %bitcast.1.core_ref, bf16[16,3,16,4096]{3,2,1,0:T(8,128)(2,1)} %all-gather.2.cloned.1.call-done.half_ref.other_ref.gathered, bf16[16,3,16,4096]{3,2,1,0:T(8,128)(2,1)} %all-gather.2.cloned.1.call-done.half_ref.other_ref.gathered), custom_call_target="tpu_custom_call" | custom-call | flops 268435456 | bytes 6291456 | tf_op jit(solution)/shard_map/pallas_call | solution.py:347
  89.6 5.0 %all-to-all-done.4 = f32[8,16,256]{2,1,0:T(8,128)S(1)} async-done(((f32[8,16,256]{2,1,0:T(8,128)}), f32[8,16,256]{2,1,0:T(8,128)S(1)}, u32[]{:S(2)}, u32[]{:S(2)}) %all-to-all-start.4) | async-done | bytes 131104 | tf_op jit(solution)/shard_map/all_to_all | solution.py:23
  94.6 0.9 copy-done.3
  95.5 5.5 %shard_map.52 = (f32[128,4096]{1,0:T(8,128)}, f32[8,32,256]{2,1,0:T(8,128)S(1)}) custom-call(f32[128,4096]{1,0:T(8,128)} %copy-done.2, bf16[128,4096]{1,0:T(8,128)(2,1)S(1)} %bitcast.12, bf16[128,4096]{1,0:T(8,128)(2,1)} %copy-done, bf16[16,3,16,4096]{3,2,1,0:T(8,128)(2,1)} %all-gather.2.cloned.1.call-done.half_ref.other_ref.gathered, ...), custom_call_target="tpu_custom_call" | custom-call | flops 1073741824 | bytes 10747904 | tf_op jit(solution)/shard_map/pallas_call | solution.py:71
  101.0 12.9 %all_to_all.48.parts_ref = f32[8,32,256]{2,1,0:T(8,128)S(1)} all-to-all(f32[8,32,256]{2,1,0:T(8,128)S(1)} %get-tuple-element.28), channel_id=1, replica_groups=mesh['prow'=8,'pcol_0'=8,'pcol_1'=4,'pcol_2'=2] {'prow'}, dimensions={0} | all-to-all | bytes 524288 | tf_op jit(solution)/shard_map/all_to_all | solution.py:23
  113.8 0.3 shard_map.53
  114.2 12.9 %all_to_all.49.copies_ref = f32[8,32,256]{2,1,0:T(8,128)S(1)} all-to-all(f32[8,32,256]{2,1,0:T(8,128)S(1)} %shard_map.53), channel_id=1, replica_groups=mesh['prow'=8,'pcol_0'=8,'pcol_1'=4,'pcol_2'=2] {'prow'}, dimensions={0} | all-to-all | bytes 524288 | tf_op jit(solution)/shard_map/all_to_all | solution.py:23
  127.1 7.1 %shard_map.54 = (f32[128,4096]{1,0:T(8,128)}, f32[128,512]{1,0:T(8,128)}) custom-call(f32[128,4096]{1,0:T(8,128)} %get-tuple-element.27.z, bf16[16,3,16,4096]{3,2,1,0:T(8,128)(2,1)} %all-gather.2.cloned.1.call-done.half_ref.other_ref.gathered, f32[8,32,256]{2,1,0:T(8,128)S(1)} %all_to_all.49.copies_ref), custom_call_target="tpu_custom_call" | custom-call | flops 1610612736 | bytes 8650752 | tf_op jit(solution)/shard_map/pallas_call | solution.py:71
  134.2 3.4 %all-to-all-start.7 = ((f32[8,16,512]{2,1,0:T(8,128)}), f32[8,16,512]{2,1,0:T(8,128)S(1)}, u32[]{:S(2)}, u32[]{:S(2)}) async-start(f32[8,16,512]{2,1,0:T(8,128)} %bitcast.6), calls=%async_computation.7 | async-start | bytes 524288 | tf_op jit(solution)/shard_map/all_to_all | solution.py:23
  137.7 1.9 %collective-permute-start.1 = (f32[128,256]{1,0:T(8,128)S(1)}, f32[128,256]{1,0:T(8,128)S(1)}, u32[]{:S(2)}, u32[]{:S(2)}) collective-permute-start(f32[128,256]{1,0:T(8,128)S(1)} %bitcast.17), channel_id=1, source_target_pairs={{0,1},{1,0},{2,3},{3,2},{4,5},{5,4},{6,7},{7,6},{8,9},{9,8},{10,11... | collective-permute-start | bytes 393224 | tf_op jit(solution)/shard_map/ppermute | solution.py:31
  139.6 1.3 collective-permute-done.1
  140.9 7.1 %all-to-all-done.7.parts_ref = f32[8,16,512]{2,1,0:T(8,128)S(1)} async-done(((f32[8,16,512]{2,1,0:T(8,128)}), f32[8,16,512]{2,1,0:T(8,128)S(1)}, u32[]{:S(2)}, u32[]{:S(2)}) %all-to-all-start.7) | async-done | bytes 262176 | tf_op jit(solution)/shard_map/all_to_all | solution.py:23
  148.0 1.2 shard_map.55
  149.3 12.9 %all_to_all.50 = f32[8,16,512]{2,1,0:T(8,128)S(1)} all-to-all(f32[8,16,512]{2,1,0:T(8,128)S(1)} %shard_map.55), channel_id=1, replica_groups=mesh['prow'=8,'pcol_0'=8,'pcol_1'=4,'pcol_2'=2] {'prow'}, dimensions={0} | all-to-all | bytes 524288 | tf_op jit(solution)/shard_map/all_to_all | solution.py:23
  162.2 5.5 %shard_map.56 = f32[4096,128]{1,0:T(8,128)} custom-call(f32[128,4096]{1,0:T(8,128)} %get-tuple-element.29.z, bf16[16,3,16,4096]{3,2,1,0:T(8,128)(2,1)} %all-gather.2.cloned.1.call-done.half_ref.other_ref.gathered, f32[128,512]{1,0:T(8,128)S(1)} %bitcast.13), custom_call_target="tpu_custom_call" | custom-call | flops 1073741824 | bytes 8650752 | tf_op jit(solution)/shard_map/pallas_call | solution.py:71
  (16 shorter events, 0.1 us)
Async XLA Ops:
  6.5 79.0 %all-gather.2.cloned.1.call-start = ((), (), s32[]{:S(2)}) async-start(), calls=%async_computation.9 | async-start | bytes 6684672 | tf_op jit(solution)/shard_map/all_gather | solution.py:318
  22.0 10.1 %copy-start.10 = (f32[4,256,256]{2,1,0:T(8,128)S(1)}, f32[4,256,256]{2,1,0:T(8,128)}, u32[]{:S(2)}) copy-start(f32[4,256,256]{2,1,0:T(8,128)} %coupling_ref.1) | copy-start | bytes 3145732
  22.0 10.1 %copy-start.11 = (f32[4,256]{1,0:T(4,128)S(1)}, f32[4,256]{1,0:T(4,128)}, u32[]{:S(2)}) copy-start(f32[4,256]{1,0:T(4,128)} %tau_ref.1) | copy-start | bytes 12292
  24.4 15.0 %all-to-all-start.1 = ((bf16[8,4,4096]{2,1,0:T(4,128)(2,1)}), bf16[8,4,4096]{2,1,0:T(4,128)(2,1)}, u32[]{:S(2)}, u32[]{:S(2)}) async-start(bf16[8,4,4096]{2,1,0:T(4,128)(2,1)} %broadcast_in_dim.10), calls=%async_computation.1 | async-start | bytes 524288 | tf_op jit(solution)/shard_map/all_to_all | solution.py:23
  28.6 1.6 copy-start.1
  30.8 1.3 copy-start.2
  34.5 0.7 copy-start.4
  35.2 0.7 copy-start.6
  36.0 0.7 copy-start.8
  55.4 4.7 %collective-permute-start = (bf16[128,4096]{1,0:T(8,128)(2,1)S(1)}, bf16[128,4096]{1,0:T(8,128)(2,1)S(1)}, u32[]{:S(2)}, u32[]{:S(2)}) collective-permute-start(bf16[128,4096]{1,0:T(8,128)(2,1)S(1)} %bitcast.10), channel_id=1, source_target_pairs={{0,1},{1,0},{2,3},{3,2},{4,5},{5,4},{6,7},{7,6},{8,9},{9,8},{10,11... | collective-permute-start | bytes 3145736 | tf_op jit(solution)/shard_map/ppermute | solution.py:31
  58.2 22.9 %copy-start.9 = (f32[256,256]{1,0:T(8,128)S(1)}, f32[256,256]{1,0:T(8,128)}, u32[]{:S(2)}) copy-start(f32[256,256]{1,0:T(8,128)} %copy-done.8) | copy-start | bytes 786436
  60.2 1.0 copy-start
  82.2 12.4 %all-to-all-start.4 = ((f32[8,16,256]{2,1,0:T(8,128)}), f32[8,16,256]{2,1,0:T(8,128)S(1)}, u32[]{:S(2)}, u32[]{:S(2)}) async-start(f32[8,16,256]{2,1,0:T(8,128)} %shard_map.50), calls=%async_computation.4 | async-start | bytes 262144 | tf_op jit(solution)/shard_map/all_to_all | solution.py:23
  94.6 0.9 copy-start.3
  95.5 18.4 %copy-start.7 = (f32[256,256]{1,0:T(8,128)S(1)}, f32[256,256]{1,0:T(8,128)}, u32[]{:S(2)}) copy-start(f32[256,256]{1,0:T(8,128)} %copy-done.6) | copy-start | bytes 786436
  127.1 21.0 %copy-start.5 = (f32[256,256]{1,0:T(8,128)S(1)}, f32[256,256]{1,0:T(8,128)}, u32[]{:S(2)}) copy-start(f32[256,256]{1,0:T(8,128)} %copy-done.4) | copy-start | bytes 786436
  134.2 13.8 %all-to-all-start.7 = ((f32[8,16,512]{2,1,0:T(8,128)}), f32[8,16,512]{2,1,0:T(8,128)S(1)}, u32[]{:S(2)}, u32[]{:S(2)}) async-start(f32[8,16,512]{2,1,0:T(8,128)} %bitcast.6), calls=%async_computation.7 | async-start | bytes 524288 | tf_op jit(solution)/shard_map/all_to_all | solution.py:23
  137.7 3.2 %collective-permute-start.1 = (f32[128,256]{1,0:T(8,128)S(1)}, f32[128,256]{1,0:T(8,128)S(1)}, u32[]{:S(2)}, u32[]{:S(2)}) collective-permute-start(f32[128,256]{1,0:T(8,128)S(1)} %bitcast.17), channel_id=1, source_target_pairs={{0,1},{1,0},{2,3},{3,2},{4,5},{5,4},{6,7},{7,6},{8,9},{9,8},{10,11... | collective-permute-start | bytes 393224 | tf_op jit(solution)/shard_map/ppermute | solution.py:31
Sparse Core Ops, SparseCore 0:
  23.0 49.3 all-gather.1

commit v7 on v6

--- a/solution.py
+++ b/solution.py
@@ -10,7 +10,7 @@
 
 PCOL = ("pcol_0", "pcol_1", "pcol_2")
 CHUNK = 1024
-PIECE = 512
+PIECE = 1024
 F32 = jnp.float32
 BF16 = jnp.bfloat16
 ROWS_BY_LANES = (((1,), (1,)), ((), ()))
@@ -111,12 +111,55 @@
     sums_ref[:, size:] = settled(products(half_ref[...], terms_ref[...]))
 
 
-def gram_kernel(core_ref, half_ref, other_ref, gram_ref):
+def cleared(*refs):
     @pl.when(pl.program_id(0) == 0)
     def _():
-        gram_ref[...] = jnp.zeros_like(gram_ref)
-
-    gram_ref[...] += products(rows_of(half_ref), rows_of(other_ref))
+        for ref in refs:
+            ref[...] = jnp.zeros_like(ref)
+
+
+def finished(sums_ref, total_ref):
+    @pl.when(pl.program_id(0) == pl.num_programs(0) - 1)
+    def _():
+        sums_ref[...] = settled(total_ref[...])
+
+
+def early_kernel(
+    core_ref, half_ref, high_ref, next_ref, own_ref, partner_ref, terms_ref,
+    gram_ref, cross_ref, sums_ref, total_ref,
+):
+    cleared(gram_ref, cross_ref, total_ref)
+    gram_ref[...] += products(rows_of(half_ref), rows_of(high_ref))
+    following = rows_of(next_ref)
+    used = jnp.concatenate([own_ref[...], partner_ref[...]], axis=0)
+    cross_ref[...] += products(following, used)
+    total_ref[...] += products(following, terms_ref[...])
+    finished(sums_ref, total_ref)
+
+
+def late_kernel(
+    high_ref, low_ref, next_ref, own_ref, partner_ref, terms_ref,
+    cross_ref, near_ref, sums_ref, total_ref,
+):
+    cleared(cross_ref, near_ref, total_ref)
+    following = jnp.concatenate([rows_of(high_ref), rows_of(low_ref)], axis=0)
+    used = jnp.concatenate([own_ref[...], partner_ref[...]], axis=0)
+    cross_ref[...] += products(following, used)
+    near_ref[...] += products(following, rows_of(next_ref))
+    total_ref[...] += products(following, terms_ref[...])
+    finished(sums_ref, total_ref)
+
+
+def middle_kernel(z_ref, own_ref, partner_ref, next_ref, image_ref, copies_ref, new_ref):
+    used = jnp.concatenate([own_ref[...], partner_ref[...], rows_of(next_ref)], axis=0)
+    image = jnp.concatenate([image_ref[...], image_of(copies_ref)], axis=1)
+    change = jnp.dot(two_terms(image), used, preferred_element_type=F32)
+    new_ref[...] = z_ref[...] - folded(change)
+
+
+def image_of(copies_ref):
+    devices, both, size = copies_ref.shape
+    return copies_ref[:, : both // 2, :].reshape(devices * both // 2, size)
 
 
 def stretch(i):
@@ -135,11 +178,6 @@
     return copies
 
 
-def returned(buffer, target, departures, i):
-    part = (slice(None), pl.ds(i * PIECE, PIECE))
-    return pltpu.make_async_copy(buffer.at[part], target.at[part], departures.at[i])
-
-
 def piece_of(buffer, i):
     if len(buffer.shape) == 2:
         return buffer[:, stretch(i)]
@@ -151,69 +189,16 @@
     return jnp.concatenate([piece_of(buffer, i) for buffer in buffers], axis=0)
 
 
-def advanced(image, sources, z_new, buffers, used, following, total, arrivals, departures):
-    z_buffer = buffers[0]
-    copies = fetched(sources, buffers, arrivals)
-    terms = two_terms(image)
-    for i, row in enumerate(copies):
-        for copy in row:
-            copy.wait()
-        change = jnp.dot(terms, stacked(used, i), preferred_element_type=F32)
-        current = z_buffer[:, stretch(i)] - folded(change)
-        z_buffer[:, stretch(i)] = current
-        part = products(stacked(following, i), two_terms(current))
-        if i == 0:
-            total[...] = part
-        else:
-            total[...] += part
-            returned(z_buffer, z_new, departures, i - 1).start()
-    returned(z_buffer, z_new, departures, len(copies) - 1).start()
-
-
-def drained(z_buffer, z_new, departures):
-    for i in range(z_buffer.shape[1] // PIECE):
-        returned(z_buffer, z_new, departures, i).wait()
-
-
-def step_kernel(
-    z, own, partner, gathered, image_ref, gram_ref, z_new, parts_ref,
-    z_buffer, own_buffer, partner_buffer, next_buffer, total, arrivals, departures,
-):
-    advanced(
-        image_ref[...],
-        [z, own, partner, gathered.at[:, 2]],
-        z_new,
-        [z_buffer, own_buffer, partner_buffer, next_buffer],
-        [own_buffer, partner_buffer],
-        [next_buffer],
-        total,
-        arrivals,
-        departures,
-    )
+def step_kernel(sums_ref, image_ref, cross_ref, gram_ref, parts_ref):
     devices, both, size = parts_ref.shape
-    parts_ref[:, : both // 2, :] = settled(total[...]).reshape(devices, both // 2, size)
+    sums = sums_ref[...] - applied(image_ref[...], cross_ref[...])
+    parts_ref[:, : both // 2, :] = sums.reshape(devices, both // 2, size)
     parts_ref[:, both // 2 :, :] = gram_ref[...].reshape(devices, both // 2, size)
-    drained(z_buffer, z_new, departures)
-
-
-def pair_kernel(
-    z, gathered, copies_ref, z_new, sums_ref,
-    z_buffer, used_buffer, high_buffer, low_buffer, total, arrivals, departures,
-):
-    devices, both, size = copies_ref.shape
-    advanced(
-        copies_ref[:, : both // 2, :].reshape(devices * both // 2, size),
-        [z, gathered.at[:, 2], gathered.at[:, 1], gathered.at[:, 0]],
-        z_new,
-        [z_buffer, used_buffer, high_buffer, low_buffer],
-        [used_buffer],
-        [high_buffer, low_buffer],
-        total,
-        arrivals,
-        departures,
-    )
-    sums_ref[...] = settled(total[...])
-    drained(z_buffer, z_new, departures)
+
+
+def pair_kernel(before_ref, image_ref, cross_ref, copies_ref, near_ref, sums_ref):
+    later = applied(image_of(copies_ref), near_ref[...])
+    sums_ref[...] = before_ref[...] - applied(image_ref[...], cross_ref[...]) - later
 
 
 def last_kernel(
@@ -344,48 +329,77 @@
 
     gathered = after(later, copies)
     owners, _, inner, _ = gathered.shape
-    gram_half = pl.pallas_call(
-        gram_kernel,
-        grid_spec=pltpu.PrefetchScalarGridSpec(
-            num_scalar_prefetch=1,
-            grid=(rows // CHUNK,),
-            in_specs=[
-                pl.BlockSpec((owners // 2, None, inner, CHUNK), lambda i, core: (core[0], 0, 0, i)),
-                pl.BlockSpec((owners, None, inner, CHUNK), lambda i, core: (0, 1, 0, i)),
-            ],
-            out_specs=pl.BlockSpec((half, size), lambda i, core: (0, 0)),
-        ),
-        out_shape=shape(half, size),
-        cost_estimate=cost(2 * half * size * rows, gathered),
-        compiler_params=pltpu.CompilerParams(
-            vmem_limit_bytes=GRAM_LIMIT, dimension_semantics=("arbitrary",)
-        ),
-    )(where_core, gathered, gathered)
-
+    def panel_at(position, start=None):
+        block = (owners if start is None else owners // 2, None, inner, CHUNK)
+        if start is None:
+            return pl.BlockSpec(block, lambda i, *_: (0, position, 0, i))
+        return pl.BlockSpec(block, lambda i, core: (core[0], position, 0, i))
+
+    def by_lanes(lines):
+        return pl.BlockSpec((lines, CHUNK), lambda i, *_: (0, i))
+
+    def fixed(*lengths):
+        return pl.BlockSpec(lengths, lambda i, *_: (0,) * len(lengths))
+
+    def streamed(kernel, scalars, in_specs, shapes, out_specs, scratch, flops, *operands):
+        return pl.pallas_call(
+            kernel,
+            grid_spec=pltpu.PrefetchScalarGridSpec(
+                num_scalar_prefetch=scalars,
+                grid=(rows // CHUNK,),
+                in_specs=in_specs,
+                out_specs=out_specs,
+                scratch_shapes=scratch,
+            ),
+            out_shape=shapes,
+            cost_estimate=cost(flops, *operands),
+            compiler_params=pltpu.CompilerParams(
+                vmem_limit_bytes=GRAM_LIMIT, dimension_semantics=("arbitrary",)
+            ),
+        )(*operands)
+
+    gram_half, cross, sums = streamed(
+        early_kernel,
+        1,
+        [
+            panel_at(0, 0), panel_at(1), panel_at(2),
+            by_lanes(half), by_lanes(half), by_lanes(2 * columns),
+        ],
+        [shape(half, size), shape(size, size), shape(columns, size)],
+        [fixed(half, size), fixed(size, size), fixed(columns, size)],
+        [pltpu.VMEM((size, 2 * columns), F32)],
+        5 * once,
+        where_core,
+        gathered,
+        gathered,
+        gathered,
+        first,
+        partner,
+        terms,
+    )
     image = exchange(copies, "prow").reshape(columns, size)
-    pieces = rows // PIECE
-    z_scratch = pltpu.VMEM((columns, rows), F32)
-    half_scratch = pltpu.VMEM((half, rows), BF16)
-    panel_scratch = pltpu.VMEM((owners, inner, rows), BF16)
-    departures = pltpu.SemaphoreType.DMA((pieces,))
-
-    def arrivals(arrays):
-        return pltpu.SemaphoreType.DMA((arrays, pieces))
-
-    spaces = [pltpu.HBM, pltpu.VMEM]
-    current, parts = fetching_call(
-        step_kernel,
-        [shape(columns, rows), shape(devices, 2 * share, size)],
-        spaces,
+    parts = local_call(
+        step_kernel, shape(devices, 2 * share, size), 1 << 26, sums, image, cross, gram_half
+    )
+    arrived = exchange(parts, "prow")
+    crosses, nears, sums = streamed(
+        late_kernel,
+        0,
         [
-            z_scratch, half_scratch, half_scratch, panel_scratch,
-            pltpu.VMEM((size, 2 * columns), F32), arrivals(4), departures,
+            panel_at(1), panel_at(0), panel_at(2),
+            by_lanes(half), by_lanes(half), by_lanes(2 * columns),
         ],
-        4 * once,
-        [current, first, partner, gathered],
-        [image, gram_half],
-    )
-    arrived = exchange(parts, "prow")
+        [shape(2 * size, size), shape(2 * size, size), shape(columns, 2 * size)],
+        [fixed(2 * size, size), fixed(2 * size, size), fixed(columns, 2 * size)],
+        [pltpu.VMEM((2 * size, 2 * columns), F32)],
+        12 * once,
+        gathered,
+        gathered,
+        gathered,
+        first,
+        partner,
+        terms,
+    )
     copies = local_call(gram_share_kernel, shape(*parts.shape), 1 << 24, arrived, factors[2])
     copies = exchange(copies, "prow")
     gram_own = copies[:, share:].reshape(half, size)
@@ -395,17 +409,26 @@
         jnp.concatenate([gram_own, gram_other]),
         jnp.concatenate([gram_other, gram_own]),
     )
-    current, sums = fetching_call(
-        pair_kernel,
-        [shape(columns, rows), shape(columns, 2 * size)],
-        spaces,
+    sums = local_call(
+        pair_kernel, shape(columns, 2 * size), 1 << 27, sums, image, crosses, copies, nears
+    )
+    current = streamed(
+        middle_kernel,
+        0,
         [
-            z_scratch, panel_scratch, panel_scratch, panel_scratch,
-            pltpu.VMEM((2 * size, 2 * columns), F32), arrivals(4), departures,
+            by_lanes(columns), by_lanes(half), by_lanes(half), panel_at(2),
+            fixed(columns, size), fixed(devices, 2 * share, size),
         ],
-        6 * once,
-        [current, gathered],
-        [copies],
+        shape(columns, rows),
+        by_lanes(columns),
+        [],
+        4 * once,
+        current,
+        first,
+        partner,
+        gathered,
+        image,
+        copies,
     )
     arrived = exchange(sums.reshape(devices, share, 2 * size), "prow")
     copies = local_call(
@@ -417,8 +440,12 @@
         [shape(*vectors.shape)],
         [pltpu.HBM],
         [
-            z_scratch, panel_scratch, panel_scratch, pltpu.VMEM(vectors.shape, F32),
-            arrivals(3), departures,
+            pltpu.VMEM((columns, rows), F32),
+            pltpu.VMEM((owners, inner, rows), BF16),
+            pltpu.VMEM((owners, inner, rows), BF16),
+            pltpu.VMEM(vectors.shape, F32),
+            pltpu.SemaphoreType.DMA((3, rows // PIECE)),
+            pltpu.SemaphoreType.DMA((rows // PIECE,)),
         ],
         4 * once,
         [current, gathered],

time: 175 us -> 177 us (1.011)
  the two profiles are of different devices: /device:TPU:2 before, /device:TPU:8 now
where the time goes in v7:
time: 177 us; the launch traced here: 175 us
  blocking collectives  62.7 us (35%)
  Pallas kernels  35.7 us (20%)
  starting transfers between devices  26.4 us (15%)
  waiting for transfers between devices  20.2 us (11%)
  local copies, waits for them, and re-layouts  16.8 us (9%)
  between operations  13.6 us (8%)
    all_to_all x4, blocking collectives, exchange(): return lax.all_to_all(parts, axis, split_axis=0, concat_axis=0, tiled=True)  62.7 us
    all_to_all x5, starting transfers between devices, exchange(): return lax.all_to_all(parts, axis, split_axis=0, concat_axis=0, tiled=True)  22.5 us
    pallas_call x3, Pallas kernels, streamed(): pl.pallas_call(kernel, grid_spec=pltpu.PrefetchScalarGridSpec(num_scalar_...  20 us
    all_to_all x5, waiting for transfers between devices, exchange(): return lax.all_to_all(parts, axis, split_axis=0, concat_axis=0, tiled=True)  16.9 us
    unnamed x42, local copies, waits for them, and re-layouts  13 us
    pallas_call x9, Pallas kernels, local_call(): pl.pallas_call(kernel, out_shape=shapes, in_specs=[whole(pltpu.SMEM)] * s...  11 us
    pallas_call x1, Pallas kernels, fetching_call(): pl.pallas_call(kernel, out_shape=shapes, in_specs=[whole(pltpu.HBM)] * le...  4.66 us
    ppermute x2, starting transfers between devices, from_partner(): return lax.ppermute(x, 'pcol_2', [(0, 1), (1, 0)])  3.83 us
  transfers between devices with their start and end apart: 8, of which 6 were waited for; matrix products, arithmetic and copies ran while one was open for 1% of the time, Pallas kernels for 15%

profile of v7, /device:TPU:8, one launch (start us, length us, event | category | flops | bytes accessed | tf_op | source)
XLA Modules:
  0.0 175.3 jit_solution(2268335035608715657)
XLA Ops:
  6.5 0.9 slice.10
  7.5 0.1 broadcast_in_dim.9
  7.6 12.2 %all_to_all.45 = bf16[4,3,4,4096]{3,2,1,0:T(4,128)(2,1)S(1)} all-to-all(bf16[4,3,4,4096]{3,2,1,0:T(4,128)(2,1)S(1)} %broadcast_in_dim.9), channel_id=1, replica_groups=mesh['prow'=8,'pcol_0'=8,'pcol_1'=4,'pcol_2'=2] {'pcol_1'}, dimensions={0} | all-to-all | bytes 786432 | tf_op jit(solution)/shard_map/all_to_all | solution.py:23
  19.8 0.2 copy.5
  20.0 0.9 all_gather_reshape.3
  20.8 0.8 slice_bitcast_fusion
  21.6 0.8 broadcast_in_dim.10
  22.4 7.5 %all-to-all-start.1 = ((bf16[8,4,4096]{2,1,0:T(4,128)(2,1)}), bf16[8,4,4096]{2,1,0:T(4,128)(2,1)S(1)}, u32[]{:S(2)}, u32[]{:S(2)}) async-start(bf16[8,4,4096]{2,1,0:T(4,128)(2,1)} %broadcast_in_dim.10), calls=%async_computation.1 | async-start | bytes 524288 | tf_op jit(solution)/shard_map/all_to_all | solution.py:23
  29.9 1.6 copy-done.6
  31.5 0.6 shard_map.46
  32.2 1.3 copy-done.5
  33.5 2.0 %copy-done.19 = f32[4,256,256]{2,1,0:T(8,128)S(1)} copy-done((f32[4,256,256]{2,1,0:T(8,128)S(1)}, f32[4,256,256]{2,1,0:T(8,128)}, u32[]{:S(2)}) %copy-start.19) | copy-done | bytes 1048600
  35.4 2.4 %shard_map.47 = (f32[256,256]{1,0:T(8,128)S(1)}, f32[256,256]{1,0:T(8,128)S(1)}, f32[256,256]{1,0:T(8,128)S(1)}, f32[256,256]{1,0:T(8,128)S(1)}) custom-call(s32[1]{0:T(128)} %bitcast.1.core_ref, f32[4,256]{1,0:T(4,128)S(1)} %copy-done.20, f32[4,256,256]{2,1,0:T(8,128)S(1)} %copy-done.19), custom_call_target="tpu_custom_call" | custom-call | flops 1610612736 | bytes 1052676 | tf_op jit(solution)/shard_map/pallas_call | solution.py:60
  37.9 0.7 copy-done.9
  38.6 0.7 copy-done.11
  39.3 0.6 copy-done.15
  40.1 16.1 %all_to_all.46 = bf16[4,32,4096]{2,1,0:T(8,128)(2,1)S(1)} all-to-all(bf16[4,32,4096]{2,1,0:T(8,128)(2,1)S(1)} %broadcast_in_dim.11), channel_id=1, replica_groups=mesh['prow'=8,'pcol_0'=8,'pcol_1'=4,'pcol_2'=2] {'pcol_1'}, dimensions={0} | all-to-all | bytes 2097152 | tf_op jit(solution)/shard_map/all_to_all | solution.py:23
  56.2 1.9 %collective-permute-start = (bf16[128,4096]{1,0:T(8,128)(2,1)S(1)}, bf16[128,4096]{1,0:T(8,128)(2,1)S(1)}, u32[]{:S(2)}, u32[]{:S(2)}) collective-permute-start(bf16[128,4096]{1,0:T(8,128)(2,1)S(1)} %bitcast.10), channel_id=1, source_target_pairs={{0,1},{1,0},{2,3},{3,2},{4,5},{5,4},{6,7},{7,6},{8,9},{9,8},{10,11... | collective-permute-start | bytes 3145736 | tf_op jit(solution)/shard_map/ppermute | solution.py:31
  58.1 0.9 shard_map.48.before_ref
  59.0 1.9 %collective-permute-done.half_ref.partner_ref = bf16[128,4096]{1,0:T(8,128)(2,1)S(1)} collective-permute-done((bf16[128,4096]{1,0:T(8,128)(2,1)S(1)}, bf16[128,4096]{1,0:T(8,128)(2,1)S(1)}, u32[]{:S(2)}, u32[]{:S(2)}) %collective-permute-start) | collective-permute-done | bytes 1048608 | tf_op jit(solution)/shard_map/ppermute | solution.py:31
  60.9 0.9 shard_map.49
  61.9 19.6 %all_to_all.47.parts_ref = f32[8,16,256]{2,1,0:T(8,128)S(1)} all-to-all(f32[8,16,256]{2,1,0:T(8,128)S(1)} %bitcast.19), channel_id=1, replica_groups=mesh['prow'=8,'pcol_0'=8,'pcol_1'=4,'pcol_2'=2] {'prow'}, dimensions={0} | all-to-all | bytes 262144 | tf_op jit(solution)/shard_map/all_to_all | solution.py:23
  81.5 1.0 shard_map.50
  82.5 3.4 %all-to-all-start.4 = ((f32[8,16,256]{2,1,0:T(8,128)}), f32[8,16,256]{2,1,0:T(8,128)S(1)}, u32[]{:S(2)}, u32[]{:S(2)}) async-start(f32[8,16,256]{2,1,0:T(8,128)} %shard_map.50), calls=%async_computation.4 | async-start | bytes 262144 | tf_op jit(solution)/shard_map/all_to_all | solution.py:23
  85.9 6.4 %shard_map.51 = (f32[128,256]{1,0:T(8,128)}, f32[256,256]{1,0:T(8,128)}, f32[128,256]{1,0:T(8,128)}) custom-call(s32[1]{0:T(128)} %bitcast.1.core_ref, bf16[16,3,16,4096]{3,2,1,0:T(8,128)(2,1)} %all-gather.2.cloned.1.call-done.half_ref.high_ref.next_ref.low_ref.gathered, ...), custom_call_target="tpu_custom_call" | custom-call | flops 1342177280 | bytes 23068676 | tf_op jit(solution)/shard_map/pallas_call | solution.py:345
  92.3 2.5 %all-to-all-done.4 = f32[8,16,256]{2,1,0:T(8,128)S(1)} async-done(((f32[8,16,256]{2,1,0:T(8,128)}), f32[8,16,256]{2,1,0:T(8,128)S(1)}, u32[]{:S(2)}, u32[]{:S(2)}) %all-to-all-start.4) | async-done | bytes 131104 | tf_op jit(solution)/shard_map/all_to_all | solution.py:23
  94.9 1.0 copy-done.14
  95.9 0.9 copy-done.17
  96.8 0.9 copy-done.18
  97.7 0.4 shard_map.52
  98.1 14.8 %all_to_all.48.parts_ref = f32[8,32,256]{2,1,0:T(8,128)S(1)} all-to-all(f32[8,32,256]{2,1,0:T(8,128)S(1)} %shard_map.52), channel_id=1, replica_groups=mesh['prow'=8,'pcol_0'=8,'pcol_1'=4,'pcol_2'=2] {'prow'}, dimensions={0} | all-to-all | bytes 524288 | tf_op jit(solution)/shard_map/all_to_all | solution.py:23
  112.9 1.0 shard_map.53
  113.9 3.4 %all-to-all-start.6 = ((f32[8,32,256]{2,1,0:T(8,128)}), f32[8,32,256]{2,1,0:T(8,128)S(1)}, u32[]{:S(2)}, u32[]{:S(2)}) async-start(f32[8,32,256]{2,1,0:T(8,128)} %shard_map.53), calls=%async_computation.6 | async-start | bytes 524288 | tf_op jit(solution)/shard_map/all_to_all | solution.py:23
  117.4 8.1 %shard_map.55 = (f32[512,256]{1,0:T(8,128)}, f32[512,256]{1,0:T(8,128)}, f32[128,512]{1,0:T(8,128)}) custom-call(bf16[16,3,16,4096]{3,2,1,0:T(8,128)(2,1)} %all-gather.2.cloned.1.call-done.half_ref.high_ref.next_ref.low_ref.gathered, bf16[16,3,16,4096]{3,2,1,0:T(8,128)(2,1)} %all-gather.2.cloned.1.call-done.half_ref.high_ref.next_ref.low_ref.gathered, ...), custom_call_target="tpu_custom_call" | custom-call | flops 3221225472 | bytes 23068672 | tf_op jit(solution)/shard_map/pallas_call | solution.py:345
  125.4 2.3 %all-to-all-done.6.copies_ref = f32[8,32,256]{2,1,0:T(8,128)S(1)} async-done(((f32[8,32,256]{2,1,0:T(8,128)}), f32[8,32,256]{2,1,0:T(8,128)S(1)}, u32[]{:S(2)}, u32[]{:S(2)}) %all-to-all-start.6) | async-done | bytes 262176 | tf_op jit(solution)/shard_map/all_to_all | solution.py:23
  127.8 1.1 copy-done.7
  128.9 1.0 copy-done.8
  129.9 0.9 copy-done.13
  130.9 1.9 %shard_map.56 = f32[128,512]{1,0:T(8,128)} custom-call(f32[128,512]{1,0:T(8,128)S(1)} %copy-done.13, f32[128,256]{1,0:T(8,128)S(1)} %bitcast.16, f32[512,256]{1,0:T(8,128)S(1)} %copy-done.7, f32[8,32,256]{2,1,0:T(8,128)S(1)} %all-to-all-done.6.copies_ref, f32[512,256]{1,0:T(8,128)S(1)} %copy-done.8), custom_call_target="tpu_custom_call" | custom-call | flops 134217728 | bytes 1703936 | tf_op jit(solution)/shard_map/pallas_call | solution.py:60
  132.7 4.8 %all-to-all-start.7 = ((f32[8,16,512]{2,1,0:T(8,128)}), f32[8,16,512]{2,1,0:T(8,128)S(1)}, u32[]{:S(2)}, u32[]{:S(2)}) async-start(f32[8,16,512]{2,1,0:T(8,128)} %bitcast.6), calls=%async_computation.7 | async-start | bytes 524288 | tf_op jit(solution)/shard_map/all_to_all | solution.py:23
  137.6 1.9 %collective-permute-start.1 = (f32[128,256]{1,0:T(8,128)S(1)}, f32[128,256]{1,0:T(8,128)S(1)}, u32[]{:S(2)}, u32[]{:S(2)}) collective-permute-start(f32[128,256]{1,0:T(8,128)S(1)} %bitcast.21), channel_id=1, source_target_pairs={{0,1},{1,0},{2,3},{3,2},{4,5},{5,4},{6,7},{7,6},{8,9},{9,8},{10,11... | collective-permute-start | bytes 393224 | tf_op jit(solution)/shard_map/ppermute | solution.py:31
  139.5 1.3 collective-permute-done.1
  140.8 7.2 %all-to-all-done.7.parts_ref = f32[8,16,512]{2,1,0:T(8,128)S(1)} async-done(((f32[8,16,512]{2,1,0:T(8,128)}), f32[8,16,512]{2,1,0:T(8,128)S(1)}, u32[]{:S(2)}, u32[]{:S(2)}) %all-to-all-start.7) | async-done | bytes 262176 | tf_op jit(solution)/shard_map/all_to_all | solution.py:23
  148.0 2.0 %shard_map.57 = f32[8,16,512]{2,1,0:T(8,128)} custom-call(f32[8,16,512]{2,1,0:T(8,128)S(1)} %all-to-all-done.7.parts_ref, f32[256,256]{1,0:T(8,128)S(1)} %copy-done.10, f32[256,256]{1,0:T(8,128)S(1)} %get-tuple-element.23.low_ref, f32[256,256]{1,0:T(8,128)S(1)} %maximum_select_fusion.gram_ref), custom_call_target="tpu_custom_call" | custom-call | flops 16777216 | bytes 1048576 | tf_op jit(solution)/shard_map/pallas_call | solution.py:60
  150.0 3.4 %all-to-all-start.8 = ((f32[8,16,512]{2,1,0:T(8,128)}), f32[8,16,512]{2,1,0:T(8,128)S(1)}, u32[]{:S(2)}, u32[]{:S(2)}) async-start(f32[8,16,512]{2,1,0:T(8,128)} %shard_map.57), calls=%async_computation.8 | async-start | bytes 524288 | tf_op jit(solution)/shard_map/all_to_all | solution.py:23
  153.4 5.5 %shard_map.54.z = f32[128,4096]{1,0:T(8,128)} custom-call(f32[128,4096]{1,0:T(8,128)} %copy-done.5, bf16[128,4096]{1,0:T(8,128)(2,1)} %bitcast.14, bf16[128,4096]{1,0:T(8,128)(2,1)} %copy-done.2, bf16[16,3,16,4096]{3,2,1,0:T(8,128)(2,1)} %all-gather.2.cloned.1.call-done.half_ref.high_ref.next_ref.low_ref.gathered, f32[128,256]{1,0:T(8,128)} %bitcast.17, ...), custom_call_target="tpu_custom_call" | custom-call | flops 1073741824 | bytes 10878976 | tf_op jit(solution)/shard_map/pallas_call | solution.py:345
  159.0 4.8 %all-to-all-done.8 = f32[8,16,512]{2,1,0:T(8,128)S(1)} async-done(((f32[8,16,512]{2,1,0:T(8,128)}), f32[8,16,512]{2,1,0:T(8,128)S(1)}, u32[]{:S(2)}, u32[]{:S(2)}) %all-to-all-start.8) | async-done | bytes 262176 | tf_op jit(solution)/shard_map/all_to_all | solution.py:23
  163.8 4.7 %shard_map.58 = f32[4096,128]{1,0:T(8,128)} custom-call(f32[128,4096]{1,0:T(8,128)} %shard_map.54.z, bf16[16,3,16,4096]{3,2,1,0:T(8,128)(2,1)} %all-gather.2.cloned.1.call-done.half_ref.high_ref.next_ref.low_ref.gathered, f32[128,512]{1,0:T(8,128)S(1)} %bitcast.18), custom_call_target="tpu_custom_call" | custom-call | flops 1073741824 | bytes 8650752 | tf_op jit(solution)/shard_map/pallas_call | solution.py:71
  (38 shorter events, 0.4 us)
Async XLA Ops:
  6.5 79.4 %all-gather.2.cloned.1.call-start = ((), (), s32[]{:S(2)}) async-start(), calls=%async_computation.9 | async-start | bytes 6684672 | tf_op jit(solution)/shard_map/all_gather | solution.py:303
  20.0 13.5 %copy-start.20 = (f32[4,256]{1,0:T(4,128)S(1)}, f32[4,256]{1,0:T(4,128)}, u32[]{:S(2)}) copy-start(f32[4,256]{1,0:T(4,128)} %tau_ref.1) | copy-start | bytes 12292
  22.4 16.9 %all-to-all-start.1 = ((bf16[8,4,4096]{2,1,0:T(4,128)(2,1)}), bf16[8,4,4096]{2,1,0:T(4,128)(2,1)S(1)}, u32[]{:S(2)}, u32[]{:S(2)}) async-start(bf16[8,4,4096]{2,1,0:T(4,128)(2,1)} %broadcast_in_dim.10), calls=%async_computation.1 | async-start | bytes 524288 | tf_op jit(solution)/shard_map/all_to_all | solution.py:23
  29.9 1.6 copy-start.6
  32.1 1.3 copy-start.5
  33.5 27.5 %copy-start = (bf16[256,4096]{1,0:T(8,128)(2,1)}, bf16[256,4096]{1,0:T(8,128)(2,1)S(1)}, u32[]{:S(2)}) copy-start(bf16[256,4096]{1,0:T(8,128)(2,1)S(1)} %get-tuple-element.22.terms_ref) | copy-start | bytes 6291460
  33.5 2.0 %copy-start.19 = (f32[4,256,256]{2,1,0:T(8,128)S(1)}, f32[4,256,256]{2,1,0:T(8,128)}, u32[]{:S(2)}) copy-start(f32[4,256,256]{2,1,0:T(8,128)} %coupling_ref.1) | copy-start | bytes 3145732
  37.9 0.7 copy-start.9
  38.6 0.7 copy-start.11
  39.3 0.7 copy-start.15
  56.2 5.6 %copy-start.1 = (bf16[4,32,4096]{2,1,0:T(8,128)(2,1)}, bf16[4,32,4096]{2,1,0:T(8,128)(2,1)S(1)}, u32[]{:S(2)}) copy-start(bf16[4,32,4096]{2,1,0:T(8,128)(2,1)S(1)} %all_to_all.46) | copy-start | bytes 3145732
  56.2 4.8 %collective-permute-start = (bf16[128,4096]{1,0:T(8,128)(2,1)S(1)}, bf16[128,4096]{1,0:T(8,128)(2,1)S(1)}, u32[]{:S(2)}, u32[]{:S(2)}) collective-permute-start(bf16[128,4096]{1,0:T(8,128)(2,1)S(1)} %bitcast.10), channel_id=1, source_target_pairs={{0,1},{1,0},{2,3},{3,2},{4,5},{5,4},{6,7},{7,6},{8,9},{9,8},{10,11... | collective-permute-start | bytes 3145736 | tf_op jit(solution)/shard_map/ppermute | solution.py:31
  59.0 22.5 %copy-start.16 = (f32[256,256]{1,0:T(8,128)S(1)}, f32[256,256]{1,0:T(8,128)}, u32[]{:S(2)}) copy-start(f32[256,256]{1,0:T(8,128)} %copy-done.15) | copy-start | bytes 786436
  60.9 1.0 copy-start.2
  82.5 12.4 %all-to-all-start.4 = ((f32[8,16,256]{2,1,0:T(8,128)}), f32[8,16,256]{2,1,0:T(8,128)S(1)}, u32[]{:S(2)}, u32[]{:S(2)}) async-start(f32[8,16,256]{2,1,0:T(8,128)} %shard_map.50), calls=%async_computation.4 | async-start | bytes 262144 | tf_op jit(solution)/shard_map/all_to_all | solution.py:23
  85.9 27.0 %copy-start.12 = (f32[256,256]{1,0:T(8,128)S(1)}, f32[256,256]{1,0:T(8,128)}, u32[]{:S(2)}) copy-start(f32[256,256]{1,0:T(8,128)} %copy-done.11) | copy-start | bytes 786436
  94.9 32.9 %copy-start.4 = (f32[8,16,256]{2,1,0:T(8,128)}, f32[8,16,256]{2,1,0:T(8,128)S(1)}, u32[]{:S(2)}) copy-start(f32[8,16,256]{2,1,0:T(8,128)S(1)} %all-to-all-done.4) | copy-start | bytes 393220
  94.9 1.0 copy-start.14
  95.9 0.9 copy-start.17
  96.8 0.9 copy-start.18
  113.9 13.8 %all-to-all-start.6 = ((f32[8,32,256]{2,1,0:T(8,128)}), f32[8,32,256]{2,1,0:T(8,128)S(1)}, u32[]{:S(2)}, u32[]{:S(2)}) async-start(f32[8,32,256]{2,1,0:T(8,128)} %shard_map.53), calls=%async_computation.6 | async-start | bytes 524288 | tf_op jit(solution)/shard_map/all_to_all | solution.py:23
  117.4 30.7 %copy-start.10 = (f32[256,256]{1,0:T(8,128)S(1)}, f32[256,256]{1,0:T(8,128)}, u32[]{:S(2)}) copy-start(f32[256,256]{1,0:T(8,128)} %copy-done.9) | copy-start | bytes 786436
  127.8 22.2 %copy-start.3 = (f32[8,32,256]{2,1,0:T(8,128)}, f32[8,32,256]{2,1,0:T(8,128)S(1)}, u32[]{:S(2)}) copy-start(f32[8,32,256]{2,1,0:T(8,128)S(1)} %all-to-all-done.6.copies_ref) | copy-start | bytes 786436
  127.8 1.1 copy-start.7
  128.9 1.0 copy-start.8
  129.9 0.9 copy-start.13
  132.7 15.3 %all-to-all-start.7 = ((f32[8,16,512]{2,1,0:T(8,128)}), f32[8,16,512]{2,1,0:T(8,128)S(1)}, u32[]{:S(2)}, u32[]{:S(2)}) async-start(f32[8,16,512]{2,1,0:T(8,128)} %bitcast.6), calls=%async_computation.7 | async-start | bytes 524288 | tf_op jit(solution)/shard_map/all_to_all | solution.py:23
  137.6 3.2 %collective-permute-start.1 = (f32[128,256]{1,0:T(8,128)S(1)}, f32[128,256]{1,0:T(8,128)S(1)}, u32[]{:S(2)}, u32[]{:S(2)}) collective-permute-start(f32[128,256]{1,0:T(8,128)S(1)} %bitcast.21), channel_id=1, source_target_pairs={{0,1},{1,0},{2,3},{3,2},{4,5},{5,4},{6,7},{7,6},{8,9},{9,8},{10,11... | collective-permute-start | bytes 393224 | tf_op jit(solution)/shard_map/ppermute | solution.py:31
  150.0 13.8 %all-to-all-start.8 = ((f32[8,16,512]{2,1,0:T(8,128)}), f32[8,16,512]{2,1,0:T(8,128)S(1)}, u32[]{:S(2)}, u32[]{:S(2)}) async-start(f32[8,16,512]{2,1,0:T(8,128)} %shard_map.57), calls=%async_computation.8 | async-start | bytes 524288 | tf_op jit(solution)/shard_map/all_to_all | solution.py:23
Sparse Core Ops, SparseCore 0:
  21.0 50.7 all-gather.1

commit v8 on v7

--- a/solution.py
+++ b/solution.py
@@ -16,7 +16,7 @@
 ROWS_BY_LANES = (((1,), (1,)), ((), ()))
 LIMIT = 24 << 20
 FETCH_LIMIT = 52 << 20
-GRAM_LIMIT = 60 << 20
+GRAM_LIMIT = 52 << 20
 
 
 def exchange(parts, axis):

time: 177 us -> 169 us (0.955)
  local copies, waits for them, and re-layouts: 16.8 us -> 10.9 us
  Pallas kernels: 35.7 us -> 33.3 us
  waiting for transfers between devices: 20.2 us -> 22.6 us
    unnamed x42 -> x28, local copies, waits for them, and re-layouts: 13 us -> 7.09 us
    pallas_call x3, Pallas kernels: 20 us -> 17.6 us  [streamed(): pl.pallas_call(kernel, grid_spec=pltpu.PrefetchScalarGridSpec(num_scalar_...]
    all_to_all x5, waiting for transfers between devices: 16.9 us -> 19.3 us  [exchange(): return lax.all_to_all(parts, axis, split_axis=0, concat_axis=0, tiled=True)]
  transfers between devices with their start and end apart: 8 -> 8, of which waited for: 6 -> 6; matrix products, arithmetic and copies ran while one was open for 1% -> 1% of each run, Pallas kernels for 15% -> 14%
where the time goes in v8:
time: 169 us; the launch traced here: 167 us
  blocking collectives  61.7 us (37%)
  Pallas kernels  33.3 us (20%)
  starting transfers between devices  25.2 us (15%)
  waiting for transfers between devices  22.6 us (13%)
  between operations  13.6 us (8%)
  local copies, waits for them, and re-layouts  10.9 us (6%)
    all_to_all x4, blocking collectives, exchange(): return lax.all_to_all(parts, axis, split_axis=0, concat_axis=0, tiled=True)  61.7 us
    all_to_all x5, starting transfers between devices, exchange(): return lax.all_to_all(parts, axis, split_axis=0, concat_axis=0, tiled=True)  21.4 us
    all_to_all x5, waiting for transfers between devices, exchange(): return lax.all_to_all(parts, axis, split_axis=0, concat_axis=0, tiled=True)  19.3 us
    pallas_call x3, Pallas kernels, streamed(): pl.pallas_call(kernel, grid_spec=pltpu.PrefetchScalarGridSpec(num_scalar_...  17.6 us
    pallas_call x9, Pallas kernels, local_call(): pl.pallas_call(kernel, out_shape=shapes, in_specs=[whole(pltpu.SMEM)] * s...  11.1 us
    unnamed x28, local copies, waits for them, and re-layouts  7.09 us
    pallas_call x1, Pallas kernels, fetching_call(): pl.pallas_call(kernel, out_shape=shapes, in_specs=[whole(pltpu.HBM)] * le...  4.67 us
    ppermute x2, starting transfers between devices, from_partner(): return lax.ppermute(x, 'pcol_2', [(0, 1), (1, 0)])  3.83 us
  transfers between devices with their start and end apart: 8, of which 6 were waited for; matrix products, arithmetic and copies ran while one was open for 1% of the time, Pallas kernels for 14%

profile of v8, /device:TPU:8, one launch (start us, length us, event | category | flops | bytes accessed | tf_op | source)
XLA Modules:
  0.0 167.4 jit_solution(5232618973390225398)
XLA Ops:
  6.5 0.9 slice.10
  7.5 0.1 broadcast_in_dim.9
  7.6 12.2 %all_to_all.45 = bf16[4,3,4,4096]{3,2,1,0:T(4,128)(2,1)S(1)} all-to-all(bf16[4,3,4,4096]{3,2,1,0:T(4,128)(2,1)S(1)} %broadcast_in_dim.9), channel_id=1, replica_groups=mesh['prow'=8,'pcol_0'=8,'pcol_1'=4,'pcol_2'=2] {'pcol_1'}, dimensions={0} | all-to-all | bytes 786432 | tf_op jit(solution)/shard_map/all_to_all | solution.py:23
  19.8 0.2 copy.5
  20.0 0.0 copy-start.13
  20.0 0.9 all_gather_reshape.3
  20.8 0.0 all-gather.2.cloned.1.call-update
  20.9 0.8 slice_bitcast_fusion
  21.6 0.8 broadcast_in_dim.10
  22.4 7.5 %all-to-all-start.1 = ((bf16[8,4,4096]{2,1,0:T(4,128)(2,1)}), bf16[8,4,4096]{2,1,0:T(4,128)(2,1)S(1)}, u32[]{:S(2)}, u32[]{:S(2)}) async-start(bf16[8,4,4096]{2,1,0:T(4,128)(2,1)} %broadcast_in_dim.10), calls=%async_computation.1 | async-start | bytes 524288 | tf_op jit(solution)/shard_map/all_to_all | solution.py:23
  30.0 1.6 copy-done.5
  31.6 0.6 shard_map.46
  32.2 1.3 copy-done.4
  33.5 2.0 %copy-done.12 = f32[4,256,256]{2,1,0:T(8,128)S(1)} copy-done((f32[4,256,256]{2,1,0:T(8,128)S(1)}, f32[4,256,256]{2,1,0:T(8,128)}, u32[]{:S(2)}) %copy-start.12) | copy-done | bytes 1048600
  35.5 2.4 %shard_map.47 = (f32[256,256]{1,0:T(8,128)S(1)}, f32[256,256]{1,0:T(8,128)S(1)}, f32[256,256]{1,0:T(8,128)S(1)}, f32[256,256]{1,0:T(8,128)S(1)}) custom-call(s32[1]{0:T(128)} %bitcast.1.core_ref, f32[4,256]{1,0:T(4,128)S(1)} %copy-done.13, f32[4,256,256]{2,1,0:T(8,128)S(1)} %copy-done.12), custom_call_target="tpu_custom_call" | custom-call | flops 1610612736 | bytes 1052676 | tf_op jit(solution)/shard_map/pallas_call | solution.py:60
  37.9 0.7 copy-done.6
  38.6 0.7 copy-done.8
  39.3 0.1 reshape.24
  39.4 0.6 copy-done.10
  40.0 0.1 broadcast_in_dim.11
  40.1 16.1 %all_to_all.46 = bf16[4,32,4096]{2,1,0:T(8,128)(2,1)S(1)} all-to-all(bf16[4,32,4096]{2,1,0:T(8,128)(2,1)S(1)} %broadcast_in_dim.11), channel_id=1, replica_groups=mesh['prow'=8,'pcol_0'=8,'pcol_1'=4,'pcol_2'=2] {'pcol_1'}, dimensions={0} | all-to-all | bytes 2097152 | tf_op jit(solution)/shard_map/all_to_all | solution.py:23
  56.2 1.9 %collective-permute-start = (bf16[128,4096]{1,0:T(8,128)(2,1)S(1)}, bf16[128,4096]{1,0:T(8,128)(2,1)S(1)}, u32[]{:S(2)}, u32[]{:S(2)}) collective-permute-start(bf16[128,4096]{1,0:T(8,128)(2,1)S(1)} %bitcast.10), channel_id=1, source_target_pairs={{0,1},{1,0},{2,3},{3,2},{4,5},{5,4},{6,7},{7,6},{8,9},{9,8},{10,11... | collective-permute-start | bytes 3145736 | tf_op jit(solution)/shard_map/ppermute | solution.py:31
  58.2 0.9 shard_map.48.before_ref
  59.0 1.9 %collective-permute-done.half_ref.partner_ref = bf16[128,4096]{1,0:T(8,128)(2,1)S(1)} collective-permute-done((bf16[128,4096]{1,0:T(8,128)(2,1)S(1)}, bf16[128,4096]{1,0:T(8,128)(2,1)S(1)}, u32[]{:S(2)}, u32[]{:S(2)}) %collective-permute-start) | collective-permute-done | bytes 1048608 | tf_op jit(solution)/shard_map/ppermute | solution.py:31
  61.0 0.9 shard_map.49
  61.9 0.1 copy-done.3
  62.0 19.6 %all_to_all.47.parts_ref = f32[8,16,256]{2,1,0:T(8,128)S(1)} all-to-all(f32[8,16,256]{2,1,0:T(8,128)S(1)} %bitcast.19), channel_id=1, replica_groups=mesh['prow'=8,'pcol_0'=8,'pcol_1'=4,'pcol_2'=2] {'prow'}, dimensions={0} | all-to-all | bytes 262144 | tf_op jit(solution)/shard_map/all_to_all | solution.py:23
  81.6 1.0 shard_map.50
  82.6 3.4 %all-to-all-start.4 = ((f32[8,16,256]{2,1,0:T(8,128)}), f32[8,16,256]{2,1,0:T(8,128)S(1)}, u32[]{:S(2)}, u32[]{:S(2)}) async-start(f32[8,16,256]{2,1,0:T(8,128)} %shard_map.50), calls=%async_computation.4 | async-start | bytes 262144 | tf_op jit(solution)/shard_map/all_to_all | solution.py:23
  86.0 0.0 all-gather.2.cloned.1.call-done.half_ref.high_ref.next_ref.low_ref.gathered
  86.0 5.4 %shard_map.51 = (f32[128,256]{1,0:T(8,128)S(1)}, f32[256,256]{1,0:T(8,128)S(1)}, f32[128,256]{1,0:T(8,128)S(1)}) custom-call(s32[1]{0:T(128)} %bitcast.1.core_ref, bf16[16,3,16,4096]{3,2,1,0:T(8,128)(2,1)} %all-gather.2.cloned.1.call-done.half_ref.high_ref.next_ref.low_ref.gathered, ...), custom_call_target="tpu_custom_call" | custom-call | flops 1342177280 | bytes 23068676 | tf_op jit(solution)/shard_map/pallas_call | solution.py:345
  91.5 3.5 %all-to-all-done.4 = f32[8,16,256]{2,1,0:T(8,128)S(1)} async-done(((f32[8,16,256]{2,1,0:T(8,128)}), f32[8,16,256]{2,1,0:T(8,128)S(1)}, u32[]{:S(2)}, u32[]{:S(2)}) %all-to-all-start.4) | async-done | bytes 131104 | tf_op jit(solution)/shard_map/all_to_all | solution.py:23
  95.0 0.4 shard_map.52
  95.4 13.9 %all_to_all.48.parts_ref = f32[8,32,256]{2,1,0:T(8,128)S(1)} all-to-all(f32[8,32,256]{2,1,0:T(8,128)S(1)} %shard_map.52), channel_id=1, replica_groups=mesh['prow'=8,'pcol_0'=8,'pcol_1'=4,'pcol_2'=2] {'prow'}, dimensions={0} | all-to-all | bytes 524288 | tf_op jit(solution)/shard_map/all_to_all | solution.py:23
  109.3 1.0 shard_map.53
  110.3 3.4 %all-to-all-start.6 = ((f32[8,32,256]{2,1,0:T(8,128)}), f32[8,32,256]{2,1,0:T(8,128)S(1)}, u32[]{:S(2)}, u32[]{:S(2)}) async-start(f32[8,32,256]{2,1,0:T(8,128)} %shard_map.53), calls=%async_computation.6 | async-start | bytes 524288 | tf_op jit(solution)/shard_map/all_to_all | solution.py:23
  113.7 6.9 %shard_map.55 = (f32[512,256]{1,0:T(8,128)S(1)}, f32[512,256]{1,0:T(8,128)S(1)}, f32[128,512]{1,0:T(8,128)S(1)}) custom-call(bf16[16,3,16,4096]{3,2,1,0:T(8,128)(2,1)} %all-gather.2.cloned.1.call-done.half_ref.high_ref.next_ref.low_ref.gathered, bf16[16,3,16,4096]{3,2,1,0:T(8,128)(2,1)} %all-gather.2.cloned.1.call-done.half_ref.high_ref.next_ref.low_ref.gathered, ...), custom_call_target="tpu_custom_call" | custom-call | flops 3221225472 | bytes 23068672 | tf_op jit(solution)/shard_map/pallas_call | solution.py:345
  120.6 3.5 %all-to-all-done.6.copies_ref = f32[8,32,256]{2,1,0:T(8,128)S(1)} async-done(((f32[8,32,256]{2,1,0:T(8,128)}), f32[8,32,256]{2,1,0:T(8,128)S(1)}, u32[]{:S(2)}, u32[]{:S(2)}) %all-to-all-start.6) | async-done | bytes 262176 | tf_op jit(solution)/shard_map/all_to_all | solution.py:23
  124.1 1.9 %shard_map.56 = f32[128,512]{1,0:T(8,128)} custom-call(f32[128,512]{1,0:T(8,128)S(1)} %get-tuple-element.32.before_ref, f32[128,256]{1,0:T(8,128)S(1)} %bitcast.16, f32[512,256]{1,0:T(8,128)S(1)} %get-tuple-element.33.cross_ref, f32[8,32,256]{2,1,0:T(8,128)S(1)} %all-to-all-done.6.copies_ref, f32[512,256]{1,0:T(8,128)S(1)} %get-tuple-element.34.near_ref), custom_call_target="tpu_custom_call" | custom-call | flops 134217728 | bytes 1703936 | tf_op jit(solution)/shard_map/pallas_call | solution.py:60
  126.0 3.7 %all-to-all-start.7 = ((f32[8,16,512]{2,1,0:T(8,128)}), f32[8,16,512]{2,1,0:T(8,128)S(1)}, u32[]{:S(2)}, u32[]{:S(2)}) async-start(f32[8,16,512]{2,1,0:T(8,128)} %bitcast.6), calls=%async_computation.7 | async-start | bytes 524288 | tf_op jit(solution)/shard_map/all_to_all | solution.py:23
  129.6 1.9 %collective-permute-start.1 = (f32[128,256]{1,0:T(8,128)S(1)}, f32[128,256]{1,0:T(8,128)S(1)}, u32[]{:S(2)}, u32[]{:S(2)}) collective-permute-start(f32[128,256]{1,0:T(8,128)S(1)} %bitcast.21), channel_id=1, source_target_pairs={{0,1},{1,0},{2,3},{3,2},{4,5},{5,4},{6,7},{7,6},{8,9},{9,8},{10,11... | collective-permute-start | bytes 393224 | tf_op jit(solution)/shard_map/ppermute | solution.py:31
  131.6 1.3 collective-permute-done.1
  132.9 7.2 %all-to-all-done.7.parts_ref = f32[8,16,512]{2,1,0:T(8,128)S(1)} async-done(((f32[8,16,512]{2,1,0:T(8,128)}), f32[8,16,512]{2,1,0:T(8,128)S(1)}, u32[]{:S(2)}, u32[]{:S(2)}) %all-to-all-start.7) | async-done | bytes 262176 | tf_op jit(solution)/shard_map/all_to_all | solution.py:23
  140.1 2.0 %shard_map.57 = f32[8,16,512]{2,1,0:T(8,128)} custom-call(f32[8,16,512]{2,1,0:T(8,128)S(1)} %all-to-all-done.7.parts_ref, f32[256,256]{1,0:T(8,128)S(1)} %copy-done.7, f32[256,256]{1,0:T(8,128)S(1)} %get-tuple-element.23.low_ref, f32[256,256]{1,0:T(8,128)S(1)} %maximum_select_fusion.gram_ref), custom_call_target="tpu_custom_call" | custom-call | flops 16777216 | bytes 1048576 | tf_op jit(solution)/shard_map/pallas_call | solution.py:60
  142.1 3.4 %all-to-all-start.8 = ((f32[8,16,512]{2,1,0:T(8,128)}), f32[8,16,512]{2,1,0:T(8,128)S(1)}, u32[]{:S(2)}, u32[]{:S(2)}) async-start(f32[8,16,512]{2,1,0:T(8,128)} %shard_map.57), calls=%async_computation.8 | async-start | bytes 524288 | tf_op jit(solution)/shard_map/all_to_all | solution.py:23
  145.5 5.2 %shard_map.54.z = f32[128,4096]{1,0:T(8,128)} custom-call(f32[128,4096]{1,0:T(8,128)} %copy-done.4, bf16[128,4096]{1,0:T(8,128)(2,1)S(1)} %bitcast.14, bf16[128,4096]{1,0:T(8,128)(2,1)} %copy-done.3, bf16[16,3,16,4096]{3,2,1,0:T(8,128)(2,1)} %all-gather.2.cloned.1.call-done.half_ref.high_ref.next_ref.low_ref.gathered, f32[128,256]{1,0:T(8,128)S(1)} %bitcast.17, ...), custom_call_target="tpu_custom_call" | custom-call | flops 1073741824 | bytes 10878976 | tf_op jit(solution)/shard_map/pallas_call | solution.py:345
  150.8 5.1 %all-to-all-done.8 = f32[8,16,512]{2,1,0:T(8,128)S(1)} async-done(((f32[8,16,512]{2,1,0:T(8,128)}), f32[8,16,512]{2,1,0:T(8,128)S(1)}, u32[]{:S(2)}, u32[]{:S(2)}) %all-to-all-start.8) | async-done | bytes 262176 | tf_op jit(solution)/shard_map/all_to_all | solution.py:23
  155.9 4.7 %shard_map.58 = f32[4096,128]{1,0:T(8,128)} custom-call(f32[128,4096]{1,0:T(8,128)} %shard_map.54.z, bf16[16,3,16,4096]{3,2,1,0:T(8,128)(2,1)} %all-gather.2.cloned.1.call-done.half_ref.high_ref.next_ref.low_ref.gathered, f32[128,512]{1,0:T(8,128)S(1)} %bitcast.18), custom_call_target="tpu_custom_call" | custom-call | flops 1073741824 | bytes 8650752 | tf_op jit(solution)/shard_map/pallas_call | solution.py:71
  (24 shorter events, 0.1 us)
Async XLA Ops:
  6.5 79.5 %all-gather.2.cloned.1.call-start = ((), (), s32[]{:S(2)}) async-start(), calls=%async_computation.9 | async-start | bytes 6684672 | tf_op jit(solution)/shard_map/all_gather | solution.py:303
  20.0 13.5 %copy-start.13 = (f32[4,256]{1,0:T(4,128)S(1)}, f32[4,256]{1,0:T(4,128)}, u32[]{:S(2)}) copy-start(f32[4,256]{1,0:T(4,128)} %tau_ref.1) | copy-start | bytes 12292
  22.4 16.9 %all-to-all-start.1 = ((bf16[8,4,4096]{2,1,0:T(4,128)(2,1)}), bf16[8,4,4096]{2,1,0:T(4,128)(2,1)S(1)}, u32[]{:S(2)}, u32[]{:S(2)}) async-start(bf16[8,4,4096]{2,1,0:T(4,128)(2,1)} %broadcast_in_dim.10), calls=%async_computation.1 | async-start | bytes 524288 | tf_op jit(solution)/shard_map/all_to_all | solution.py:23
  30.0 1.6 copy-start.5
  32.2 1.3 copy-start.4
  33.5 27.5 %copy-start = (bf16[256,4096]{1,0:T(8,128)(2,1)}, bf16[256,4096]{1,0:T(8,128)(2,1)S(1)}, u32[]{:S(2)}) copy-start(bf16[256,4096]{1,0:T(8,128)(2,1)S(1)} %get-tuple-element.22.terms_ref) | copy-start | bytes 6291460
  33.5 2.0 %copy-start.12 = (f32[4,256,256]{2,1,0:T(8,128)S(1)}, f32[4,256,256]{2,1,0:T(8,128)}, u32[]{:S(2)}) copy-start(f32[4,256,256]{2,1,0:T(8,128)} %coupling_ref.1) | copy-start | bytes 3145732
  37.9 0.7 copy-start.6
  38.6 0.7 copy-start.8
  39.3 0.7 copy-start.10
  56.2 29.8 %copy-start.1 = (bf16[4,32,4096]{2,1,0:T(8,128)(2,1)}, bf16[4,32,4096]{2,1,0:T(8,128)(2,1)S(1)}, u32[]{:S(2)}) copy-start(bf16[4,32,4096]{2,1,0:T(8,128)(2,1)S(1)} %all_to_all.46) | copy-start | bytes 3145732
  56.2 4.8 %collective-permute-start = (bf16[128,4096]{1,0:T(8,128)(2,1)S(1)}, bf16[128,4096]{1,0:T(8,128)(2,1)S(1)}, u32[]{:S(2)}, u32[]{:S(2)}) collective-permute-start(bf16[128,4096]{1,0:T(8,128)(2,1)S(1)} %bitcast.10), channel_id=1, source_target_pairs={{0,1},{1,0},{2,3},{3,2},{4,5},{5,4},{6,7},{7,6},{8,9},{9,8},{10,11... | collective-permute-start | bytes 3145736 | tf_op jit(solution)/shard_map/ppermute | solution.py:31
  59.0 22.6 %copy-start.11 = (f32[256,256]{1,0:T(8,128)S(1)}, f32[256,256]{1,0:T(8,128)}, u32[]{:S(2)}) copy-start(f32[256,256]{1,0:T(8,128)} %copy-done.10) | copy-start | bytes 786436
  61.0 1.0 copy-start.3
  82.6 12.4 %all-to-all-start.4 = ((f32[8,16,256]{2,1,0:T(8,128)}), f32[8,16,256]{2,1,0:T(8,128)S(1)}, u32[]{:S(2)}, u32[]{:S(2)}) async-start(f32[8,16,256]{2,1,0:T(8,128)} %shard_map.50), calls=%async_computation.4 | async-start | bytes 262144 | tf_op jit(solution)/shard_map/all_to_all | solution.py:23
  86.0 23.3 %copy-start.9 = (f32[256,256]{1,0:T(8,128)S(1)}, f32[256,256]{1,0:T(8,128)}, u32[]{:S(2)}) copy-start(f32[256,256]{1,0:T(8,128)} %copy-done.8) | copy-start | bytes 786436
  110.3 13.8 %all-to-all-start.6 = ((f32[8,32,256]{2,1,0:T(8,128)}), f32[8,32,256]{2,1,0:T(8,128)S(1)}, u32[]{:S(2)}, u32[]{:S(2)}) async-start(f32[8,32,256]{2,1,0:T(8,128)} %shard_map.53), calls=%async_computation.6 | async-start | bytes 524288 | tf_op jit(solution)/shard_map/all_to_all | solution.py:23
  120.6 19.5 %copy-start.7 = (f32[256,256]{1,0:T(8,128)S(1)}, f32[256,256]{1,0:T(8,128)}, u32[]{:S(2)}) copy-start(f32[256,256]{1,0:T(8,128)} %copy-done.6) | copy-start | bytes 786436
  124.1 21.4 %copy-start.2 = (bf16[4,32,4096]{2,1,0:T(8,128)(2,1)S(1)}, bf16[4,32,4096]{2,1,0:T(8,128)(2,1)}, u32[]{:S(2)}) copy-start(bf16[4,32,4096]{2,1,0:T(8,128)(2,1)} %copy-done.1) | copy-start | bytes 3145732
  126.0 14.1 %all-to-all-start.7 = ((f32[8,16,512]{2,1,0:T(8,128)}), f32[8,16,512]{2,1,0:T(8,128)S(1)}, u32[]{:S(2)}, u32[]{:S(2)}) async-start(f32[8,16,512]{2,1,0:T(8,128)} %bitcast.6), calls=%async_computation.7 | async-start | bytes 524288 | tf_op jit(solution)/shard_map/all_to_all | solution.py:23
  129.6 3.2 %collective-permute-start.1 = (f32[128,256]{1,0:T(8,128)S(1)}, f32[128,256]{1,0:T(8,128)S(1)}, u32[]{:S(2)}, u32[]{:S(2)}) collective-permute-start(f32[128,256]{1,0:T(8,128)S(1)} %bitcast.21), channel_id=1, source_target_pairs={{0,1},{1,0},{2,3},{3,2},{4,5},{5,4},{6,7},{7,6},{8,9},{9,8},{10,11... | collective-permute-start | bytes 393224 | tf_op jit(solution)/shard_map/ppermute | solution.py:31
  142.1 13.8 %all-to-all-start.8 = ((f32[8,16,512]{2,1,0:T(8,128)}), f32[8,16,512]{2,1,0:T(8,128)S(1)}, u32[]{:S(2)}, u32[]{:S(2)}) async-start(f32[8,16,512]{2,1,0:T(8,128)} %shard_map.57), calls=%async_computation.8 | async-start | bytes 524288 | tf_op jit(solution)/shard_map/all_to_all | solution.py:23
Sparse Core Ops, SparseCore 0:
  21.0 50.8 all-gather.1

commit v9 on v8

--- a/solution.py
+++ b/solution.py
@@ -138,8 +138,8 @@
 
 
 def late_kernel(
-    high_ref, low_ref, next_ref, own_ref, partner_ref, terms_ref,
-    cross_ref, near_ref, sums_ref, total_ref,
+    high_ref, low_ref, next_ref, own_ref, partner_ref, terms_ref, image_ref,
+    near_ref, sums_ref, cross_ref, total_ref,
 ):
     cleared(cross_ref, near_ref, total_ref)
     following = jnp.concatenate([rows_of(high_ref), rows_of(low_ref)], axis=0)
@@ -147,7 +147,10 @@
     cross_ref[...] += products(following, used)
     near_ref[...] += products(following, rows_of(next_ref))
     total_ref[...] += products(following, terms_ref[...])
-    finished(sums_ref, total_ref)
+
+    @pl.when(pl.program_id(0) == pl.num_programs(0) - 1)
+    def _():
+        sums_ref[...] = settled(total_ref[...]) - applied(image_ref[...], cross_ref[...])
 
 
 def middle_kernel(z_ref, own_ref, partner_ref, next_ref, image_ref, copies_ref, new_ref):
@@ -196,9 +199,8 @@
     parts_ref[:, both // 2 :, :] = gram_ref[...].reshape(devices, both // 2, size)
 
 
-def pair_kernel(before_ref, image_ref, cross_ref, copies_ref, near_ref, sums_ref):
-    later = applied(image_of(copies_ref), near_ref[...])
-    sums_ref[...] = before_ref[...] - applied(image_ref[...], cross_ref[...]) - later
+def pair_kernel(before_ref, copies_ref, near_ref, sums_ref):
+    sums_ref[...] = before_ref[...] - applied(image_of(copies_ref), near_ref[...])
 
 
 def last_kernel(
@@ -382,16 +384,17 @@
         step_kernel, shape(devices, 2 * share, size), 1 << 26, sums, image, cross, gram_half
     )
     arrived = exchange(parts, "prow")
-    crosses, nears, sums = streamed(
+    nears, sums = streamed(
         late_kernel,
         0,
         [
             panel_at(1), panel_at(0), panel_at(2),
             by_lanes(half), by_lanes(half), by_lanes(2 * columns),
+            fixed(columns, size),
         ],
-        [shape(2 * size, size), shape(2 * size, size), shape(columns, 2 * size)],
-        [fixed(2 * size, size), fixed(2 * size, size), fixed(columns, 2 * size)],
-        [pltpu.VMEM((2 * size, 2 * columns), F32)],
+        [shape(2 * size, size), shape(columns, 2 * size)],
+        [fixed(2 * size, size), fixed(columns, 2 * size)],
+        [pltpu.VMEM((2 * size, size), F32), pltpu.VMEM((2 * size, 2 * columns), F32)],
         12 * once,
         gathered,
         gathered,
@@ -399,6 +402,7 @@
         first,
         partner,
         terms,
+        image,
     )
     copies = local_call(gram_share_kernel, shape(*parts.shape), 1 << 24, arrived, factors[2])
     copies = exchange(copies, "prow")
@@ -410,7 +414,7 @@
         jnp.concatenate([gram_other, gram_own]),
     )
     sums = local_call(
-        pair_kernel, shape(columns, 2 * size), 1 << 27, sums, image, crosses, copies, nears
+        pair_kernel, shape(columns, 2 * size), 1 << 27, sums, copies, nears
     )
     current = streamed(
         middle_kernel,

time: 169 us -> 168 us (level)
    unnamed x28 -> x24, local copies, waits for them, and re-layouts: 7.09 us -> 7.11 us
where the time goes in v9:
time: 168 us; the launch traced here: 167 us
  blocking collectives  61.7 us (37%)
  Pallas kernels  33.2 us (20%)
  starting transfers between devices  25.6 us (15%)
  waiting for transfers between devices  22.2 us (13%)
  between operations  13.6 us (8%)
  local copies, waits for them, and re-layouts  10.9 us (6%)
    all_to_all x4, blocking collectives, exchange(): return lax.all_to_all(parts, axis, split_axis=0, concat_axis=0, tiled=True)  61.7 us
    all_to_all x5, starting transfers between devices, exchange(): return lax.all_to_all(parts, axis, split_axis=0, concat_axis=0, tiled=True)  21.7 us
    all_to_all x5, waiting for transfers between devices, exchange(): return lax.all_to_all(parts, axis, split_axis=0, concat_axis=0, tiled=True)  18.9 us
    pallas_call x3, Pallas kernels, streamed(): pl.pallas_call(kernel, grid_spec=pltpu.PrefetchScalarGridSpec(num_scalar_...  18 us
    pallas_call x9, Pallas kernels, local_call(): pl.pallas_call(kernel, out_shape=shapes, in_specs=[whole(pltpu.SMEM)] * s...  10.5 us
    unnamed x24, local copies, waits for them, and re-layouts  7.11 us
    pallas_call x1, Pallas kernels, fetching_call(): pl.pallas_call(kernel, out_shape=shapes, in_specs=[whole(pltpu.HBM)] * le...  4.66 us
    ppermute x2, starting transfers between devices, from_partner(): return lax.ppermute(x, 'pcol_2', [(0, 1), (1, 0)])  3.83 us
  transfers between devices with their start and end apart: 8, of which 6 were waited for; matrix products, arithmetic and copies ran while one was open for 1% of the time, Pallas kernels for 14%

profile of v9, /device:TPU:8, one launch (start us, length us, event | category | flops | bytes accessed | tf_op | source)
XLA Modules:
  0.0 167.2 jit_solution(15589320398427217591)
XLA Ops:
  6.5 0.9 slice.10
  7.5 0.1 broadcast_in_dim.9
  7.6 12.2 %all_to_all.45 = bf16[4,3,4,4096]{3,2,1,0:T(4,128)(2,1)S(1)} all-to-all(bf16[4,3,4,4096]{3,2,1,0:T(4,128)(2,1)S(1)} %broadcast_in_dim.9), channel_id=1, replica_groups=mesh['prow'=8,'pcol_0'=8,'pcol_1'=4,'pcol_2'=2] {'pcol_1'}, dimensions={0} | all-to-all | bytes 786432 | tf_op jit(solution)/shard_map/all_to_all | solution.py:23
  19.8 0.2 copy.5
  20.0 0.0 copy-start.11
  20.0 0.8 all_gather_reshape.3
  20.8 0.0 all-gather.2.cloned.1.call-update
  20.8 0.8 slice_bitcast_fusion
  21.6 0.8 broadcast_in_dim.10
  22.4 7.5 %all-to-all-start.1 = ((bf16[8,4,4096]{2,1,0:T(4,128)(2,1)}), bf16[8,4,4096]{2,1,0:T(4,128)(2,1)S(1)}, u32[]{:S(2)}, u32[]{:S(2)}) async-start(bf16[8,4,4096]{2,1,0:T(4,128)(2,1)} %broadcast_in_dim.10), calls=%async_computation.1 | async-start | bytes 524288 | tf_op jit(solution)/shard_map/all_to_all | solution.py:23
  30.0 1.6 copy-done.3
  31.6 0.6 shard_map.46
  32.2 1.3 copy-done.2
  33.5 2.0 %copy-done.10 = f32[4,256,256]{2,1,0:T(8,128)S(1)} copy-done((f32[4,256,256]{2,1,0:T(8,128)S(1)}, f32[4,256,256]{2,1,0:T(8,128)}, u32[]{:S(2)}) %copy-start.10) | copy-done | bytes 1048600
  35.5 2.4 %shard_map.47 = (f32[256,256]{1,0:T(8,128)S(1)}, f32[256,256]{1,0:T(8,128)S(1)}, f32[256,256]{1,0:T(8,128)S(1)}, f32[256,256]{1,0:T(8,128)S(1)}) custom-call(s32[1]{0:T(128)} %bitcast.1.core_ref, f32[4,256]{1,0:T(4,128)S(1)} %copy-done.11, f32[4,256,256]{2,1,0:T(8,128)S(1)} %copy-done.10), custom_call_target="tpu_custom_call" | custom-call | flops 1610612736 | bytes 1052676 | tf_op jit(solution)/shard_map/pallas_call | solution.py:60
  37.9 0.7 copy-done.4
  38.6 0.7 copy-done.6
  39.3 0.1 reshape.24
  39.4 0.6 copy-done.8
  40.0 0.1 broadcast_in_dim.11
  40.1 16.1 %all_to_all.46 = bf16[4,32,4096]{2,1,0:T(8,128)(2,1)S(1)} all-to-all(bf16[4,32,4096]{2,1,0:T(8,128)(2,1)S(1)} %broadcast_in_dim.11), channel_id=1, replica_groups=mesh['prow'=8,'pcol_0'=8,'pcol_1'=4,'pcol_2'=2] {'pcol_1'}, dimensions={0} | all-to-all | bytes 2097152 | tf_op jit(solution)/shard_map/all_to_all | solution.py:23
  56.2 1.9 %collective-permute-start = (bf16[128,4096]{1,0:T(8,128)(2,1)S(1)}, bf16[128,4096]{1,0:T(8,128)(2,1)S(1)}, u32[]{:S(2)}, u32[]{:S(2)}) collective-permute-start(bf16[128,4096]{1,0:T(8,128)(2,1)S(1)} %bitcast.10), channel_id=1, source_target_pairs={{0,1},{1,0},{2,3},{3,2},{4,5},{5,4},{6,7},{7,6},{8,9},{9,8},{10,11... | collective-permute-start | bytes 3145736 | tf_op jit(solution)/shard_map/ppermute | solution.py:31
  58.2 0.9 shard_map.48.before_ref
  59.0 1.9 %collective-permute-done.half_ref.partner_ref = bf16[128,4096]{1,0:T(8,128)(2,1)S(1)} collective-permute-done((bf16[128,4096]{1,0:T(8,128)(2,1)S(1)}, bf16[128,4096]{1,0:T(8,128)(2,1)S(1)}, u32[]{:S(2)}, u32[]{:S(2)}) %collective-permute-start) | collective-permute-done | bytes 1048608 | tf_op jit(solution)/shard_map/ppermute | solution.py:31
  61.0 0.9 shard_map.49
  61.9 0.2 copy-done.1
  62.0 19.6 %all_to_all.47.parts_ref = f32[8,16,256]{2,1,0:T(8,128)S(1)} all-to-all(f32[8,16,256]{2,1,0:T(8,128)S(1)} %bitcast.19), channel_id=1, replica_groups=mesh['prow'=8,'pcol_0'=8,'pcol_1'=4,'pcol_2'=2] {'prow'}, dimensions={0} | all-to-all | bytes 262144 | tf_op jit(solution)/shard_map/all_to_all | solution.py:23
  81.6 1.0 shard_map.50
  82.6 3.4 %all-to-all-start.4 = ((f32[8,16,256]{2,1,0:T(8,128)}), f32[8,16,256]{2,1,0:T(8,128)S(1)}, u32[]{:S(2)}, u32[]{:S(2)}) async-start(f32[8,16,256]{2,1,0:T(8,128)} %shard_map.50), calls=%async_computation.4 | async-start | bytes 262144 | tf_op jit(solution)/shard_map/all_to_all | solution.py:23
  86.0 0.0 all-gather.2.cloned.1.call-done.half_ref.high_ref.next_ref.low_ref.gathered
  86.0 5.4 %shard_map.51 = (f32[128,256]{1,0:T(8,128)S(1)}, f32[256,256]{1,0:T(8,128)S(1)}, f32[128,256]{1,0:T(8,128)S(1)}) custom-call(s32[1]{0:T(128)} %bitcast.1.core_ref, bf16[16,3,16,4096]{3,2,1,0:T(8,128)(2,1)} %all-gather.2.cloned.1.call-done.half_ref.high_ref.next_ref.low_ref.gathered, ...), custom_call_target="tpu_custom_call" | custom-call | flops 1342177280 | bytes 23068676 | tf_op jit(solution)/shard_map/pallas_call | solution.py:347
  91.5 3.5 %all-to-all-done.4 = f32[8,16,256]{2,1,0:T(8,128)S(1)} async-done(((f32[8,16,256]{2,1,0:T(8,128)}), f32[8,16,256]{2,1,0:T(8,128)S(1)}, u32[]{:S(2)}, u32[]{:S(2)}) %all-to-all-start.4) | async-done | bytes 131104 | tf_op jit(solution)/shard_map/all_to_all | solution.py:23
  95.0 0.4 shard_map.52
  95.4 13.9 %all_to_all.48.parts_ref = f32[8,32,256]{2,1,0:T(8,128)S(1)} all-to-all(f32[8,32,256]{2,1,0:T(8,128)S(1)} %shard_map.52), channel_id=1, replica_groups=mesh['prow'=8,'pcol_0'=8,'pcol_1'=4,'pcol_2'=2] {'prow'}, dimensions={0} | all-to-all | bytes 524288 | tf_op jit(solution)/shard_map/all_to_all | solution.py:23
  109.3 1.0 shard_map.53
  110.3 3.4 %all-to-all-start.6 = ((f32[8,32,256]{2,1,0:T(8,128)}), f32[8,32,256]{2,1,0:T(8,128)S(1)}, u32[]{:S(2)}, u32[]{:S(2)}) async-start(f32[8,32,256]{2,1,0:T(8,128)} %shard_map.53), calls=%async_computation.6 | async-start | bytes 524288 | tf_op jit(solution)/shard_map/all_to_all | solution.py:23
  113.7 7.3 %shard_map.55 = (f32[512,256]{1,0:T(8,128)S(1)}, f32[128,512]{1,0:T(8,128)S(1)}) custom-call(bf16[16,3,16,4096]{3,2,1,0:T(8,128)(2,1)} %all-gather.2.cloned.1.call-done.half_ref.high_ref.next_ref.low_ref.gathered, bf16[16,3,16,4096]{3,2,1,0:T(8,128)(2,1)} %all-gather.2.cloned.1.call-done.half_ref.high_ref.next_ref.low_ref.gathered, ...), custom_call_target="tpu_custom_call" | custom-call | flops 3221225472 | bytes 23199744 | tf_op jit(solution)/shard_map/pallas_call | solution.py:347
  121.0 3.1 %all-to-all-done.6.copies_ref = f32[8,32,256]{2,1,0:T(8,128)S(1)} async-done(((f32[8,32,256]{2,1,0:T(8,128)}), f32[8,32,256]{2,1,0:T(8,128)S(1)}, u32[]{:S(2)}, u32[]{:S(2)}) %all-to-all-start.6) | async-done | bytes 262176 | tf_op jit(solution)/shard_map/all_to_all | solution.py:23
  124.1 1.3 shard_map.56
  125.4 4.0 %all-to-all-start.7 = ((f32[8,16,512]{2,1,0:T(8,128)}), f32[8,16,512]{2,1,0:T(8,128)S(1)}, u32[]{:S(2)}, u32[]{:S(2)}) async-start(f32[8,16,512]{2,1,0:T(8,128)} %bitcast.6), calls=%async_computation.7 | async-start | bytes 524288 | tf_op jit(solution)/shard_map/all_to_all | solution.py:23
  129.4 1.9 %collective-permute-start.1 = (f32[128,256]{1,0:T(8,128)S(1)}, f32[128,256]{1,0:T(8,128)S(1)}, u32[]{:S(2)}, u32[]{:S(2)}) collective-permute-start(f32[128,256]{1,0:T(8,128)S(1)} %bitcast.21), channel_id=1, source_target_pairs={{0,1},{1,0},{2,3},{3,2},{4,5},{5,4},{6,7},{7,6},{8,9},{9,8},{10,11... | collective-permute-start | bytes 393224 | tf_op jit(solution)/shard_map/ppermute | solution.py:31
  131.4 1.3 collective-permute-done.1
  132.7 7.2 %all-to-all-done.7.parts_ref = f32[8,16,512]{2,1,0:T(8,128)S(1)} async-done(((f32[8,16,512]{2,1,0:T(8,128)}), f32[8,16,512]{2,1,0:T(8,128)S(1)}, u32[]{:S(2)}, u32[]{:S(2)}) %all-to-all-start.7) | async-done | bytes 262176 | tf_op jit(solution)/shard_map/all_to_all | solution.py:23
  139.9 2.0 %shard_map.57 = f32[8,16,512]{2,1,0:T(8,128)} custom-call(f32[8,16,512]{2,1,0:T(8,128)S(1)} %all-to-all-done.7.parts_ref, f32[256,256]{1,0:T(8,128)S(1)} %copy-done.5, f32[256,256]{1,0:T(8,128)S(1)} %get-tuple-element.22.low_ref, f32[256,256]{1,0:T(8,128)S(1)} %maximum_select_fusion.gram_ref), custom_call_target="tpu_custom_call" | custom-call | flops 16777216 | bytes 1048576 | tf_op jit(solution)/shard_map/pallas_call | solution.py:60
  141.9 3.4 %all-to-all-start.8 = ((f32[8,16,512]{2,1,0:T(8,128)}), f32[8,16,512]{2,1,0:T(8,128)S(1)}, u32[]{:S(2)}, u32[]{:S(2)}) async-start(f32[8,16,512]{2,1,0:T(8,128)} %shard_map.57), calls=%async_computation.8 | async-start | bytes 524288 | tf_op jit(solution)/shard_map/all_to_all | solution.py:23
  145.3 5.3 %shard_map.54.z = f32[128,4096]{1,0:T(8,128)} custom-call(f32[128,4096]{1,0:T(8,128)} %copy-done.2, bf16[128,4096]{1,0:T(8,128)(2,1)S(1)} %bitcast.14, bf16[128,4096]{1,0:T(8,128)(2,1)} %copy-done.1, bf16[16,3,16,4096]{3,2,1,0:T(8,128)(2,1)} %all-gather.2.cloned.1.call-done.half_ref.high_ref.next_ref.low_ref.gathered, f32[128,256]{1,0:T(8,128)S(1)} %bitcast.17, ...), custom_call_target="tpu_custom_call" | custom-call | flops 1073741824 | bytes 10878976 | tf_op jit(solution)/shard_map/pallas_call | solution.py:347
  150.6 5.1 %all-to-all-done.8 = f32[8,16,512]{2,1,0:T(8,128)S(1)} async-done(((f32[8,16,512]{2,1,0:T(8,128)}), f32[8,16,512]{2,1,0:T(8,128)S(1)}, u32[]{:S(2)}, u32[]{:S(2)}) %all-to-all-start.8) | async-done | bytes 262176 | tf_op jit(solution)/shard_map/all_to_all | solution.py:23
  155.7 4.7 %shard_map.58 = f32[4096,128]{1,0:T(8,128)} custom-call(f32[128,4096]{1,0:T(8,128)} %shard_map.54.z, bf16[16,3,16,4096]{3,2,1,0:T(8,128)(2,1)} %all-gather.2.cloned.1.call-done.half_ref.high_ref.next_ref.low_ref.gathered, f32[128,512]{1,0:T(8,128)S(1)} %bitcast.18), custom_call_target="tpu_custom_call" | custom-call | flops 1073741824 | bytes 8650752 | tf_op jit(solution)/shard_map/pallas_call | solution.py:71
  (20 shorter events, 0.1 us)
Async XLA Ops:
  6.5 79.5 %all-gather.2.cloned.1.call-start = ((), (), s32[]{:S(2)}) async-start(), calls=%async_computation.9 | async-start | bytes 6684672 | tf_op jit(solution)/shard_map/all_gather | solution.py:305
  20.0 13.5 %copy-start.11 = (f32[4,256]{1,0:T(4,128)S(1)}, f32[4,256]{1,0:T(4,128)}, u32[]{:S(2)}) copy-start(f32[4,256]{1,0:T(4,128)} %tau_ref.1) | copy-start | bytes 12292
  22.4 16.9 %all-to-all-start.1 = ((bf16[8,4,4096]{2,1,0:T(4,128)(2,1)}), bf16[8,4,4096]{2,1,0:T(4,128)(2,1)S(1)}, u32[]{:S(2)}, u32[]{:S(2)}) async-start(bf16[8,4,4096]{2,1,0:T(4,128)(2,1)} %broadcast_in_dim.10), calls=%async_computation.1 | async-start | bytes 524288 | tf_op jit(solution)/shard_map/all_to_all | solution.py:23
  30.0 1.6 copy-start.3
  32.2 1.3 copy-start.2
  33.5 27.5 %copy-start = (bf16[256,4096]{1,0:T(8,128)(2,1)}, bf16[256,4096]{1,0:T(8,128)(2,1)S(1)}, u32[]{:S(2)}) copy-start(bf16[256,4096]{1,0:T(8,128)(2,1)S(1)} %get-tuple-element.21.terms_ref) | copy-start | bytes 6291460
  33.5 2.0 %copy-start.10 = (f32[4,256,256]{2,1,0:T(8,128)S(1)}, f32[4,256,256]{2,1,0:T(8,128)}, u32[]{:S(2)}) copy-start(f32[4,256,256]{2,1,0:T(8,128)} %coupling_ref.1) | copy-start | bytes 3145732
  37.9 0.7 copy-start.4
  38.6 0.7 copy-start.6
  39.3 0.7 copy-start.8
  56.2 4.8 %collective-permute-start = (bf16[128,4096]{1,0:T(8,128)(2,1)S(1)}, bf16[128,4096]{1,0:T(8,128)(2,1)S(1)}, u32[]{:S(2)}, u32[]{:S(2)}) collective-permute-start(bf16[128,4096]{1,0:T(8,128)(2,1)S(1)} %bitcast.10), channel_id=1, source_target_pairs={{0,1},{1,0},{2,3},{3,2},{4,5},{5,4},{6,7},{7,6},{8,9},{9,8},{10,11... | collective-permute-start | bytes 3145736 | tf_op jit(solution)/shard_map/ppermute | solution.py:31
  59.0 22.6 %copy-start.9 = (f32[256,256]{1,0:T(8,128)S(1)}, f32[256,256]{1,0:T(8,128)}, u32[]{:S(2)}) copy-start(f32[256,256]{1,0:T(8,128)} %copy-done.8) | copy-start | bytes 786436
  61.0 1.0 copy-start.1
  82.6 12.4 %all-to-all-start.4 = ((f32[8,16,256]{2,1,0:T(8,128)}), f32[8,16,256]{2,1,0:T(8,128)S(1)}, u32[]{:S(2)}, u32[]{:S(2)}) async-start(f32[8,16,256]{2,1,0:T(8,128)} %shard_map.50), calls=%async_computation.4 | async-start | bytes 262144 | tf_op jit(solution)/shard_map/all_to_all | solution.py:23
  86.0 23.3 %copy-start.7 = (f32[256,256]{1,0:T(8,128)S(1)}, f32[256,256]{1,0:T(8,128)}, u32[]{:S(2)}) copy-start(f32[256,256]{1,0:T(8,128)} %copy-done.6) | copy-start | bytes 786436
  110.3 13.8 %all-to-all-start.6 = ((f32[8,32,256]{2,1,0:T(8,128)}), f32[8,32,256]{2,1,0:T(8,128)S(1)}, u32[]{:S(2)}, u32[]{:S(2)}) async-start(f32[8,32,256]{2,1,0:T(8,128)} %shard_map.53), calls=%async_computation.6 | async-start | bytes 524288 | tf_op jit(solution)/shard_map/all_to_all | solution.py:23
  121.0 18.9 %copy-start.5 = (f32[256,256]{1,0:T(8,128)S(1)}, f32[256,256]{1,0:T(8,128)}, u32[]{:S(2)}) copy-start(f32[256,256]{1,0:T(8,128)} %copy-done.4) | copy-start | bytes 786436
  125.4 14.5 %all-to-all-start.7 = ((f32[8,16,512]{2,1,0:T(8,128)}), f32[8,16,512]{2,1,0:T(8,128)S(1)}, u32[]{:S(2)}, u32[]{:S(2)}) async-start(f32[8,16,512]{2,1,0:T(8,128)} %bitcast.6), calls=%async_computation.7 | async-start | bytes 524288 | tf_op jit(solution)/shard_map/all_to_all | solution.py:23
  129.4 3.2 %collective-permute-start.1 = (f32[128,256]{1,0:T(8,128)S(1)}, f32[128,256]{1,0:T(8,128)S(1)}, u32[]{:S(2)}, u32[]{:S(2)}) collective-permute-start(f32[128,256]{1,0:T(8,128)S(1)} %bitcast.21), channel_id=1, source_target_pairs={{0,1},{1,0},{2,3},{3,2},{4,5},{5,4},{6,7},{7,6},{8,9},{9,8},{10,11... | collective-permute-start | bytes 393224 | tf_op jit(solution)/shard_map/ppermute | solution.py:31
  141.9 13.8 %all-to-all-start.8 = ((f32[8,16,512]{2,1,0:T(8,128)}), f32[8,16,512]{2,1,0:T(8,128)S(1)}, u32[]{:S(2)}, u32[]{:S(2)}) async-start(f32[8,16,512]{2,1,0:T(8,128)} %shard_map.57), calls=%async_computation.8 | async-start | bytes 524288 | tf_op jit(solution)/shard_map/all_to_all | solution.py:23
Sparse Core Ops, SparseCore 0:
  21.0 50.8 all-gather.1
